TPU v7x, 8 devices: a whole 2x2x1 slice. The times are simulated.
8 devices in a mesh: dp: 2 (over z, y), tp: 4 (over x, core).
Axes of the slice: x: 2, y: 2, z: 1, core: 2. Of those that a mesh axis runs over, the one named last changes fastest.
Arguments:
- x: bfloat16 [16, 384, 7168], P('dp'), parts along dimension 0
- seq_lens: int32 [16], P('dp'), parts along dimension 0
- w_query: bfloat16 [7168, 7168], P(None, 'tp')
- w_key: bfloat16 [7168, 1024], P(None, 'tp')
- w_value: bfloat16 [7168, 1024], P(None, 'tp')
- w_out: bfloat16 [7168, 7168], P('tp')
- w_gate: bfloat16 [7168, 20480], P(None, 'tp')
- w_up: bfloat16 [7168, 20480], P(None, 'tp')
- w_down: bfloat16 [20480, 7168], P('tp')
- attn_gain: bfloat16 [7168], replicated
- mlp_gain: bfloat16 [7168], replicated
- k_cache: bfloat16 [16, 768, 8, 128], P('dp', None, 'tp'), parts along dimension 0
- v_cache: bfloat16 [16, 768, 8, 128], P('dp', None, 'tp'), parts along dimension 0
Outputs:
- output 1: bfloat16 [16, 384, 7168], P('dp'), parts along dimension 0
- output 2: bfloat16 [16, 768, 8, 128], P('dp', None, 'tp'), parts along dimension 0
- output 3: bfloat16 [16, 768, 8, 128], P('dp', None, 'tp'), parts along dimension 0
There are 2 independent parts. A program takes and returns all parts, laid end to end along the dimension named above; an argument that names none is the same for every part.
All inputs are finite; a program needn't handle non-finite values.
Results may differ from a plain program's by a relative error of at most 0.0113591.
Values are sent between devices in bfloat16 or wider.
A program may use at most 1.5 GiB of HBM per device.

v0:
```python
import jax
import jax.numpy as jnp
from jax import lax
from jax.sharding import PartitionSpec as P

EPS = 1e-5
ROPE_BASE = 10000.0


def rms_norm(rows, gain):
    rows32 = rows.astype(jnp.float32)
    inv_rms = lax.rsqrt(jnp.mean(rows32 * rows32, axis=-1, keepdims=True) + EPS)
    return (rows32 * inv_rms * gain.astype(jnp.float32)).astype(jnp.bfloat16)


def rotary(vecs):
    seq_len = vecs.shape[1]
    head_dim = vecs.shape[-1]
    half_dim = head_dim // 2
    inv_freq = ROPE_BASE ** (-jnp.arange(0, head_dim, 2).astype(jnp.float32) / head_dim)
    angles = jnp.arange(seq_len).astype(jnp.float32)[:, None] * inv_freq[None, :]
    table_shape = (1, seq_len) + (1,) * (vecs.ndim - 3) + (half_dim,)
    cos_tab = jnp.cos(angles).reshape(table_shape)
    sin_tab = jnp.sin(angles).reshape(table_shape)
    pairs = vecs.reshape(vecs.shape[:-1] + (half_dim, 2))
    even_part = pairs[..., 0]
    odd_part = pairs[..., 1]
    turned = jnp.stack([even_part * cos_tab - odd_part * sin_tab, even_part * sin_tab + odd_part * cos_tab], axis=-1)
    return turned.reshape(vecs.shape).astype(jnp.bfloat16)


def causal_attention(queries, keys, values, seq_lens):
    seq_len = queries.shape[1]
    head_dim = queries.shape[-1]
    scores = jnp.einsum("bqkgh,bskh->bkgqs", queries, keys, preferred_element_type=jnp.float32) * head_dim ** -0.5
    positions = jnp.arange(seq_len)
    allowed = (positions[None, None, :] <= positions[None, :, None]) & (positions[None, None, :] < seq_lens[:, None, None])
    scores = jnp.where(allowed[:, None, None], scores, -jnp.inf)
    probs = jax.nn.softmax(scores, axis=-1).astype(jnp.bfloat16)
    return jnp.einsum("bkgqs,bskh->bqkgh", probs, values, preferred_element_type=jnp.float32).astype(jnp.bfloat16)


def sum_partials(partial, resid_rows, tp_size):
    batch_size, seq_len, model_width = partial.shape
    stacked = partial.reshape(batch_size, tp_size, seq_len // tp_size, model_width)
    received = lax.all_to_all(stacked, "tp", 1, 1, tiled=True)
    summed = jnp.sum(received.astype(jnp.float32), axis=1)
    return (resid_rows.astype(jnp.float32) + summed).astype(jnp.bfloat16)


def solution(mesh):
    tp_size = mesh.shape["tp"]

    def layer_shard(x, seq_lens, w_query, w_key, w_value, w_out, w_gate, w_up, w_down, attn_gain, mlp_gain, k_cache, v_cache):
        batch_size, seq_len, model_width = x.shape
        head_dim = k_cache.shape[3]
        kv_local = k_cache.shape[2]
        group_size = w_query.shape[1] // (head_dim * kv_local)
        rows_each = seq_len // tp_size
        tp_index = lax.axis_index("tp")
        normed = rms_norm(x, attn_gain)
        queries = rotary(jnp.einsum("bsd,dk->bsk", normed, w_query, preferred_element_type=jnp.float32).reshape(batch_size, seq_len, kv_local, group_size, head_dim))
        keys = rotary(jnp.einsum("bsd,dk->bsk", normed, w_key, preferred_element_type=jnp.float32).reshape(batch_size, seq_len, kv_local, head_dim))
        values = jnp.einsum("bsd,dk->bsk", normed, w_value, preferred_element_type=jnp.float32).astype(jnp.bfloat16).reshape(batch_size, seq_len, kv_local, head_dim)
        valid = (jnp.arange(seq_len)[None, :] < seq_lens[:, None])[:, :, None, None]
        keys = jnp.where(valid, keys, jnp.zeros_like(keys))
        values = jnp.where(valid, values, jnp.zeros_like(values))
        k_cache_out = lax.dynamic_update_slice(k_cache, keys, (0, 0, 0, 0))
        v_cache_out = lax.dynamic_update_slice(v_cache, values, (0, 0, 0, 0))
        attn_rows = causal_attention(queries, keys, values, seq_lens).reshape(batch_size, seq_len, -1)
        attn_part = jnp.einsum("bsk,kd->bsd", attn_rows, w_out, preferred_element_type=jnp.float32).astype(jnp.bfloat16)
        x_rows = lax.dynamic_slice_in_dim(x, tp_index * rows_each, rows_each, axis=1)
        hidden_rows = sum_partials(attn_part, x_rows, tp_size)
        normed_mlp = lax.all_gather(rms_norm(hidden_rows, mlp_gain), "tp", axis=1, tiled=True)
        gate_pre = jnp.einsum("bsd,df->bsf", normed_mlp, w_gate, preferred_element_type=jnp.float32)
        up_pre = jnp.einsum("bsd,df->bsf", normed_mlp, w_up, preferred_element_type=jnp.float32)
        gated = (jax.nn.silu(gate_pre) * up_pre).astype(jnp.bfloat16)
        mlp_part = jnp.einsum("bsf,fd->bsd", gated, w_down, preferred_element_type=jnp.float32).astype(jnp.bfloat16)
        out_rows = sum_partials(mlp_part, hidden_rows, tp_size)
        y = lax.all_gather(out_rows, "tp", axis=1, tiled=True)
        return y, k_cache_out, v_cache_out

    cache_spec = P("dp", None, "tp", None)
    return jax.shard_map(layer_shard, mesh=mesh, in_specs=(P("dp", None, None), P("dp"), P(None, "tp"), P(None, "tp"), P(None, "tp"), P("tp", None), P(None, "tp"), P(None, "tp"), P("tp", None), P(), P(), cache_spec, cache_spec), out_specs=(P("dp", None, None), cache_spec, cache_spec), check_vma=False)
```

profile of v0, /device:TPU:0, one launch (start us, length us, event | category | flops | bytes accessed | tf_op | source)
XLA Modules:
  0.0 2891.9 jit_solution(1465122398754406987)
XLA Ops:
  7.2 5.7 copy.80
  12.9 5.7 copy.81
  18.6 0.6 iota_convert_fusion
  19.2 0.5 multiply_power_fusion
  19.7 0.7 iota_compare_fusion
  20.4 0.7 convert_element_type.109
  21.1 14.7 fusion.1
  35.8 20.0 fusion.27
  55.8 3.5 copy.67
  59.3 20.9 fusion.40
  80.2 0.0 copy-done.12
  80.2 0.6 iota_compare_fusion.1
  80.8 93.2 %fusion.18 = f32[8,384,1792]{2,1,0:T(8,128)} fusion(bf16[7168,1792]{1,0:T(8,128)(2,1)} %param.15, bf16[8,384,7168]{2,1,0:T(8,128)(2,1)} %param.13, f32[7168]{0:T(1024)S(1)} %convert_element_type.109, f32[8,384]{1,0:T(8,128)S(1)} %add_rsqrt_fusion), kind=kOutput, calls=%fused_computation.29 | convolution fusion | flops 79008104448 | bytes 91791360 | tf_op jit(solution)/shard_map/bsd,dk->bsk/dot_general | solution.py:62
  174.1 22.1 copy.45
  196.1 0.0 copy-done.10
  196.1 0.0 copy-done.11
  196.1 0.0 copy-start.8
  196.2 0.0 copy-start.6
  196.2 0.4 multiply_cosine_fusion
  196.6 0.0 copy-done.3
  196.6 0.5 subtract_convert_fusion.1
  197.1 8.7 subtract_convert_fusion
  205.8 0.2 pad_maximum_fusion.1
  206.0 0.0 copy-done.7
  206.0 0.0 copy-done.8
  206.0 1.5 broadcast_and_fusion
  207.6 0.0 copy-done.6
  207.6 1.1 copy_select_fusion
  208.6 0.0 copy-start.1
  208.6 0.0 copy-start.4
  208.7 5.4 pad_maximum_fusion
  214.1 27.4 fusion.35
  241.4 0.0 copy-done.1
  241.5 69.0 %fusion.50 = (f32[8,2,7,384]{3,2,1,0:T(8,128)S(1)}, f32[8,2,7,384,384]{3,4,2,1,0:T(8,128)}) fusion(f32[8,2,384,384,7]{3,2,4,1,0:T(8,128)} %fusion.35, pred[8,384,384]{1,2,0:T(8,128)(4,1)} %broadcast_and_fusion), kind=kOutput, calls=%fused_computation.70 | output fusion | flops 99090816 | bytes 133472256 | tf_op jit(solution)/shard_map/sub | solution.py:39
  310.4 0.0 copy-done.4
  310.4 26.3 fusion.37
  336.7 89.9 %fusion.20 = bf16[8,384,7168]{2,1,0:T(8,128)(2,1)} fusion(bf16[8,384,1792]{1,2,0:T(8,128)(2,1)} %bitcast.67, bf16[1792,7168]{1,0:T(8,128)(2,1)} %param.18), kind=kOutput, calls=%fused_computation.31 | convolution fusion | flops 78942044160 | bytes 80740352 | tf_op jit(solution)/shard_map/bsk,kd->bsd/dot_general | solution.py:71
  426.6 29.6 %copy.51 = bf16[8,4,96,7168]{3,2,0,1:T(8,128)(2,1)} copy(bf16[8,4,96,7168]{3,2,1,0:T(8,128)(2,1)} %bitcast.60) | data formatting | bytes 88080384 | tf_op jit(solution)/shard_map/reshape | solution.py:45
  456.2 11.6 all-to-all-start
  467.7 0.0 all-gather.3.cloned.1.call-start
  467.8 0.0 copy-done.9
  467.8 475.8 %all-to-all-done = bf16[8,4,96,7168]{3,2,0,1:T(8,128)(2,1)} async-done(((bf16[8,4,96,7168]{3,2,0,1:T(8,128)(2,1)}), bf16[8,4,96,7168]{3,2,0,1:T(8,128)(2,1)}, u32[]{:S(2)}, u32[]{:S(2)}) %all-to-all-start) | async-done | bytes 44040224 | tf_op jit(solution)/shard_map/all_to_all | solution.py:46
  943.6 25.1 convert_reduce_fusion.1
  968.7 7.5 fusion.31
  976.3 4.0 copy-done
  980.3 5.8 fusion.33
  986.1 0.0 all-gather.3.cloned.1.call-update
  986.1 0.0 all-gather.5.cloned.1.call-start
  986.2 260.5 %all-gather.3.cloned.1.call-done = bf16[8,384,7168]{2,1,0:T(8,128)(2,1)} async-done(((bf16[8,96,7168]{2,1,0:T(8,128)(2,1)}), bf16[8,384,7168]{2,1,0:T(8,128)(2,1)}) %all-gather.3.cloned.1.call-update) | async-done | bytes 44040208 | tf_op jit(solution)/shard_map/all_gather | solution.py:74
  1246.7 243.1 %fusion.6 = f32[8,384,5120]{2,1,0:T(8,128)} fusion(bf16[8,384,7168]{2,1,0:T(8,128)(2,1)} %all-gather.3.cloned.1.call-done, bf16[7168,5120]{1,0:T(8,128)(2,1)} %param.20), kind=kOutput, calls=%fused_computation.10 | convolution fusion | flops 225485783040 | bytes 180355072 | tf_op jit(solution)/shard_map/bsd,df->bsf/dot_general | solution.py:76
  1489.7 242.6 %fusion.8 = f32[8,384,5120]{2,1,0:T(8,128)} fusion(bf16[8,384,7168]{2,1,0:T(8,128)(2,1)} %all-gather.3.cloned.1.call-done, bf16[7168,5120]{1,0:T(8,128)(2,1)} %param.19), kind=kOutput, calls=%fused_computation.12 | convolution fusion | flops 225485783040 | bytes 180355072 | tf_op jit(solution)/shard_map/bsd,df->bsf/dot_general | solution.py:75
  1732.4 51.0 %multiply_convert_fusion.6 = bf16[8,384,5120]{2,1,0:T(8,128)(2,1)} fusion(f32[8,384,5120]{2,1,0:T(8,128)} %fusion.6, f32[8,384,5120]{2,1,0:T(8,128)} %fusion.8), kind=kLoop, calls=%fused_computation.17.clone.clone.clone.clone.1 | loop fusion | flops 94371840 | bytes 157286400 | tf_op jit(solution)/shard_map/bsf,fd->bsd/dot_general | solution.py:78
  1783.3 239.0 %fusion.23 = bf16[8,384,7168]{2,1,0:T(8,128)(2,1)} fusion(bf16[5120,7168]{1,0:T(8,128)(2,1)} %param.21, bf16[8,384,5120]{2,1,0:T(8,128)(2,1)} %multiply_convert_fusion.6), kind=kOutput, calls=%fused_computation.32 | convolution fusion | flops 225507803136 | bytes 148897792 | tf_op jit(solution)/shard_map/bsf,fd->bsd/dot_general | solution.py:78
  2022.3 29.5 %copy.52 = bf16[8,4,96,7168]{3,2,0,1:T(8,128)(2,1)} copy(bf16[8,4,96,7168]{3,2,1,0:T(8,128)(2,1)} %bitcast.61) | data formatting | bytes 88080384 | tf_op jit(solution)/shard_map/reshape | solution.py:45
  2051.8 498.2 %all_to_all.10 = bf16[8,4,96,7168]{3,2,0,1:T(8,128)(2,1)} all-to-all(bf16[8,4,96,7168]{3,2,0,1:T(8,128)(2,1)} %copy.52), channel_id=1, replica_groups=mesh['dp'=2,'tp'=4] {'tp'}, dimensions={1} | all-to-all | bytes 88080384 | tf_op jit(solution)/shard_map/all_to_all | solution.py:46
  2550.0 33.0 %convert_reduce_fusion = f32[8,96,7168]{2,1,0:T(8,128)} fusion(bf16[8,4,96,7168]{3,2,0,1:T(8,128)(2,1)} %all_to_all.10), kind=kLoop, calls=%fused_computation.6 | loop fusion | flops 38535168 | bytes 66060288 | tf_op jit(solution)/shard_map/reduce_sum | solution.py:47
  2583.0 13.0 fusion.34
  2596.0 0.0 all-gather.5.cloned.1.call-update
  2596.1 2.5 copy.53
  2598.6 0.0 copy-done.5
  2598.6 1.4 copy.54
  2600.0 5.4 constant_dynamic-update-slice_fusion
  2605.3 250.3 %all-gather.5.cloned.1.call-done = bf16[8,384,7168]{2,1,0:T(8,128)(2,1)} async-done(((bf16[8,96,7168]{2,1,0:T(8,128)(2,1)}), bf16[8,384,7168]{2,1,0:T(8,128)(2,1)}) %all-gather.5.cloned.1.call-update) | async-done | bytes 44040208 | tf_op jit(solution)/shard_map/all_gather | solution.py:80
  2855.7 29.1 %copy.82 = bf16[8,384,7168]{2,1,0:T(8,128)(2,1)} copy(bf16[8,384,7168]{2,1,0:T(8,128)(2,1)} %all-gather.5.cloned.1.call-done) | data formatting | bytes 88080384
  (20 shorter events, 0.0 us)
Async XLA Ops:
  59.3 20.9 copy-start.12
  174.0 22.1 copy-start.10
  174.0 22.1 copy-start.11
  174.0 22.5 copy-start.3
  196.1 9.9 copy-start.7
  196.1 9.9 copy-start.8
  196.2 11.4 copy-start.6
  208.6 32.8 %copy-start.1 = (bf16[8,384,2,128]{1,0,3,2:T(8,128)(2,1)}, bf16[8,384,2,128]{1,0,3,2:T(8,128)(2,1)S(1)}, u32[]{:S(2)}) copy-start(bf16[8,384,2,128]{1,0,3,2:T(8,128)(2,1)S(1)} %get-tuple-element.10) | copy-start | bytes 4718596
  208.6 101.8 %copy-start.4 = (bf16[8,384,2,128]{1,0,3,2:T(8,128)(2,1)}, bf16[8,384,2,128]{1,0,3,2:T(8,128)(2,1)S(1)}, u32[]{:S(2)}) copy-start(bf16[8,384,2,128]{1,0,3,2:T(8,128)(2,1)S(1)} %get-tuple-element.9) | copy-start | bytes 4718596
  456.2 11.6 copy-start.9
  456.2 487.4 %all-to-all-start = ((bf16[8,4,96,7168]{3,2,0,1:T(8,128)(2,1)}), bf16[8,4,96,7168]{3,2,0,1:T(8,128)(2,1)}, u32[]{:S(2)}, u32[]{:S(2)}) async-start(bf16[8,4,96,7168]{3,2,0,1:T(8,128)(2,1)} %copy.51), calls=%async_computation | async-start | bytes 88080384 | tf_op jit(solution)/shard_map/all_to_all | solution.py:46
  467.7 778.9 %all-gather.3.cloned.1.call-start = ((), (), s32[]{:S(2)}) async-start(), calls=%async_computation.2 | async-start | bytes 55050240 | tf_op jit(solution)/shard_map/all_gather | solution.py:74
  976.2 4.0 copy-start
  986.1 1869.6 %all-gather.5.cloned.1.call-start = ((), (), s32[]{:S(2)}) async-start(), calls=%async_computation.3 | async-start | bytes 55050240 | tf_op jit(solution)/shard_map/all_gather | solution.py:80
  2051.8 531.2 %slice-start = ((s8[11010048]{0:T(1024)(128)(4,1)}), s8[4194304]{0:T(1024)(128)(4,1)S(1)}, s32[]{:S(2)}) async-start(s8[11010048]{0:T(1024)(128)(4,1)} %bitcast.56), calls=%async_computation.4 | async-start | bytes 8388608
  2051.8 531.2 %slice-start.1 = ((s8[11010048]{0:T(1024)(128)(4,1)}), s8[4194304]{0:T(1024)(128)(4,1)S(1)}, s32[]{:S(2)}) async-start(s8[11010048]{0:T(1024)(128)(4,1)} %bitcast.56), calls=%async_computation.5 | async-start | bytes 8388608
  2550.0 33.0 %slice-start.2 = ((s8[11010048]{0:T(1024)(128)(4,1)}), s8[2621440]{0:T(1024)(128)(4,1)S(1)}, s32[]{:S(2)}) async-start(s8[11010048]{0:T(1024)(128)(4,1)} %bitcast.56), calls=%async_computation.6 | async-start | bytes 5242880
  2583.0 13.0 copy-start.2
  2583.0 15.5 copy-start.5
Sparse Core Ops, SparseCore 0:
  986.2 260.3 all-gather.2
  2596.2 259.4 all-gather.4
where the time goes:
time: 2900 us; the launch traced here: 2890 us
  matrix products  1000 us (34%)
  waiting for transfers between devices  987 us (34%)
  blocking collectives  498 us (17%)
  other arithmetic  240 us (8%)
  local copies, waits for them, and re-layouts  139 us (5%)
    all_to_all x1, blocking collectives, sum_partials(): received = lax.all_to_all(stacked, 'tp', 1, 1, tiled=True)  498 us
    all_to_all x1, waiting for transfers between devices, sum_partials(): received = lax.all_to_all(stacked, 'tp', 1, 1, tiled=True)  476 us
    all_gather x1, waiting for transfers between devices, layer_shard(): lax.all_gather(rms_norm(hidden_rows, mlp_gain), 'tp', axis=1, tiled=True)  260 us
    all_gather x1, waiting for transfers between devices, layer_shard(): y = lax.all_gather(out_rows, 'tp', axis=1, tiled=True)  250 us
    dot_general x1, matrix products, layer_shard(): jnp.einsum('bsd,df->bsf', normed_mlp, w_up, preferred_element_type=jnp.fl...  243 us
    dot_general x1, matrix products, layer_shard(): jnp.einsum('bsd,df->bsf', normed_mlp, w_gate, preferred_element_type=jnp....  243 us
    dot_general x1, matrix products, layer_shard(): jnp.einsum('bsf,fd->bsd', gated, w_down, preferred_element_type=jnp.float32)  239 us
    dot_general x1, matrix products, layer_shard(): jnp.einsum('bsd,dk->bsk', normed, w_query, preferred_element_type=jnp.flo...  93.2 us
  transfers between devices with their start and end apart: 3, of which 3 were waited for; matrix products, arithmetic and copies ran while one was open for 0% of the time, Pallas kernels for 0%

commit v1 on v0

v1 whole, which is shorter than its diff:
```python
import functools

import jax
import jax.numpy as jnp
from jax import lax
from jax.experimental import pallas as pl
from jax.experimental.pallas import tpu as pltpu
from jax.sharding import PartitionSpec as P


EPS = 1e-5
ROPE_BASE = 10000.0
CHUNKS = (1, 2, 2, 2, 1)
F32 = jnp.float32
BF16 = jnp.bfloat16
ANY = pl.BlockSpec(memory_space=pl.ANY)


def rope_tables(seq_len, head_dim):
    inv_freq = ROPE_BASE ** (-jnp.arange(0, head_dim, 2).astype(F32) / head_dim)
    angles = jnp.arange(seq_len).astype(F32)[:, None] * inv_freq[None, :]
    cos_tab = jnp.repeat(jnp.cos(angles), 2, axis=1)
    sin_tab = jnp.sin(angles)
    sin_tab = jnp.stack([-sin_tab, sin_tab], axis=-1).reshape(seq_len, head_dim)
    return cos_tab, sin_tab


def turn(vecs, cos_tab, sin_tab, even_lane):
    width = vecs.shape[1]
    swapped = jnp.where(even_lane, pltpu.roll(vecs, width - 1, 1), pltpu.roll(vecs, 1, 1))
    return vecs * cos_tab + swapped * sin_tab


def attention_kernel(first_seq, group_size, head_dim, lens_ref, q_ref, k_ref, v_ref, cos_ref, sin_ref, o_ref, k_out_ref, v_out_ref):
    seq_len = q_ref.shape[0]
    length = lens_ref[first_seq + pl.program_id(0)]
    cos_tab = cos_ref[...]
    sin_tab = sin_ref[...]
    even_lane = lax.broadcasted_iota(jnp.int32, (seq_len, head_dim), 1) % 2 == 0
    valid = lax.broadcasted_iota(jnp.int32, (seq_len, head_dim), 0) < length
    keys = jnp.where(valid, turn(k_ref[...], cos_tab, sin_tab, even_lane), 0.0).astype(BF16)
    values = jnp.where(valid, v_ref[...], 0.0).astype(BF16)
    k_out_ref[...] = keys
    v_out_ref[...] = values
    step = 128
    for head in range(group_size):
        cols = slice(head * head_dim, (head + 1) * head_dim)
        queries = turn(q_ref[:, cols], cos_tab, sin_tab, even_lane).astype(BF16)
        for start in range(0, seq_len, step):
            stop = start + step
            scores = lax.dot_general(queries[start:stop], keys[:stop], (((1,), (1,)), ((), ())), preferred_element_type=F32) * head_dim ** -0.5
            row = lax.broadcasted_iota(jnp.int32, (step, stop), 0) + start
            col = lax.broadcasted_iota(jnp.int32, (step, stop), 1)
            scores = jnp.where((col <= row) & (col < length), scores, -jnp.inf)
            exps = jnp.exp(scores - jnp.max(scores, axis=1, keepdims=True))
            probs = (exps / jnp.sum(exps, axis=1, keepdims=True)).astype(BF16)
            o_ref[start:stop, cols] = jnp.dot(probs, values[:stop], preferred_element_type=F32).astype(BF16)


def attention(lens, queries, kv, cos_tab, sin_tab, first_seq, n_seq, seq_len, head_dim):
    rows = n_seq * seq_len
    kv_local = kv.shape[1] // 2 // head_dim
    group_size = queries.shape[1] // (kv_local * head_dim)
    wide = group_size * head_dim
    per_head = pl.BlockSpec((seq_len, head_dim), lambda b, g, lens: (b, g))
    grouped = pl.BlockSpec((seq_len, wide), lambda b, g, lens: (b, g))
    table = pl.BlockSpec((seq_len, head_dim), lambda b, g, lens: (0, 0))
    return pl.pallas_call(
        functools.partial(attention_kernel, first_seq, group_size, head_dim),
        grid_spec=pltpu.PrefetchScalarGridSpec(
            num_scalar_prefetch=1,
            grid=(n_seq, kv_local),
            in_specs=[grouped, per_head, pl.BlockSpec((seq_len, head_dim), lambda b, g, lens: (b, kv_local + g)), table, table],
            out_specs=[grouped, per_head, per_head],
        ),
        out_shape=[
            jax.ShapeDtypeStruct((rows, queries.shape[1]), BF16),
            jax.ShapeDtypeStruct((rows, kv_local * head_dim), BF16),
            jax.ShapeDtypeStruct((rows, kv_local * head_dim), BF16),
        ],
        cost_estimate=pl.CostEstimate(flops=16 * rows * queries.shape[1] * seq_len, bytes_accessed=rows * queries.shape[1] * 8, transcendentals=rows * seq_len * group_size * kv_local),
        name="attention",
    )(lens, queries, kv, kv, cos_tab, sin_tab)


def rows_norm_kernel(x_ref, gain_ref, *rest):
    out_ref = rest[-1]
    x32 = x_ref[...].astype(F32)
    inv_rms = lax.rsqrt(jnp.mean(x32 * x32, axis=-1, keepdims=True) + EPS)
    out_ref[...] = (x32 * inv_rms * gain_ref[...]).astype(BF16)


def rows_norm(x_rows, gain, first_row, rows, deps):
    width = x_rows.shape[1]
    block = 128
    return pl.pallas_call(
        rows_norm_kernel,
        grid=(rows // block,),
        in_specs=[pl.BlockSpec((block, width), lambda i: (first_row // block + i, 0)), pl.BlockSpec((1, width), lambda i: (0, 0))] + [ANY] * len(deps),
        out_specs=pl.BlockSpec((block, width), lambda i: (i, 0)),
        out_shape=jax.ShapeDtypeStruct((rows, width), BF16),
        cost_estimate=pl.CostEstimate(flops=rows * width * 400, bytes_accessed=rows * width * 4, transcendentals=0),
        name="rows_norm",
    )(x_rows, gain, *deps)


def hidden_norm_kernel(h_ref, gain_ref, *rest):
    out_ref = rest[-1]
    parts, _, cols = h_ref.shape
    total = 0.0
    for part in range(parts):
        h32 = h_ref[part].astype(F32)
        total = total + jnp.sum(h32 * h32, axis=-1, keepdims=True)
    inv_rms = lax.rsqrt(total / (parts * cols) + EPS)
    for part in range(parts):
        span = slice(part * cols, (part + 1) * cols)
        out_ref[:, span] = (h_ref[part].astype(F32) * inv_rms * gain_ref[:, span]).astype(BF16)


def hidden_norm(hidden, gain, deps):
    parts, rows, cols = hidden.shape
    block = 128
    width = parts * cols
    return pl.pallas_call(
        hidden_norm_kernel,
        grid=(rows // block,),
        in_specs=[pl.BlockSpec((parts, block, cols), lambda i: (0, i, 0)), pl.BlockSpec((1, width), lambda i: (0, 0))] + [ANY] * len(deps),
        out_specs=pl.BlockSpec((block, width), lambda i: (i, 0)),
        out_shape=jax.ShapeDtypeStruct((rows, width), BF16),
        cost_estimate=pl.CostEstimate(flops=rows * width * 400, bytes_accessed=rows * width * 4, transcendentals=0),
        name="hidden_norm",
    )(hidden, gain, *deps)


def out_proj_kernel(n_far, place_ref, heads_ref, x_ref, own_ref, near_ref, *rest):
    far_refs, h_ref = rest[:n_far], rest[-1]
    tp_index, dp_index = place_ref[0], place_ref[1]
    total = x_ref[...].astype(F32)
    half = far_refs[0].shape[0]
    for hop, block in enumerate((own_ref, near_ref)):
        total = total + jnp.dot(heads_ref[tp_index ^ hop], block[...], preferred_element_type=F32).astype(BF16).astype(F32)
    for hop in range(2, 2 + len(far_refs) // 2):
        part = 0.0
        for side in range(2):
            start = pl.multiple_of((dp_index ^ side) * half, half)
            part = part + jnp.dot(heads_ref[tp_index ^ hop, :, pl.ds(start, half)], far_refs[2 * (hop - 2) + side][...], preferred_element_type=F32)
        total = total + part.astype(BF16).astype(F32)
    h_ref[...] = total.astype(BF16)


def out_proj(place, heads, x_rows, w_out, near, far, first_row, deps):
    parts, rows, width = heads.shape
    cols = near.shape[1]
    block = 256
    steps = cols // block
    half = far[0].shape[0]
    return pl.pallas_call(
        functools.partial(out_proj_kernel, len(far)),
        grid_spec=pltpu.PrefetchScalarGridSpec(
            num_scalar_prefetch=1,
            grid=(steps,),
            in_specs=[
                pl.BlockSpec((parts, rows, width), lambda n, place: (0, 0, 0)),
                pl.BlockSpec((rows, block), lambda n, place: (first_row // rows, place[0] * steps + n)) if first_row % rows == 0 else pl.BlockSpec((pl.Element(rows), pl.Element(block)), lambda n, place: (first_row, (place[0] * steps + n) * block)),
                pl.BlockSpec((width, block), lambda n, place: (0, place[0] * steps + n)),
                pl.BlockSpec((width, block), lambda n, place: (0, n)),
            ] + [pl.BlockSpec((half, block), lambda n, place: (0, n))] * len(far) + [ANY] * len(deps),
            out_specs=pl.BlockSpec((rows, block), lambda n, place: (0, n)),
        ),
        out_shape=jax.ShapeDtypeStruct((rows, cols), BF16),
        compiler_params=pltpu.CompilerParams(vmem_limit_bytes=56 * 2**20),
        cost_estimate=pl.CostEstimate(flops=2 * parts * rows * width * cols, bytes_accessed=parts * (rows + cols) * width * 2, transcendentals=0),
        name="out_proj",
    )(place, heads, x_rows, w_out, near, *far, *deps)


def sum_kernel(place_ref, received_ref, h_ref, *rest):
    out_ref = rest[-1]
    parts, _, cols = h_ref.shape
    for part in range(parts):
        span = slice(part * cols, (part + 1) * cols)
        total = received_ref[0, :, span].astype(F32)
        for source in range(1, parts):
            total = total + received_ref[source, :, span].astype(F32)
        out_ref[:, span] = (h_ref[part].astype(F32) + total).astype(BF16)


def sum_rows(place, received, hidden, deps):
    parts, rows, width = received.shape
    cols = hidden.shape[2]
    block = 48
    steps = rows // block
    return pl.pallas_call(
        sum_kernel,
        grid_spec=pltpu.PrefetchScalarGridSpec(
            num_scalar_prefetch=1,
            grid=(steps,),
            in_specs=[
                pl.BlockSpec((parts, block, width), lambda i, place: (0, i, 0)),
                pl.BlockSpec((parts, block, cols), lambda i, place: (0, place[0] * steps + i, 0)),
            ] + [ANY] * len(deps),
            out_specs=pl.BlockSpec((block, width), lambda i, place: (i, 0)),
        ),
        out_shape=jax.ShapeDtypeStruct((rows, width), BF16),
        cost_estimate=pl.CostEstimate(flops=rows * width * 600, bytes_accessed=rows * width * 12, transcendentals=0),
        name="sum_rows",
    )(place, received, hidden, *deps)


def store_kernel(*refs):
    refs[-1][...] = refs[0][...]


def store_rows(y, y_part, first_row, total_rows, deps):
    rows, width = y_part.shape
    block = 128
    return pl.pallas_call(
        store_kernel,
        grid=(rows // block,),
        in_specs=[pl.BlockSpec((block, width), lambda i: (i, 0))] + [ANY] * (len(deps) + (y is not None)),
        out_specs=pl.BlockSpec((block, width), lambda i: (first_row // block + i, 0)),
        out_shape=jax.ShapeDtypeStruct((total_rows, width), BF16),
        input_output_aliases={} if y is None else {1: 0},
        cost_estimate=pl.CostEstimate(flops=rows * width * 300, bytes_accessed=rows * width * 4, transcendentals=0),
        name="store_rows",
    )(*([y_part] if y is None else [y_part, y]), *deps)


def solution(mesh):
    tp_size = mesh.shape["tp"]
    dp_size = mesh.shape["dp"]

    def layer_shard(x, seq_lens, w_query, w_key, w_value, w_out, w_gate, w_up, w_down, attn_gain, mlp_gain, k_cache, v_cache):
        batch_size, seq_len, width = x.shape
        kv_local, head_dim = k_cache.shape[2:]
        q_width = w_query.shape[1]
        tp_index = lax.axis_index("tp")
        dp_index = lax.axis_index("dp")
        place = jnp.stack([tp_index, dp_index]).astype(jnp.int32)
        part_cols = width // tp_size
        total_rows = batch_size * seq_len
        x_rows = x.reshape(total_rows, width)
        chunks = len(CHUNKS)
        first = [sum(CHUNKS[:c]) for c in range(chunks)]

        half = q_width // dp_size
        swaps = [[(i, i ^ hop) for i in range(tp_size)] for hop in range(tp_size)]
        dp_ring = [(i, (i + 1) % dp_size) for i in range(dp_size)]
        mine = []
        other = []
        for hop in range(2, tp_size):
            block = lax.dynamic_slice(w_out, (dp_index * half, (tp_index ^ hop) * part_cols), (half, part_cols))
            mine.append(lax.ppermute(block, "tp", swaps[hop]))
            other.append(lax.ppermute(mine[-1], "dp", dp_ring))
        block = lax.dynamic_slice_in_dim(w_out, (tp_index ^ 1) * part_cols, part_cols, axis=1)
        near = lax.ppermute(block, "tp", swaps[1])

        w_kv = jnp.concatenate([w_key, w_value], axis=1)
        cos_tab, sin_tab = rope_tables(seq_len, head_dim)
        gain = attn_gain.astype(F32).reshape(1, width)
        mlp_gain32 = mlp_gain.astype(F32).reshape(1, width)

        heads = []
        new_keys = []
        new_values = []
        deps = []
        for c in range(chunks):
            rows = CHUNKS[c] * seq_len
            if c >= 3:
                deps = deps + [mine[c - 3]]
            normed = rows_norm(x_rows, gain, first[c] * seq_len, rows, deps)
            queries = jnp.dot(normed, w_query, preferred_element_type=F32)
            kv = jnp.dot(normed, w_kv, preferred_element_type=F32)
            out, keys, values = attention(seq_lens, queries, kv, cos_tab, sin_tab, first[c], CHUNKS[c], seq_len, head_dim)
            deps = [out]
            heads.append(lax.all_gather(out, "tp", axis=0))
            new_keys.append(keys)
            new_values.append(values)

        hidden = {}
        received = {}
        gathered = {}
        y = None

        def project(c, deps):
            local = out_proj(place, heads[c], x_rows, w_out, near, [mine[0], other[0], mine[1], other[1]], first[c] * seq_len, deps)
            hidden[c] = lax.all_gather(local, "tp", axis=0)
            return [local]

        def finish(c, deps):
            y_rows = sum_rows(place, received[c], hidden[c], deps)
            gathered[c] = lax.all_gather(y_rows, "tp", axis=0, tiled=True)
            return [y_rows]

        def store(c, y, deps):
            return store_rows(y, gathered[c], first[c] * seq_len, total_rows, deps)

        deps = project(0, deps)
        deps = project(1, deps)
        for c in range(chunks):
            rows = CHUNKS[c] * seq_len
            normed = hidden_norm(hidden[c], mlp_gain32, deps)
            gate = lax.optimization_barrier(jnp.dot(normed, w_gate, preferred_element_type=F32))
            up = jnp.dot(normed, w_up, preferred_element_type=F32)
            gated = lax.optimization_barrier((jax.nn.silu(gate) * up).astype(BF16))
            part = jnp.dot(gated, w_down, preferred_element_type=F32).astype(BF16)
            received[c] = lax.all_to_all(part.reshape(tp_size, rows // tp_size, width), "tp", 0, 0, tiled=True)
            deps = [part]
            if c >= 1:
                deps = finish(c - 1, deps)
            if c >= 2:
                y = store(c - 2, y, deps)
                deps = [y]
            if c + 2 < chunks:
                deps = project(c + 2, deps)
        y = store(chunks - 2, y, [])
        finish(chunks - 1, [])
        y = store(chunks - 1, y, [])

        def cache(old, new):
            new = jnp.concatenate(new, axis=0).reshape(batch_size, seq_len, kv_local, head_dim)
            return lax.dynamic_update_slice(old, new, (0, 0, 0, 0))

        return y.reshape(x.shape), cache(k_cache, new_keys), cache(v_cache, new_values)

    cache_spec = P("dp", None, "tp", None)
    return jax.shard_map(layer_shard, mesh=mesh, in_specs=(P("dp", None, None), P("dp"), P(None, "tp"), P(None, "tp"), P(None, "tp"), P("tp", None), P(None, "tp"), P(None, "tp"), P("tp", None), P(), P(), cache_spec, cache_spec), out_specs=(P("dp", None, None), cache_spec, cache_spec), check_vma=False)
```

time: 2900 us -> 1830 us (0.63)
  waiting for transfers between devices: 987 us -> 158 us
  Pallas kernels: 0 us -> 453 us
  blocking collectives: 498 us -> 127 us
  other arithmetic: 240 us -> 2.62 us
  local copies, waits for them, and re-layouts: 139 us -> 45.4 us
    all_gather x2 -> x15, waiting for transfers between devices: 511 us -> 9.71 us  [the longest x5 4.95 us: project(): hidden[c] = lax.all_gather(local, 'tp', axis=0)]
    pallas_call x0 -> x30, Pallas kernels: none -> 453 us  [the longest x5 138 us: attention(): pl.pallas_call(functools.partial(attention_kernel, first_seq, group_size,...]
    all_to_all x1 -> x4, waiting for transfers between devices: 476 us -> 94.3 us  [layer_shard(): lax.all_to_all(part.reshape(tp_size, rows // tp_size, width), 'tp', 0, 0,...]
    all_to_all x1, blocking collectives: 498 us -> 127 us  [layer_shard(): lax.all_to_all(part.reshape(tp_size, rows // tp_size, width), 'tp', 0, 0,...]
    reduce_sum x4 -> x0, other arithmetic: 80.4 us -> none  [the longest x2 58.2 us: sum_partials(): summed = jnp.sum(received.astype(jnp.float32), axis=1)]
    sub x1 -> x0, other arithmetic: 69 us -> none  [causal_attention(): probs = jax.nn.softmax(scores, axis=-1).astype(jnp.bfloat16)]
    reshape x2 -> x6, local copies, waits for them, and re-layouts: 59.1 us -> 4.69 us  [the longest x2 2.78 us: cache(): jnp.concatenate(new, axis=0)]
    ppermute x0 -> x5, waiting for transfers between devices: none -> 52.5 us  [the longest x2 52.5 us: layer_shard(): mine.append(lax.ppermute(block, 'tp', swaps[hop]))]
  transfers between devices with their start and end apart: 3 -> 24, of which waited for: 3 -> 5; matrix products, arithmetic and copies ran while one was open for 0% -> 55% of each run, Pallas kernels for 0% -> 23%
where the time goes in v1:
time: 1830 us; the launch traced here: 1820 us
  matrix products  991 us (54%)
  Pallas kernels  453 us (25%)
  waiting for transfers between devices  158 us (9%)
  blocking collectives  127 us (7%)
  local copies, waits for them, and re-layouts  45.4 us (2%)
  starting transfers between devices  31.9 us (2%)
    dot_general x5, matrix products, layer_shard(): up = jnp.dot(normed, w_up, preferred_element_type=F32)  284 us
    dot_general x5, matrix products, layer_shard(): jnp.dot(normed, w_gate, preferred_element_type=F32)  283 us
    dot_general x5, matrix products, layer_shard(): part = jnp.dot(gated, w_down, preferred_element_type=F32).astype(BF16)  269 us
    pallas_call x5, Pallas kernels, attention(): pl.pallas_call(functools.partial(attention_kernel, first_seq, group_size,...  138 us
    pallas_call x5, Pallas kernels, out_proj(): pl.pallas_call(functools.partial(out_proj_kernel, len(far)), grid_spec=pl...  134 us
    all_to_all x1, blocking collectives, layer_shard(): lax.all_to_all(part.reshape(tp_size, rows // tp_size, width), 'tp', 0, 0,...  127 us
    dot_general x5, matrix products, layer_shard(): queries = jnp.dot(normed, w_query, preferred_element_type=F32)  110 us
    all_to_all x4, waiting for transfers between devices, layer_shard(): lax.all_to_all(part.reshape(tp_size, rows // tp_size, width), 'tp', 0, 0,...  94.3 us
  transfers between devices with their start and end apart: 24, of which 5 were waited for; matrix products, arithmetic and copies ran while one was open for 55% of the time, Pallas kernels for 23%

profile of v1, /device:TPU:0, one launch (start us, length us, event | category | flops | bytes accessed | tf_op | source)
XLA Modules:
  0.0 1823.2 jit_solution(6737529755555669869)
XLA Ops:
  7.2 5.9 copy.59
  18.3 7.5 rows_norm.5
  30.1 8.7 fusion.3.k_ref.v_ref
  38.8 15.2 fusion.2.q_ref
  56.3 18.4 %attention.5 = (bf16[384,1792]{1,0:T(8,128)(2,1)}, bf16[384,256]{1,0:T(8,128)(2,1)}, bf16[384,256]{1,0:T(8,128)(2,1)}) custom-call(s32[8]{0:T(128)} %lens_ref.9, f32[384,1792]{1,0:T(8,128)} %fusion.2.q_ref, f32[384,512]{1,0:T(8,128)} %fusion.3.k_ref.v_ref, f32[384,512]{1,0:T(8,128)} %fusion.3.k_ref.v_ref, f32[384,128]{1,0:T(8,128)} %copy.31.cos_ref, ...), custom_call_target="tpu_custom_call" | custom-call | flops 4227858432 | bytes 5505024 | tf_op jit(solution)/shard_map/attention/pallas_call | solution.py:68
  74.7 6.1 fusion.1
  84.3 6.2 constant_dynamic-slice_fusion
  90.7 12.2 rows_norm.6
  102.9 11.8 fusion.5.k_ref.v_ref
  114.7 26.0 %fusion.4.q_ref = f32[768,1792]{1,0:T(8,128)} fusion(bf16[768,7168]{1,0:T(8,128)(2,1)S(1)} %copy-done.1, bf16[7168,1792]{1,0:T(8,128)(2,1)} %param.15), kind=kOutput, calls=%fused_computation.35 | convolution fusion | flops 19730006016 | bytes 42205184 | tf_op jit(solution)/shard_map/dot_general | solution.py:272
  140.7 33.6 %attention.6 = (bf16[768,1792]{1,0:T(8,128)(2,1)}, bf16[768,256]{1,0:T(8,128)(2,1)}, bf16[768,256]{1,0:T(8,128)(2,1)}) custom-call(s32[8]{0:T(128)} %lens_ref.9, f32[768,1792]{1,0:T(8,128)} %fusion.4.q_ref, f32[768,512]{1,0:T(8,128)} %fusion.5.k_ref.v_ref, f32[768,512]{1,0:T(8,128)} %fusion.5.k_ref.v_ref, f32[384,128]{1,0:T(8,128)} %copy.31.cos_ref, ...), custom_call_target="tpu_custom_call" | custom-call | flops 8455716864 | bytes 11010048 | tf_op jit(solution)/shard_map/attention/pallas_call | solution.py:68
  174.3 13.6 rows_norm.7
  187.9 26.8 %fusion.6.q_ref = f32[768,1792]{1,0:T(8,128)} fusion(bf16[768,7168]{1,0:T(8,128)(2,1)} %rows_norm.7, bf16[7168,1792]{1,0:T(8,128)(2,1)} %param.15), kind=kOutput, calls=%fused_computation.37 | convolution fusion | flops 19730006016 | bytes 42205184 | tf_op jit(solution)/shard_map/dot_general | solution.py:272
  215.3 7.0 fusion.7.k_ref.v_ref
  222.3 33.7 %attention.7 = (bf16[768,1792]{1,0:T(8,128)(2,1)}, bf16[768,256]{1,0:T(8,128)(2,1)}, bf16[768,256]{1,0:T(8,128)(2,1)}) custom-call(s32[8]{0:T(128)} %lens_ref.9, f32[768,1792]{1,0:T(8,128)} %fusion.6.q_ref, f32[768,512]{1,0:T(8,128)} %fusion.7.k_ref.v_ref, f32[768,512]{1,0:T(8,128)} %fusion.7.k_ref.v_ref, f32[384,128]{1,0:T(8,128)} %copy.31.cos_ref, ...), custom_call_target="tpu_custom_call" | custom-call | flops 8455716864 | bytes 11010048 | tf_op jit(solution)/shard_map/attention/pallas_call | solution.py:68
  258.0 52.5 %collective-permute-done.1.rest_1_.rest_2_ = bf16[896,1792]{1,0:T(8,128)(2,1)} collective-permute-done((bf16[896,1792]{1,0:T(8,128)(2,1)}, bf16[896,1792]{1,0:T(8,128)(2,1)}, u32[]{:S(2)}, u32[]{:S(2)}) %collective-permute-start.1) | collective-permute-done | bytes 3211296 | tf_op jit(solution)/shard_map/ppermute | solution.py:253
  312.4 12.0 rows_norm.8
  324.4 26.8 %fusion.8.q_ref = f32[768,1792]{1,0:T(8,128)} fusion(bf16[768,7168]{1,0:T(8,128)(2,1)} %rows_norm.8, bf16[7168,1792]{1,0:T(8,128)(2,1)} %param.15), kind=kOutput, calls=%fused_computation.39 | convolution fusion | flops 19730006016 | bytes 42205184 | tf_op jit(solution)/shard_map/dot_general | solution.py:272
  351.2 9.0 fusion.9.k_ref.v_ref
  360.1 33.8 %attention.8 = (bf16[768,1792]{1,0:T(8,128)(2,1)}, bf16[768,256]{1,0:T(8,128)(2,1)}, bf16[768,256]{1,0:T(8,128)(2,1)}) custom-call(s32[8]{0:T(128)} %lens_ref.9, f32[768,1792]{1,0:T(8,128)} %fusion.8.q_ref, f32[768,512]{1,0:T(8,128)} %fusion.9.k_ref.v_ref, f32[768,512]{1,0:T(8,128)} %fusion.9.k_ref.v_ref, f32[384,128]{1,0:T(8,128)} %copy.31.cos_ref, ...), custom_call_target="tpu_custom_call" | custom-call | flops 8455716864 | bytes 11010048 | tf_op jit(solution)/shard_map/attention/pallas_call | solution.py:68
  394.0 7.4 rows_norm.9
  401.3 8.7 fusion.11.k_ref.v_ref
  410.1 15.2 fusion.10.q_ref
  425.3 18.6 %attention.9 = (bf16[384,1792]{1,0:T(8,128)(2,1)}, bf16[384,256]{1,0:T(8,128)(2,1)}, bf16[384,256]{1,0:T(8,128)(2,1)}) custom-call(s32[8]{0:T(128)} %lens_ref.9, f32[384,1792]{1,0:T(8,128)} %fusion.10.q_ref, f32[384,512]{1,0:T(8,128)} %fusion.11.k_ref.v_ref, f32[384,512]{1,0:T(8,128)} %fusion.11.k_ref.v_ref, f32[384,128]{1,0:T(8,128)} %copy.31.cos_ref, ...), custom_call_target="tpu_custom_call" | custom-call | flops 4227858432 | bytes 5505024 | tf_op jit(solution)/shard_map/attention/pallas_call | solution.py:68
  445.6 19.2 %out_proj.5.rest_4_ = bf16[384,1792]{1,0:T(8,128)(2,1)} custom-call(s32[2]{0:T(128)} %pad_add_fusion.place_ref, bf16[4,384,1792]{2,1,0:T(8,128)(2,1)} %bitcast.107, bf16[3072,7168]{1,0:T(8,128)(2,1)} %bitcast.80, bf16[1792,7168]{1,0:T(8,128)(2,1)} %own_ref.9, bf16[1792,1792]{1,0:T(8,128)(2,1)} %collective-permute-done.2.near_ref, ...), custom_call_target="tpu_custom_call" | custom-call | flops 9865003008 | bytes 31195136 | tf_op jit(solution)/shard_map/out_proj/pallas_call | solution.py:157
  465.5 32.4 %out_proj.6.rest_0_ = bf16[768,1792]{1,0:T(8,128)(2,1)} custom-call(s32[2]{0:T(128)} %pad_add_fusion.place_ref, bf16[4,768,1792]{2,1,0:T(8,128)(2,1)} %bitcast.101, bf16[3072,7168]{1,0:T(8,128)(2,1)} %bitcast.81, bf16[1792,7168]{1,0:T(8,128)(2,1)} %own_ref.9, bf16[1792,1792]{1,0:T(8,128)(2,1)} %collective-permute-done.2.near_ref, ...), custom_call_target="tpu_custom_call" | custom-call | flops 19730006016 | bytes 36700160 | tf_op jit(solution)/shard_map/out_proj/pallas_call | solution.py:157
  503.5 8.1 hidden_norm.5
  511.7 40.1 %fusion.12 = f32[384,5120]{1,0:T(8,128)} fusion(bf16[384,7168]{1,0:T(8,128)(2,1)} %hidden_norm.5, bf16[7168,5120]{1,0:T(8,128)(2,1)} %param.19), kind=kOutput, calls=%fused_computation.43 | convolution fusion | flops 28185722880 | bytes 86769664 | tf_op jit(solution)/shard_map/dot_general | solution.py:303
  551.8 40.7 %multiply_convert_fusion.4 = bf16[384,5120]{1,0:T(8,128)(2,1)} fusion(f32[384,5120]{1,0:T(8,128)} %fusion.12, bf16[384,7168]{1,0:T(8,128)(2,1)} %hidden_norm.5, bf16[7168,5120]{1,0:T(8,128)(2,1)} %param.20), kind=kOutput, calls=%fused_computation.9 | convolution fusion | flops 28197519360 | bytes 90701824 | tf_op jit(solution)/shard_map/dot_general | solution.py:304
  592.5 37.7 %convolution_convert_fusion.4.rest_4_ = bf16[384,7168]{1,0:T(8,128)(2,1)} fusion(bf16[384,5120]{1,0:T(8,128)(2,1)} %multiply_convert_fusion.4, bf16[5120,7168]{1,0:T(8,128)(2,1)} %param.21), kind=kOutput, calls=%fused_computation.7 | convolution fusion | flops 28188475392 | bytes 82837504 | tf_op jit(solution)/shard_map/dot_general | solution.py:306
  630.2 5.1 all-to-all-start
  635.4 30.9 %out_proj.7.rest_0_ = bf16[768,1792]{1,0:T(8,128)(2,1)} custom-call(s32[2]{0:T(128)} %pad_add_fusion.place_ref, bf16[4,768,1792]{2,1,0:T(8,128)(2,1)} %bitcast.103, bf16[3072,7168]{1,0:T(8,128)(2,1)} %bitcast.82, bf16[1792,7168]{1,0:T(8,128)(2,1)} %own_ref.9, bf16[1792,1792]{1,0:T(8,128)(2,1)} %collective-permute-done.2.near_ref, ...), custom_call_target="tpu_custom_call" | custom-call | flops 19730006016 | bytes 36700160 | tf_op jit(solution)/shard_map/out_proj/pallas_call | solution.py:157
  666.3 12.2 hidden_norm.6
  678.6 67.9 %fusion.13 = f32[768,5120]{1,0:T(8,128)} fusion(bf16[768,7168]{1,0:T(8,128)(2,1)} %hidden_norm.6, bf16[7168,5120]{1,0:T(8,128)(2,1)} %param.19), kind=kOutput, calls=%fused_computation.44 | convolution fusion | flops 56371445760 | bytes 100139008 | tf_op jit(solution)/shard_map/dot_general | solution.py:303
  746.5 67.3 %multiply_convert_fusion.2 = bf16[768,5120]{1,0:T(8,128)(2,1)S(1)} fusion(f32[768,5120]{1,0:T(8,128)} %fusion.13, bf16[768,7168]{1,0:T(8,128)(2,1)} %hidden_norm.6, bf16[7168,5120]{1,0:T(8,128)(2,1)} %param.20), kind=kOutput, calls=%fused_computation.2 | convolution fusion | flops 56395038720 | bytes 108003328 | tf_op jit(solution)/shard_map/dot_general | solution.py:304
  813.7 63.9 %convolution_convert_fusion.2.rest_0_ = bf16[768,7168]{1,0:T(8,128)(2,1)} fusion(bf16[768,5120]{1,0:T(8,128)(2,1)S(1)} %multiply_convert_fusion.2, bf16[5120,7168]{1,0:T(8,128)(2,1)} %param.21), kind=kOutput, calls=%fused_computation.5 | convolution fusion | flops 56376950784 | bytes 92274688 | tf_op jit(solution)/shard_map/dot_general | solution.py:306
  883.4 32.5 %out_proj.8.rest_0_ = bf16[768,1792]{1,0:T(8,128)(2,1)} custom-call(s32[2]{0:T(128)} %pad_add_fusion.place_ref, bf16[4,768,1792]{2,1,0:T(8,128)(2,1)} %bitcast.102, bf16[3072,7168]{1,0:T(8,128)(2,1)} %bitcast.83, bf16[1792,7168]{1,0:T(8,128)(2,1)} %own_ref.9, bf16[1792,1792]{1,0:T(8,128)(2,1)} %collective-permute-done.2.near_ref, ...), custom_call_target="tpu_custom_call" | custom-call | flops 19730006016 | bytes 36700160 | tf_op jit(solution)/shard_map/out_proj/pallas_call | solution.py:157
  915.9 12.1 hidden_norm.7
  928.0 68.9 %fusion.14 = f32[768,5120]{1,0:T(8,128)} fusion(bf16[768,7168]{1,0:T(8,128)(2,1)} %hidden_norm.7, bf16[7168,5120]{1,0:T(8,128)(2,1)} %param.19), kind=kOutput, calls=%fused_computation.45 | convolution fusion | flops 56371445760 | bytes 100139008 | tf_op jit(solution)/shard_map/dot_general | solution.py:303
  997.0 69.5 %multiply_convert_fusion.1 = bf16[768,5120]{1,0:T(8,128)(2,1)} fusion(f32[768,5120]{1,0:T(8,128)} %fusion.14, bf16[768,7168]{1,0:T(8,128)(2,1)} %hidden_norm.7, bf16[7168,5120]{1,0:T(8,128)(2,1)} %param.20), kind=kOutput, calls=%fused_computation.1 | convolution fusion | flops 56395038720 | bytes 108003328 | tf_op jit(solution)/shard_map/dot_general | solution.py:304
  1066.4 6.1 all-to-all-start.1
  1072.6 65.8 %convolution_convert_fusion.1.rest_0_ = bf16[768,7168]{1,0:T(8,128)(2,1)} fusion(bf16[768,5120]{1,0:T(8,128)(2,1)} %multiply_convert_fusion.1, bf16[5120,7168]{1,0:T(8,128)(2,1)} %param.21), kind=kOutput, calls=%fused_computation.4 | convolution fusion | flops 56376950784 | bytes 92274688 | tf_op jit(solution)/shard_map/dot_general | solution.py:306
  1138.5 55.4 %all-to-all-done.1.received_ref = bf16[4,192,7168]{2,1,0:T(8,128)(2,1)} async-done(((bf16[4,192,7168]{2,1,0:T(8,128)(2,1)}), bf16[4,192,7168]{2,1,0:T(8,128)(2,1)}, u32[]{:S(2)}, u32[]{:S(2)}) %all-to-all-start.1) | async-done | bytes 11010080 | tf_op jit(solution)/shard_map/all_to_all | solution.py:307
  1193.8 7.9 sum_rows.6.refs_1_
  1201.7 6.5 all-to-all-start.2
  1208.3 6.8 store_rows.5.rest_4_.refs_1_
  1215.1 19.2 %out_proj.9.rest_0_ = bf16[384,1792]{1,0:T(8,128)(2,1)} custom-call(s32[2]{0:T(128)} %pad_add_fusion.place_ref, bf16[4,384,1792]{2,1,0:T(8,128)(2,1)} %bitcast.104, bf16[3072,7168]{1,0:T(8,128)(2,1)} %bitcast.84, bf16[1792,7168]{1,0:T(8,128)(2,1)} %own_ref.9, bf16[1792,1792]{1,0:T(8,128)(2,1)} %collective-permute-done.2.near_ref, ...), custom_call_target="tpu_custom_call" | custom-call | flops 9865003008 | bytes 31195136 | tf_op jit(solution)/shard_map/out_proj/pallas_call | solution.py:157
  1234.4 12.1 hidden_norm.8
  1246.4 67.9 %fusion.15 = f32[768,5120]{1,0:T(8,128)} fusion(bf16[768,7168]{1,0:T(8,128)(2,1)} %hidden_norm.8, bf16[7168,5120]{1,0:T(8,128)(2,1)} %param.19), kind=kOutput, calls=%fused_computation.46 | convolution fusion | flops 56371445760 | bytes 100139008 | tf_op jit(solution)/shard_map/dot_general | solution.py:303
  1314.3 67.0 %multiply_convert_fusion = bf16[768,5120]{1,0:T(8,128)(2,1)S(1)} fusion(f32[768,5120]{1,0:T(8,128)} %fusion.15, bf16[768,7168]{1,0:T(8,128)(2,1)} %hidden_norm.8, bf16[7168,5120]{1,0:T(8,128)(2,1)} %param.20), kind=kOutput, calls=%fused_computation | convolution fusion | flops 56395038720 | bytes 108003328 | tf_op jit(solution)/shard_map/dot_general | solution.py:304
  1381.4 63.9 %convolution_convert_fusion.rest_0_ = bf16[768,7168]{1,0:T(8,128)(2,1)} fusion(bf16[768,5120]{1,0:T(8,128)(2,1)S(1)} %multiply_convert_fusion, bf16[5120,7168]{1,0:T(8,128)(2,1)} %param.21), kind=kOutput, calls=%fused_computation.3 | convolution fusion | flops 56376950784 | bytes 92274688 | tf_op jit(solution)/shard_map/dot_general | solution.py:306
  1445.3 6.0 all-to-all-start.4
  1451.3 7.8 sum_rows.7.refs_2_
  1459.3 10.3 store_rows.6.rest_0_.refs_1_
  1469.6 7.9 hidden_norm.9
  1477.5 38.4 %fusion.16 = f32[384,5120]{1,0:T(8,128)} fusion(bf16[384,7168]{1,0:T(8,128)(2,1)} %hidden_norm.9, bf16[7168,5120]{1,0:T(8,128)(2,1)} %param.19), kind=kOutput, calls=%fused_computation.47 | convolution fusion | flops 28185722880 | bytes 86769664 | tf_op jit(solution)/shard_map/dot_general | solution.py:303
  1515.9 39.2 %multiply_convert_fusion.3 = bf16[384,5120]{1,0:T(8,128)(2,1)} fusion(f32[384,5120]{1,0:T(8,128)} %fusion.16, bf16[384,7168]{1,0:T(8,128)(2,1)} %hidden_norm.9, bf16[7168,5120]{1,0:T(8,128)(2,1)} %param.20), kind=kOutput, calls=%fused_computation.8 | convolution fusion | flops 28197519360 | bytes 90701824 | tf_op jit(solution)/shard_map/dot_general | solution.py:304
  1555.0 37.6 %convolution_convert_fusion.3.rest_0_ = bf16[384,7168]{1,0:T(8,128)(2,1)} fusion(bf16[384,5120]{1,0:T(8,128)(2,1)} %multiply_convert_fusion.3, bf16[5120,7168]{1,0:T(8,128)(2,1)} %param.21), kind=kOutput, calls=%fused_computation.6 | convolution fusion | flops 28188475392 | bytes 82837504 | tf_op jit(solution)/shard_map/dot_general | solution.py:306
  1592.7 38.9 %all-to-all-done.4.received_ref = bf16[4,192,7168]{2,1,0:T(8,128)(2,1)} async-done(((bf16[4,192,7168]{2,1,0:T(8,128)(2,1)}), bf16[4,192,7168]{2,1,0:T(8,128)(2,1)}, u32[]{:S(2)}, u32[]{:S(2)}) %all-to-all-start.4) | async-done | bytes 11010080 | tf_op jit(solution)/shard_map/all_to_all | solution.py:307
  1631.6 7.8 sum_rows.9.refs_2_
  1639.5 126.5 %all_to_all.25.received_ref = bf16[4,96,7168]{2,1,0:T(8,128)(2,1)} all-to-all(bf16[4,96,7168]{2,1,0:T(8,128)(2,1)} %bitcast.97), channel_id=1, replica_groups=mesh['dp'=2,'tp'=4] {'tp'}, dimensions={0} | all-to-all | bytes 11010048 | tf_op jit(solution)/shard_map/all_to_all | solution.py:307
  1786.6 9.6 store_rows.7.refs_1_
  1796.1 9.6 store_rows.8.refs_1_
  1810.3 5.9 store_rows.9
  (126 shorter events, 59.1 us)
Async XLA Ops:
  7.2 8.4 copy-start.12
  7.2 5.9 copy-start.6
  7.2 436.8 %all-gather.38.cloned.1.call-start = ((), (), s32[]{:S(2)}) async-start(), calls=%async_computation.11 | async-start | bytes 6881280 | tf_op jit(solution)/shard_map/all_gather | solution.py:276
  7.2 9.0 copy-start.5
  25.8 13.0 slice-start
  30.1 8.7 slice-start.1
  74.7 390.8 %all-gather.42.cloned.1.call-start = ((), (), s32[]{:S(2)}) async-start(), calls=%async_computation.13 | async-start | bytes 13762560 | tf_op jit(solution)/shard_map/all_gather | solution.py:276
  80.8 175.2 %collective-permute-start = (bf16[896,1792]{1,0:T(8,128)(2,1)}, bf16[896,1792]{1,0:T(8,128)(2,1)}, u32[]{:S(2)}, u32[]{:S(2)}) collective-permute-start(bf16[896,1792]{1,0:T(8,128)(2,1)} %get-tuple-element.34), channel_id=1, source_target_pairs={{0,2},{1,3},{2,0},{3,1},{4,6},{5,7},{6,4},{7,5}} | collective-permute-start | bytes 9633800 | tf_op jit(solution)/shard_map/ppermute | solution.py:253
  84.3 226.2 %collective-permute-start.1 = (bf16[896,1792]{1,0:T(8,128)(2,1)}, bf16[896,1792]{1,0:T(8,128)(2,1)}, u32[]{:S(2)}, u32[]{:S(2)}) collective-permute-start(bf16[896,1792]{1,0:T(8,128)(2,1)} %get-tuple-element.33), channel_id=1, source_target_pairs={{0,3},{1,2},{2,1},{3,0},{4,7},{5,6},{6,5},{7,4}} | collective-permute-start | bytes 9633800 | tf_op jit(solution)/shard_map/ppermute | solution.py:253
  90.5 353.5 %collective-permute-start.2 = (bf16[1792,1792]{1,0:T(8,128)(2,1)}, bf16[1792,1792]{1,0:T(8,128)(2,1)}, u32[]{:S(2)}, u32[]{:S(2)}) collective-permute-start(bf16[1792,1792]{1,0:T(8,128)(2,1)} %constant_dynamic-slice_fusion), channel_id=1, source_target_pairs={{0,1},{1,0},{2,3},{3,2},{4,5},{5,4},{6,7},{7,6}} | collective-permute-start | bytes 19267592 | tf_op jit(solution)/shard_map/ppermute | solution.py:256
  102.9 11.8 copy-start.1
  174.2 329.3 %all-gather.40.cloned.1.call-start = ((), (), s32[]{:S(2)}) async-start(), calls=%async_computation.12 | async-start | bytes 6881280 | tf_op jit(solution)/shard_map/all_gather | solution.py:287
  174.3 41.0 %slice-start.2 = ((s8[7340032]{0:T(1024)(128)(4,1)}), s8[3145728]{0:T(1024)(128)(4,1)S(1)}, s32[]{:S(2)}) async-start(s8[7340032]{0:T(1024)(128)(4,1)} %bitcast.108), calls=%async_computation.22 | async-start | bytes 6291456
  187.9 27.4 %copy-start.2 = (bf16[768,7168]{1,0:T(8,128)(2,1)S(1)}, bf16[768,7168]{1,0:T(8,128)(2,1)}, u32[]{:S(2)}) copy-start(bf16[768,7168]{1,0:T(8,128)(2,1)} %rows_norm.7) | copy-start | bytes 33030148
  187.9 27.4 %slice-start.3 = ((s8[7340032]{0:T(1024)(128)(4,1)}), s8[4194304]{0:T(1024)(128)(4,1)S(1)}, s32[]{:S(2)}) async-start(s8[7340032]{0:T(1024)(128)(4,1)} %bitcast.108), calls=%async_computation.23 | async-start | bytes 8388608
  256.0 187.9 %collective-permute-start.3 = (bf16[896,1792]{1,0:T(8,128)(2,1)}, bf16[896,1792]{1,0:T(8,128)(2,1)S(1)}, u32[]{:S(2)}, u32[]{:S(2)}) collective-permute-start(bf16[896,1792]{1,0:T(8,128)(2,1)} %collective-permute-done.rest_1_.rest_0_), channel_id=1, source_target_pairs={{0,4},{4,0},{1,5},{5,1},{2,6},{6,2},{3,7},{7,3}} | collective-permute-start | bytes 9633800 | tf_op jit(solution)/shard_map/ppermute | solution.py:254
  310.5 133.4 %collective-permute-start.4 = (bf16[896,1792]{1,0:T(8,128)(2,1)}, bf16[896,1792]{1,0:T(8,128)(2,1)}, u32[]{:S(2)}, u32[]{:S(2)}) collective-permute-start(bf16[896,1792]{1,0:T(8,128)(2,1)} %collective-permute-done.1.rest_1_.rest_2_), channel_id=1, source_target_pairs={{0,4},{4,0},{1,5},{5,1},{2,6},{6,2},{3,7},{7,3}} | collective-permute-start | bytes 9633800 | tf_op jit(solution)/shard_map/ppermute | solution.py:254
  324.4 26.8 %copy-start.3 = (bf16[768,7168]{1,0:T(8,128)(2,1)S(1)}, bf16[768,7168]{1,0:T(8,128)(2,1)}, u32[]{:S(2)}) copy-start(bf16[768,7168]{1,0:T(8,128)(2,1)} %rows_norm.8) | copy-start | bytes 33030148
  401.3 8.7 copy-start.4
  443.9 1.7 copy-start
  464.8 170.5 %all-gather.46.cloned.1.call-start = ((), (), s32[]{:S(2)}) async-start(), calls=%async_computation.15 | async-start | bytes 13762560 | tf_op jit(solution)/shard_map/all_gather | solution.py:276
  465.4 200.9 %all-gather.44.cloned.1.call-start = ((), (), s32[]{:S(2)}) async-start(), calls=%async_computation.14 | async-start | bytes 13762560 | tf_op jit(solution)/shard_map/all_gather | solution.py:287
  465.5 32.5 %copy-start.13 = (bf16[7168]{0:T(1024)(128)(2,1)S(1)}, bf16[7168]{0:T(1024)(128)(2,1)}, u32[]{:S(2)}) copy-start(bf16[7168]{0:T(1024)(128)(2,1)} %param.23) | copy-start | bytes 43012
  497.9 385.5 %all-gather.50.cloned.1.call-start = ((), (), s32[]{:S(2)}) async-start(), calls=%async_computation.17 | async-start | bytes 13762560 | tf_op jit(solution)/shard_map/all_gather | solution.py:276
  630.2 247.4 %all-to-all-start = ((bf16[4,96,7168]{2,1,0:T(8,128)(2,1)}), bf16[4,96,7168]{2,1,0:T(8,128)(2,1)}, u32[]{:S(2)}, u32[]{:S(2)}) async-start(bf16[4,96,7168]{2,1,0:T(8,128)(2,1)} %bitcast.100), calls=%async_computation | async-start | bytes 11010048 | tf_op jit(solution)/shard_map/all_to_all | solution.py:307
  635.3 280.6 %all-gather.48.cloned.1.call-start = ((), (), s32[]{:S(2)}) async-start(), calls=%async_computation.16 | async-start | bytes 13762560 | tf_op jit(solution)/shard_map/all_gather | solution.py:287
  666.3 542.0 %all-gather.26.cloned.1.call-start = ((), (), s32[]{:S(2)}) async-start(), calls=%async_computation.5 | async-start | bytes 6881280 | tf_op jit(solution)/shard_map/all_gather | solution.py:292
  882.6 332.5 %all-gather.36.cloned.1.call-start = ((), (), s32[]{:S(2)}) async-start(), calls=%async_computation.10 | async-start | bytes 6881280 | tf_op jit(solution)/shard_map/all_gather | solution.py:276
  883.3 351.0 %all-gather.54.cloned.1.call-start = ((), (), s32[]{:S(2)}) async-start(), calls=%async_computation.19 | async-start | bytes 13762560 | tf_op jit(solution)/shard_map/all_gather | solution.py:287
  1066.4 127.4 %all-to-all-start.1 = ((bf16[4,192,7168]{2,1,0:T(8,128)(2,1)}), bf16[4,192,7168]{2,1,0:T(8,128)(2,1)}, u32[]{:S(2)}, u32[]{:S(2)}) async-start(bf16[4,192,7168]{2,1,0:T(8,128)(2,1)} %bitcast.93), calls=%async_computation.1 | async-start | bytes 22020096 | tf_op jit(solution)/shard_map/all_to_all | solution.py:307
  1072.6 386.7 %all-gather.28.cloned.1.call-start = ((), (), s32[]{:S(2)}) async-start(), calls=%async_computation.6 | async-start | bytes 13762560 | tf_op jit(solution)/shard_map/all_gather | solution.py:292
  1201.7 243.6 %all-to-all-start.2 = ((bf16[4,192,7168]{2,1,0:T(8,128)(2,1)}), bf16[4,192,7168]{2,1,0:T(8,128)(2,1)}, u32[]{:S(2)}, u32[]{:S(2)}) async-start(bf16[4,192,7168]{2,1,0:T(8,128)(2,1)} %bitcast.92), calls=%async_computation.2 | async-start | bytes 22020096 | tf_op jit(solution)/shard_map/all_to_all | solution.py:307
  1208.2 261.3 %all-gather.52.cloned.1.call-start = ((), (), s32[]{:S(2)}) async-start(), calls=%async_computation.18 | async-start | bytes 6881280 | tf_op jit(solution)/shard_map/all_gather | solution.py:287
  1445.3 186.3 %all-to-all-start.4 = ((bf16[4,192,7168]{2,1,0:T(8,128)(2,1)}), bf16[4,192,7168]{2,1,0:T(8,128)(2,1)}, u32[]{:S(2)}, u32[]{:S(2)}) async-start(bf16[4,192,7168]{2,1,0:T(8,128)(2,1)} %bitcast.94), calls=%async_computation.4 | async-start | bytes 22020096 | tf_op jit(solution)/shard_map/all_to_all | solution.py:307
  1451.3 335.3 %all-gather.34.cloned.1.call-start = ((), (), s32[]{:S(2)}) async-start(), calls=%async_computation.9 | async-start | bytes 13762560 | tf_op jit(solution)/shard_map/all_gather | solution.py:292
  1459.2 336.9 %all-gather.32.cloned.1.call-start = ((), (), s32[]{:S(2)}) async-start(), calls=%async_computation.8 | async-start | bytes 13762560 | tf_op jit(solution)/shard_map/all_gather | solution.py:292
  1639.5 170.9 %all-gather.30.cloned.1.call-start = ((), (), s32[]{:S(2)}) async-start(), calls=%async_computation.7 | async-start | bytes 6881280 | tf_op jit(solution)/shard_map/all_gather | solution.py:292
  1766.0 6.8 copy-start.8
  1766.0 6.9 copy-start.10
  1766.0 6.9 copy-start.7
  1766.0 7.7 copy-start.9
  1771.0 6.0 copy-start.11
Sparse Core Ops, SparseCore 0:
  74.8 71.5 all-gather.37
  174.4 130.8 all-gather.41
  464.9 38.5 all-gather.39
  504.9 70.3 all-gather.45
  576.7 77.1 all-gather.43
  655.2 109.7 all-gather.49
  766.6 70.3 all-gather.47
  882.7 40.0 all-gather.25
  924.4 39.1 all-gather.35
  997.1 71.1 all-gather.53
  1201.8 127.4 all-gather.27
  1330.7 69.6 all-gather.51
  1459.3 130.0 all-gather.33
  1639.6 127.2 all-gather.31
  1771.2 39.0 all-gather.29

commit v2 on v1

--- a/solution.py
+++ b/solution.py
@@ -43,26 +43,32 @@
     k_out_ref[...] = keys
     v_out_ref[...] = values
     step = 128
+    turned = []
     for head in range(group_size):
         cols = slice(head * head_dim, (head + 1) * head_dim)
-        queries = turn(q_ref[:, cols], cos_tab, sin_tab, even_lane).astype(BF16)
-        for start in range(0, seq_len, step):
-            stop = start + step
-            scores = lax.dot_general(queries[start:stop], keys[:stop], (((1,), (1,)), ((), ())), preferred_element_type=F32) * head_dim ** -0.5
-            row = lax.broadcasted_iota(jnp.int32, (step, stop), 0) + start
-            col = lax.broadcasted_iota(jnp.int32, (step, stop), 1)
-            scores = jnp.where((col <= row) & (col < length), scores, -jnp.inf)
-            exps = jnp.exp(scores - jnp.max(scores, axis=1, keepdims=True))
-            probs = (exps / jnp.sum(exps, axis=1, keepdims=True)).astype(BF16)
-            o_ref[start:stop, cols] = jnp.dot(probs, values[:stop], preferred_element_type=F32).astype(BF16)
-
-
-def attention(lens, queries, kv, cos_tab, sin_tab, first_seq, n_seq, seq_len, head_dim):
+        turned.append(turn(q_ref[:, cols], cos_tab, sin_tab, even_lane).astype(BF16))
+    factor = head_dim ** -0.5 * 1.4426950408889634
+    for start in range(0, seq_len, step):
+        stop = start + step
+        queries = jnp.concatenate([head[start:stop] for head in turned], axis=0)
+        scores = lax.dot_general(queries, keys[:stop], (((1,), (1,)), ((), ())), preferred_element_type=F32)
+        row = lax.broadcasted_iota(jnp.int32, (step, stop), 0) + start
+        col = lax.broadcasted_iota(jnp.int32, (step, stop), 1)
+        hide = jnp.where((col <= row) & (col < length), 0.0, -jnp.inf)
+        scores = scores.reshape(group_size, step, stop) + hide[None]
+        exps = jnp.exp2((scores - jnp.max(scores, axis=2, keepdims=True)) * factor)
+        probs = (exps * (1.0 / jnp.sum(exps, axis=2, keepdims=True))).astype(BF16)
+        mixed = jnp.dot(probs.reshape(group_size * step, stop), values[:stop], preferred_element_type=F32).astype(BF16)
+        for head in range(group_size):
+            o_ref[start:stop, head * head_dim:(head + 1) * head_dim] = mixed[head * step:(head + 1) * step]
+
+
+def attention(lens, qkv, cos_tab, sin_tab, first_seq, n_seq, seq_len, head_dim, kv_local):
     rows = n_seq * seq_len
-    kv_local = kv.shape[1] // 2 // head_dim
-    group_size = queries.shape[1] // (kv_local * head_dim)
+    heads = qkv.shape[1] // head_dim - 2 * kv_local
+    group_size = heads // kv_local
     wide = group_size * head_dim
-    per_head = pl.BlockSpec((seq_len, head_dim), lambda b, g, lens: (b, g))
+    per_head = [pl.BlockSpec((seq_len, head_dim), functools.partial(lambda offset, b, g, lens: (b, offset + g), offset)) for offset in (heads, heads + kv_local, 0)]
     grouped = pl.BlockSpec((seq_len, wide), lambda b, g, lens: (b, g))
     table = pl.BlockSpec((seq_len, head_dim), lambda b, g, lens: (0, 0))
     return pl.pallas_call(
@@ -70,66 +76,124 @@
         grid_spec=pltpu.PrefetchScalarGridSpec(
             num_scalar_prefetch=1,
             grid=(n_seq, kv_local),
-            in_specs=[grouped, per_head, pl.BlockSpec((seq_len, head_dim), lambda b, g, lens: (b, kv_local + g)), table, table],
-            out_specs=[grouped, per_head, per_head],
+            in_specs=[grouped, per_head[0], per_head[1], table, table],
+            out_specs=[grouped, per_head[2], per_head[2]],
         ),
         out_shape=[
-            jax.ShapeDtypeStruct((rows, queries.shape[1]), BF16),
+            jax.ShapeDtypeStruct((rows, heads * head_dim), BF16),
             jax.ShapeDtypeStruct((rows, kv_local * head_dim), BF16),
             jax.ShapeDtypeStruct((rows, kv_local * head_dim), BF16),
         ],
-        cost_estimate=pl.CostEstimate(flops=16 * rows * queries.shape[1] * seq_len, bytes_accessed=rows * queries.shape[1] * 8, transcendentals=rows * seq_len * group_size * kv_local),
+        cost_estimate=pl.CostEstimate(flops=16 * rows * heads * head_dim * seq_len, bytes_accessed=rows * heads * head_dim * 8, transcendentals=rows * seq_len * heads),
         name="attention",
-    )(lens, queries, kv, kv, cos_tab, sin_tab)
-
-
-def rows_norm_kernel(x_ref, gain_ref, *rest):
-    out_ref = rest[-1]
-    x32 = x_ref[...].astype(F32)
-    inv_rms = lax.rsqrt(jnp.mean(x32 * x32, axis=-1, keepdims=True) + EPS)
-    out_ref[...] = (x32 * inv_rms * gain_ref[...]).astype(BF16)
-
-
-def rows_norm(x_rows, gain, first_row, rows, deps):
+    )(lens, qkv, qkv, qkv, cos_tab, sin_tab)
+
+
+NORM_ROWS = 128
+NORM_COLS = 512
+TILE = 256
+
+
+def inv_rms_of(parts):
+    total = 0.0
+    width = 0
+    for part in parts:
+        for start in range(0, part.shape[1], NORM_COLS // 2):
+            x32 = part[:, start:start + NORM_COLS // 2].astype(F32)
+            square = x32 * x32
+            for lane in range(0, square.shape[1], 128):
+                total = total + square[:, lane:lane + 128]
+        width += part.shape[1]
+    return lax.rsqrt(jnp.sum(total, axis=1, keepdims=True) / width + EPS)
+
+
+def norm_into(parts, gain_ref, normed_ref, row):
+    inv_rms = inv_rms_of(parts)
+    column = 0
+    for part in parts:
+        for start in range(0, part.shape[1], NORM_COLS // 2):
+            span = slice(column, column + NORM_COLS // 2)
+            normed_ref[pl.ds(row, part.shape[0]), span] = (part[:, start:start + NORM_COLS // 2].astype(F32) * inv_rms * gain_ref[:, span]).astype(BF16)
+            column += NORM_COLS // 2
+
+
+def qkv_kernel(steps, q_tiles, x_ref, gain_ref, wq_ref, wkv_ref, *rest):
+    out_ref, normed_ref = rest[-2:]
+    i = pl.program_id(0)
+
+    @pl.when(i < steps)
+    def _():
+        norm_into([x_ref], gain_ref, normed_ref, pl.multiple_of(i * NORM_ROWS, NORM_ROWS))
+
+    @pl.when((i >= steps) & (i < steps + q_tiles))
+    def _():
+        out_ref[...] = jnp.dot(normed_ref[...], wq_ref[...], preferred_element_type=F32)
+
+    @pl.when(i >= steps + q_tiles)
+    def _():
+        out_ref[...] = jnp.dot(normed_ref[...], wkv_ref[...], preferred_element_type=F32)
+
+
+def qkv_proj(x_rows, gain, w_query, w_kv, first_row, rows, deps):
     width = x_rows.shape[1]
-    block = 128
-    return pl.pallas_call(
-        rows_norm_kernel,
-        grid=(rows // block,),
-        in_specs=[pl.BlockSpec((block, width), lambda i: (first_row // block + i, 0)), pl.BlockSpec((1, width), lambda i: (0, 0))] + [ANY] * len(deps),
-        out_specs=pl.BlockSpec((block, width), lambda i: (i, 0)),
-        out_shape=jax.ShapeDtypeStruct((rows, width), BF16),
-        cost_estimate=pl.CostEstimate(flops=rows * width * 400, bytes_accessed=rows * width * 4, transcendentals=0),
-        name="rows_norm",
-    )(x_rows, gain, *deps)
-
-
-def hidden_norm_kernel(h_ref, gain_ref, *rest):
-    out_ref = rest[-1]
-    parts, _, cols = h_ref.shape
-    total = 0.0
-    for part in range(parts):
-        h32 = h_ref[part].astype(F32)
-        total = total + jnp.sum(h32 * h32, axis=-1, keepdims=True)
-    inv_rms = lax.rsqrt(total / (parts * cols) + EPS)
-    for part in range(parts):
-        span = slice(part * cols, (part + 1) * cols)
-        out_ref[:, span] = (h_ref[part].astype(F32) * inv_rms * gain_ref[:, span]).astype(BF16)
-
-
-def hidden_norm(hidden, gain, deps):
-    parts, rows, cols = hidden.shape
-    block = 128
-    width = parts * cols
-    return pl.pallas_call(
-        hidden_norm_kernel,
-        grid=(rows // block,),
-        in_specs=[pl.BlockSpec((parts, block, cols), lambda i: (0, i, 0)), pl.BlockSpec((1, width), lambda i: (0, 0))] + [ANY] * len(deps),
-        out_specs=pl.BlockSpec((block, width), lambda i: (i, 0)),
-        out_shape=jax.ShapeDtypeStruct((rows, width), BF16),
-        cost_estimate=pl.CostEstimate(flops=rows * width * 400, bytes_accessed=rows * width * 4, transcendentals=0),
-        name="hidden_norm",
-    )(hidden, gain, *deps)
+    steps = rows // NORM_ROWS
+    q_tiles = w_query.shape[1] // TILE
+    kv_tiles = w_kv.shape[1] // TILE
+    cols = w_query.shape[1] + w_kv.shape[1]
+    return pl.pallas_call(
+        functools.partial(qkv_kernel, steps, q_tiles),
+        grid=(steps + q_tiles + kv_tiles,),
+        in_specs=[
+            pl.BlockSpec((NORM_ROWS, width), lambda i: (first_row // NORM_ROWS + jnp.minimum(i, steps - 1), 0)),
+            pl.BlockSpec((1, width), lambda i: (0, 0)),
+            pl.BlockSpec((width, TILE), lambda i: (0, jnp.clip(i - steps, 0, q_tiles - 1))),
+            pl.BlockSpec((width, TILE), lambda i: (0, jnp.clip(i - steps - q_tiles, 0, kv_tiles - 1))),
+        ] + [ANY] * len(deps),
+        out_specs=pl.BlockSpec((rows, TILE), lambda i: (0, jnp.maximum(i - steps, 0))),
+        out_shape=jax.ShapeDtypeStruct((rows, cols), F32),
+        scratch_shapes=[pltpu.VMEM((rows, width), BF16)],
+        compiler_params=pltpu.CompilerParams(vmem_limit_bytes=50 * 2**20),
+        cost_estimate=pl.CostEstimate(flops=2 * rows * width * cols, bytes_accessed=width * cols * 2 + rows * width * 2 + rows * cols * 4, transcendentals=0),
+        name="qkv_proj",
+    )(x_rows, gain, w_query, w_kv, *deps)
+
+
+def gated_kernel(steps, h_ref, gain_ref, gate_ref, up_ref, *rest):
+    out_ref, normed_ref = rest[-2:]
+    i = pl.program_id(0)
+
+    @pl.when(i < steps)
+    def _():
+        norm_into([h_ref.at[part] for part in range(h_ref.shape[0])], gain_ref, normed_ref, pl.multiple_of(i * NORM_ROWS, NORM_ROWS))
+
+    @pl.when(i >= steps)
+    def _():
+        gate = jnp.dot(normed_ref[...], gate_ref[...], preferred_element_type=F32)
+        up = jnp.dot(normed_ref[...], up_ref[...], preferred_element_type=F32)
+        out_ref[...] = (jax.nn.silu(gate) * up).astype(BF16)
+
+
+def gated_proj(hidden, gain, w_gate, w_up, deps):
+    parts, rows, part_cols = hidden.shape
+    width, cols = w_gate.shape
+    steps = rows // NORM_ROWS
+    weight = pl.BlockSpec((width, TILE), lambda i: (0, jnp.maximum(i - steps, 0)))
+    return pl.pallas_call(
+        functools.partial(gated_kernel, steps),
+        grid=(steps + cols // TILE,),
+        in_specs=[
+            pl.BlockSpec((parts, NORM_ROWS, part_cols), lambda i: (0, jnp.minimum(i, steps - 1), 0)),
+            pl.BlockSpec((1, width), lambda i: (0, 0)),
+            weight,
+            weight,
+        ] + [ANY] * len(deps),
+        out_specs=pl.BlockSpec((rows, TILE), lambda i: (0, jnp.maximum(i - steps, 0))),
+        out_shape=jax.ShapeDtypeStruct((rows, cols), BF16),
+        scratch_shapes=[pltpu.VMEM((rows, width), BF16)],
+        compiler_params=pltpu.CompilerParams(vmem_limit_bytes=50 * 2**20),
+        cost_estimate=pl.CostEstimate(flops=4 * rows * width * cols, bytes_accessed=width * cols * 4 + rows * width * 2 + rows * cols * 2, transcendentals=rows * cols),
+        name="gated_proj",
+    )(hidden, gain, w_gate, w_up, *deps)
 
 
 def out_proj_kernel(n_far, place_ref, heads_ref, x_ref, own_ref, near_ref, *rest):
@@ -268,10 +332,8 @@
             rows = CHUNKS[c] * seq_len
             if c >= 3:
                 deps = deps + [mine[c - 3]]
-            normed = rows_norm(x_rows, gain, first[c] * seq_len, rows, deps)
-            queries = jnp.dot(normed, w_query, preferred_element_type=F32)
-            kv = jnp.dot(normed, w_kv, preferred_element_type=F32)
-            out, keys, values = attention(seq_lens, queries, kv, cos_tab, sin_tab, first[c], CHUNKS[c], seq_len, head_dim)
+            qkv = qkv_proj(x_rows, gain, w_query, w_kv, first[c] * seq_len, rows, deps)
+            out, keys, values = attention(seq_lens, qkv, cos_tab, sin_tab, first[c], CHUNKS[c], seq_len, head_dim, kv_local)
             deps = [out]
             heads.append(lax.all_gather(out, "tp", axis=0))
             new_keys.append(keys)
@@ -299,10 +361,7 @@
         deps = project(1, deps)
         for c in range(chunks):
             rows = CHUNKS[c] * seq_len
-            normed = hidden_norm(hidden[c], mlp_gain32, deps)
-            gate = lax.optimization_barrier(jnp.dot(normed, w_gate, preferred_element_type=F32))
-            up = jnp.dot(normed, w_up, preferred_element_type=F32)
-            gated = lax.optimization_barrier((jax.nn.silu(gate) * up).astype(BF16))
+            gated = gated_proj(hidden[c], mlp_gain32, w_gate, w_up, deps)
             part = jnp.dot(gated, w_down, preferred_element_type=F32).astype(BF16)
             received[c] = lax.all_to_all(part.reshape(tp_size, rows // tp_size, width), "tp", 0, 0, tiled=True)
             deps = [part]

time: 1830 us -> 1770 us (0.967)
  matrix products: 991 us -> 273 us
  Pallas kernels: 453 us -> 973 us
  waiting for transfers between devices: 158 us -> 280 us
    dot_general x20 -> x0, matrix products: 722 us -> none  [the longest x5 284 us: layer_shard(): up = jnp.dot(normed, w_up, preferred_element_type=F32)]
    pallas_call x10, Pallas kernels: 105 us -> 699 us  [the longest x5 532 us: gated_proj(): pl.pallas_call(functools.partial(gated_kernel, steps), grid=(steps + cols...]
    ppermute x2, waiting for transfers between devices: 52.5 us -> 131 us  [layer_shard(): mine.append(lax.ppermute(block, 'tp', swaps[hop]))]
    pallas_call x5, Pallas kernels: 138 us -> 64.9 us  [attention(): pl.pallas_call(functools.partial(attention_kernel, first_seq, group_size,...]
    all_to_all x4, waiting for transfers between devices: 94.3 us -> 119 us  [layer_shard(): lax.all_to_all(part.reshape(tp_size, rows // tp_size, width), 'tp', 0, 0,...]
    all_gather x5, waiting for transfers between devices: 4.95 us -> 23.6 us  [project(): hidden[c] = lax.all_gather(local, 'tp', axis=0)]
  transfers between devices with their start and end apart: 24 -> 24, of which waited for: 5 -> 7; matrix products, arithmetic and copies ran while one was open for 55% -> 17% of each run, Pallas kernels for 23% -> 53%
where the time goes in v2:
time: 1770 us; the launch traced here: 1760 us
  Pallas kernels  973 us (55%)
  waiting for transfers between devices  280 us (16%)
  matrix products  273 us (15%)
  blocking collectives  127 us (7%)
  local copies, waits for them, and re-layouts  56.1 us (3%)
  starting transfers between devices  32.4 us (2%)
    pallas_call x5, Pallas kernels, gated_proj(): pl.pallas_call(functools.partial(gated_kernel, steps), grid=(steps + cols...  532 us
    dot_general x5, matrix products, layer_shard(): part = jnp.dot(gated, w_down, preferred_element_type=F32).astype(BF16)  273 us
    pallas_call x5, Pallas kernels, qkv_proj(): pl.pallas_call(functools.partial(qkv_kernel, steps, q_tiles), grid=(steps...  167 us
    pallas_call x5, Pallas kernels, out_proj(): pl.pallas_call(functools.partial(out_proj_kernel, len(far)), grid_spec=pl...  134 us
    ppermute x2, waiting for transfers between devices, layer_shard(): mine.append(lax.ppermute(block, 'tp', swaps[hop]))  131 us
    all_to_all x1, blocking collectives, layer_shard(): lax.all_to_all(part.reshape(tp_size, rows // tp_size, width), 'tp', 0, 0,...  127 us
    all_to_all x4, waiting for transfers between devices, layer_shard(): lax.all_to_all(part.reshape(tp_size, rows // tp_size, width), 'tp', 0, 0,...  119 us
    pallas_call x5, Pallas kernels, attention(): pl.pallas_call(functools.partial(attention_kernel, first_seq, group_size,...  64.9 us
  transfers between devices with their start and end apart: 24, of which 7 were waited for; matrix products, arithmetic and copies ran while one was open for 17% of the time, Pallas kernels for 53%

profile of v2, /device:TPU:0, one launch (start us, length us, event | category | flops | bytes accessed | tf_op | source)
XLA Modules:
  0.0 1757.4 jit_solution(8517716759732015253)
XLA Ops:
  7.2 5.9 copy.59
  13.1 1.7 copy.58
  15.6 2.1 constant_dynamic-update-slice_fusion.1
  19.9 4.1 constant_dynamic-update-slice_fusion.wkv_ref
  24.0 23.7 %qkv_proj.5.q_ref.k_ref.v_ref = f32[384,2304]{1,0:T(8,128)S(1)} custom-call(bf16[3072,7168]{1,0:T(8,128)(2,1)} %bitcast.45, f32[1,7168]{1,0:T(1,128)S(1)} %bitcast.35, bf16[7168,1792]{1,0:T(8,128)(2,1)} %wq_ref.9, bf16[7168,512]{1,0:T(8,128)(2,1)} %constant_dynamic-update-slice_fusion.wkv_ref), custom_call_target="tpu_custom_call" | custom-call | flops 12683575296 | bytes 42074112 | tf_op jit(solution)/shard_map/qkv_proj/pallas_call | solution.py:143
  47.7 1.8 copy-done.5
  49.4 9.3 attention.5
  60.4 39.7 %qkv_proj.6.q_ref.k_ref.v_ref = f32[768,2304]{1,0:T(8,128)} custom-call(bf16[3072,7168]{1,0:T(8,128)(2,1)} %bitcast.46, f32[1,7168]{1,0:T(1,128)S(1)} %bitcast.36, bf16[7168,1792]{1,0:T(8,128)(2,1)} %wq_ref.9, bf16[7168,512]{1,0:T(8,128)(2,1)} %constant_dynamic-update-slice_fusion.wkv_ref, bf16[384,1792]{1,0:T(8,128)(2,1)S(1)} %copy-done.8), custom_call_target="tpu_custom_call" | custom-call | flops 25367150592 | bytes 51118080 | tf_op jit(solution)/shard_map/qkv_proj/pallas_call | solution.py:143
  100.1 15.4 attention.6
  115.6 6.0 fusion.1
  121.6 3.9 collective-permute-start
  125.5 7.2 constant_dynamic-slice_fusion
  132.9 39.6 %qkv_proj.7.q_ref.k_ref.v_ref = f32[768,2304]{1,0:T(8,128)} custom-call(bf16[3072,7168]{1,0:T(8,128)(2,1)} %bitcast.47, f32[1,7168]{1,0:T(1,128)S(1)} %bitcast.37, bf16[7168,1792]{1,0:T(8,128)(2,1)} %wq_ref.9, bf16[7168,512]{1,0:T(8,128)(2,1)} %constant_dynamic-update-slice_fusion.wkv_ref, bf16[768,1792]{1,0:T(8,128)(2,1)S(1)} %copy-done.6), custom_call_target="tpu_custom_call" | custom-call | flops 25367150592 | bytes 51118080 | tf_op jit(solution)/shard_map/qkv_proj/pallas_call | solution.py:143
  173.1 15.4 attention.7
  188.5 66.7 %collective-permute-done.rest_1_.rest_0_ = bf16[896,1792]{1,0:T(8,128)(2,1)} collective-permute-done((bf16[896,1792]{1,0:T(8,128)(2,1)}, bf16[896,1792]{1,0:T(8,128)(2,1)}, u32[]{:S(2)}, u32[]{:S(2)}) %collective-permute-start) | collective-permute-done | bytes 3211296 | tf_op jit(solution)/shard_map/ppermute | solution.py:317
  255.2 2.1 collective-permute-start.3
  257.3 64.5 %collective-permute-done.1.rest_1_.rest_2_ = bf16[896,1792]{1,0:T(8,128)(2,1)} collective-permute-done((bf16[896,1792]{1,0:T(8,128)(2,1)}, bf16[896,1792]{1,0:T(8,128)(2,1)}, u32[]{:S(2)}, u32[]{:S(2)}) %collective-permute-start.1) | collective-permute-done | bytes 3211296 | tf_op jit(solution)/shard_map/ppermute | solution.py:317
  323.4 1.8 copy-done.7
  325.2 39.1 %qkv_proj.8.q_ref.k_ref.v_ref = f32[768,2304]{1,0:T(8,128)} custom-call(bf16[3072,7168]{1,0:T(8,128)(2,1)} %bitcast.48, f32[1,7168]{1,0:T(1,128)S(1)} %bitcast.38, bf16[7168,1792]{1,0:T(8,128)(2,1)} %wq_ref.9, bf16[7168,512]{1,0:T(8,128)(2,1)} %constant_dynamic-update-slice_fusion.wkv_ref, bf16[768,1792]{1,0:T(8,128)(2,1)S(1)} %copy-done.7, ...), custom_call_target="tpu_custom_call" | custom-call | flops 25367150592 | bytes 51118080 | tf_op jit(solution)/shard_map/qkv_proj/pallas_call | solution.py:143
  364.3 15.5 attention.8
  379.8 1.8 copy-done
  381.6 24.8 %qkv_proj.9.q_ref.k_ref.v_ref = f32[384,2304]{1,0:T(8,128)} custom-call(bf16[3072,7168]{1,0:T(8,128)(2,1)} %bitcast.49, f32[1,7168]{1,0:T(1,128)S(1)} %bitcast.39, bf16[7168,1792]{1,0:T(8,128)(2,1)} %wq_ref.9, bf16[7168,512]{1,0:T(8,128)(2,1)} %constant_dynamic-update-slice_fusion.wkv_ref, bf16[768,1792]{1,0:T(8,128)(2,1)S(1)} %copy-done, ...), custom_call_target="tpu_custom_call" | custom-call | flops 12683575296 | bytes 42074112 | tf_op jit(solution)/shard_map/qkv_proj/pallas_call | solution.py:143
  406.4 9.3 attention.9
  415.8 19.2 %out_proj.5.rest_4_ = bf16[384,1792]{1,0:T(8,128)(2,1)} custom-call(s32[2]{0:T(128)} %pad_add_fusion.place_ref, bf16[4,384,1792]{2,1,0:T(8,128)(2,1)} %bitcast.75, bf16[3072,7168]{1,0:T(8,128)(2,1)} %bitcast.50, bf16[1792,7168]{1,0:T(8,128)(2,1)} %own_ref.9, bf16[1792,1792]{1,0:T(8,128)(2,1)} %collective-permute-done.2.near_ref, ...), custom_call_target="tpu_custom_call" | custom-call | flops 9865003008 | bytes 31195136 | tf_op jit(solution)/shard_map/out_proj/pallas_call | solution.py:221
  435.7 32.4 %out_proj.6.rest_0_ = bf16[768,1792]{1,0:T(8,128)(2,1)} custom-call(s32[2]{0:T(128)} %pad_add_fusion.place_ref, bf16[4,768,1792]{2,1,0:T(8,128)(2,1)} %bitcast.61, bf16[3072,7168]{1,0:T(8,128)(2,1)} %bitcast.51, bf16[1792,7168]{1,0:T(8,128)(2,1)} %own_ref.9, bf16[1792,1792]{1,0:T(8,128)(2,1)} %collective-permute-done.2.near_ref, ...), custom_call_target="tpu_custom_call" | custom-call | flops 19730006016 | bytes 36700160 | tf_op jit(solution)/shard_map/out_proj/pallas_call | solution.py:221
  468.8 6.0 all-gather.40.cloned.1.call-done
  474.8 72.3 %gated_proj.5 = bf16[384,5120]{1,0:T(8,128)(2,1)} custom-call(bf16[4,384,1792]{2,1,0:T(8,128)(2,1)} %bitcast.71, f32[1,7168]{1,0:T(1,128)S(1)} %bitcast.40, bf16[7168,5120]{1,0:T(8,128)(2,1)} %gate_ref.9, bf16[7168,5120]{1,0:T(8,128)(2,1)} %up_ref.9, bf16[768,1792]{1,0:T(8,128)(2,1)S(1)} %copy-done.3), custom_call_target="tpu_custom_call" | custom-call | flops 56371445760 | bytes 156237824 | tf_op jit(solution)/shard_map/gated_proj/pallas_call | solution.py:181
  547.1 39.4 %convolution_convert_fusion.4.rest_4_ = bf16[384,7168]{1,0:T(8,128)(2,1)} fusion(bf16[384,5120]{1,0:T(8,128)(2,1)} %gated_proj.5, bf16[5120,7168]{1,0:T(8,128)(2,1)} %param.21), kind=kOutput, calls=%fused_computation.4 | convolution fusion | flops 28188475392 | bytes 82837504 | tf_op jit(solution)/shard_map/dot_general | solution.py:365
  586.5 5.1 all-to-all-start
  591.7 30.7 %out_proj.7.rest_0_ = bf16[768,1792]{1,0:T(8,128)(2,1)} custom-call(s32[2]{0:T(128)} %pad_add_fusion.place_ref, bf16[4,768,1792]{2,1,0:T(8,128)(2,1)} %bitcast.63, bf16[3072,7168]{1,0:T(8,128)(2,1)} %bitcast.52, bf16[1792,7168]{1,0:T(8,128)(2,1)} %own_ref.9, bf16[1792,1792]{1,0:T(8,128)(2,1)} %collective-permute-done.2.near_ref, ...), custom_call_target="tpu_custom_call" | custom-call | flops 19730006016 | bytes 36700160 | tf_op jit(solution)/shard_map/out_proj/pallas_call | solution.py:221
  622.5 17.6 all-gather.44.cloned.1.call-done
  640.0 1.8 copy-done.2
  641.8 130.9 %gated_proj.6 = bf16[768,5120]{1,0:T(8,128)(2,1)} custom-call(bf16[4,768,1792]{2,1,0:T(8,128)(2,1)} %bitcast.68, f32[1,7168]{1,0:T(1,128)S(1)} %bitcast.41, bf16[7168,5120]{1,0:T(8,128)(2,1)} %gate_ref.9, bf16[7168,5120]{1,0:T(8,128)(2,1)} %up_ref.9, bf16[768,1792]{1,0:T(8,128)(2,1)S(1)} %copy-done.2), custom_call_target="tpu_custom_call" | custom-call | flops 112742891520 | bytes 165675008 | tf_op jit(solution)/shard_map/gated_proj/pallas_call | solution.py:181
  772.7 65.6 %convolution_convert_fusion.2.rest_0_ = bf16[768,7168]{1,0:T(8,128)(2,1)} fusion(bf16[768,5120]{1,0:T(8,128)(2,1)} %gated_proj.6, bf16[5120,7168]{1,0:T(8,128)(2,1)} %param.21), kind=kOutput, calls=%fused_computation.2 | convolution fusion | flops 56376950784 | bytes 92274688 | tf_op jit(solution)/shard_map/dot_general | solution.py:365
  838.3 4.9 sum_rows.5.rest_4_
  844.1 32.6 %out_proj.8.rest_0_ = bf16[768,1792]{1,0:T(8,128)(2,1)} custom-call(s32[2]{0:T(128)} %pad_add_fusion.place_ref, bf16[4,768,1792]{2,1,0:T(8,128)(2,1)} %bitcast.62, bf16[3072,7168]{1,0:T(8,128)(2,1)} %bitcast.53, bf16[1792,7168]{1,0:T(8,128)(2,1)} %own_ref.9, bf16[1792,1792]{1,0:T(8,128)(2,1)} %collective-permute-done.2.near_ref, ...), custom_call_target="tpu_custom_call" | custom-call | flops 19730006016 | bytes 36700160 | tf_op jit(solution)/shard_map/out_proj/pallas_call | solution.py:221
  876.7 1.8 copy-done.1
  878.5 129.3 %gated_proj.7 = bf16[768,5120]{1,0:T(8,128)(2,1)} custom-call(bf16[4,768,1792]{2,1,0:T(8,128)(2,1)} %bitcast.64, f32[1,7168]{1,0:T(1,128)S(1)} %bitcast.42, bf16[7168,5120]{1,0:T(8,128)(2,1)} %gate_ref.9, bf16[7168,5120]{1,0:T(8,128)(2,1)} %up_ref.9, bf16[768,1792]{1,0:T(8,128)(2,1)S(1)} %copy-done.1), custom_call_target="tpu_custom_call" | custom-call | flops 112742891520 | bytes 165675008 | tf_op jit(solution)/shard_map/gated_proj/pallas_call | solution.py:181
  1007.9 6.0 all-to-all-start.1
  1013.9 65.8 %convolution_convert_fusion.1.rest_0_ = bf16[768,7168]{1,0:T(8,128)(2,1)} fusion(bf16[768,5120]{1,0:T(8,128)(2,1)} %gated_proj.7, bf16[5120,7168]{1,0:T(8,128)(2,1)} %param.21), kind=kOutput, calls=%fused_computation.1 | convolution fusion | flops 56376950784 | bytes 92274688 | tf_op jit(solution)/shard_map/dot_general | solution.py:365
  1079.8 55.3 %all-to-all-done.1.received_ref = bf16[4,192,7168]{2,1,0:T(8,128)(2,1)} async-done(((bf16[4,192,7168]{2,1,0:T(8,128)(2,1)}), bf16[4,192,7168]{2,1,0:T(8,128)(2,1)}, u32[]{:S(2)}, u32[]{:S(2)}) %all-to-all-start.1) | async-done | bytes 11010080 | tf_op jit(solution)/shard_map/all_to_all | solution.py:366
  1135.1 7.8 sum_rows.6.refs_1_
  1143.0 6.4 all-to-all-start.2
  1149.5 6.3 store_rows.5.rest_4_.refs_1_
  1155.8 19.3 %out_proj.9.rest_0_ = bf16[384,1792]{1,0:T(8,128)(2,1)} custom-call(s32[2]{0:T(128)} %pad_add_fusion.place_ref, bf16[4,384,1792]{2,1,0:T(8,128)(2,1)} %bitcast.70, bf16[3072,7168]{1,0:T(8,128)(2,1)} %bitcast.54, bf16[1792,7168]{1,0:T(8,128)(2,1)} %own_ref.9, bf16[1792,1792]{1,0:T(8,128)(2,1)} %collective-permute-done.2.near_ref, ...), custom_call_target="tpu_custom_call" | custom-call | flops 9865003008 | bytes 31195136 | tf_op jit(solution)/shard_map/out_proj/pallas_call | solution.py:221
  1176.6 129.4 %gated_proj.8 = bf16[768,5120]{1,0:T(8,128)(2,1)} custom-call(bf16[4,768,1792]{2,1,0:T(8,128)(2,1)} %bitcast.66, f32[1,7168]{1,0:T(1,128)S(1)} %bitcast.43, bf16[7168,5120]{1,0:T(8,128)(2,1)} %gate_ref.9, bf16[7168,5120]{1,0:T(8,128)(2,1)} %up_ref.9, bf16[384,1792]{1,0:T(8,128)(2,1)S(1)} %copy-done.4), custom_call_target="tpu_custom_call" | custom-call | flops 112742891520 | bytes 165675008 | tf_op jit(solution)/shard_map/gated_proj/pallas_call | solution.py:181
  1306.0 65.6 %convolution_convert_fusion.rest_0_ = bf16[768,7168]{1,0:T(8,128)(2,1)} fusion(bf16[768,5120]{1,0:T(8,128)(2,1)} %gated_proj.8, bf16[5120,7168]{1,0:T(8,128)(2,1)} %param.21), kind=kOutput, calls=%fused_computation | convolution fusion | flops 56376950784 | bytes 92274688 | tf_op jit(solution)/shard_map/dot_general | solution.py:365
  1371.6 7.8 sum_rows.7.refs_2_
  1379.5 6.2 all-to-all-start.4
  1385.8 10.7 store_rows.6.rest_0_.refs_1_
  1396.4 69.7 %gated_proj.9 = bf16[384,5120]{1,0:T(8,128)(2,1)S(1)} custom-call(bf16[4,384,1792]{2,1,0:T(8,128)(2,1)} %bitcast.73, f32[1,7168]{1,0:T(1,128)S(1)} %bitcast.44, bf16[7168,5120]{1,0:T(8,128)(2,1)} %gate_ref.9, bf16[7168,5120]{1,0:T(8,128)(2,1)} %up_ref.9, bf16[3072,7168]{1,0:T(8,128)(2,1)} %store_rows.6.rest_0_.refs_1_), custom_call_target="tpu_custom_call" | custom-call | flops 56371445760 | bytes 156237824 | tf_op jit(solution)/shard_map/gated_proj/pallas_call | solution.py:181
  1466.2 36.6 %convolution_convert_fusion.3.rest_0_ = bf16[384,7168]{1,0:T(8,128)(2,1)} fusion(bf16[384,5120]{1,0:T(8,128)(2,1)S(1)} %gated_proj.9, bf16[5120,7168]{1,0:T(8,128)(2,1)} %param.21), kind=kOutput, calls=%fused_computation.3 | convolution fusion | flops 28188475392 | bytes 82837504 | tf_op jit(solution)/shard_map/dot_general | solution.py:365
  1502.7 63.2 %all-to-all-done.4.received_ref = bf16[4,192,7168]{2,1,0:T(8,128)(2,1)} async-done(((bf16[4,192,7168]{2,1,0:T(8,128)(2,1)}), bf16[4,192,7168]{2,1,0:T(8,128)(2,1)}, u32[]{:S(2)}, u32[]{:S(2)}) %all-to-all-start.4) | async-done | bytes 11010080 | tf_op jit(solution)/shard_map/all_to_all | solution.py:366
  1565.9 7.8 sum_rows.9.refs_2_
  1573.8 126.8 %all_to_all.25.received_ref = bf16[4,96,7168]{2,1,0:T(8,128)(2,1)} all-to-all(bf16[4,96,7168]{2,1,0:T(8,128)(2,1)} %bitcast.59), channel_id=1, replica_groups=mesh['dp'=2,'tp'=4] {'tp'}, dimensions={0} | all-to-all | bytes 11010048 | tf_op jit(solution)/shard_map/all_to_all | solution.py:366
  1700.6 5.0 sum_rows.8
  1705.7 1.8 constant_dynamic-update-slice_fusion.6
  1714.0 2.4 reshape.171
  1716.4 2.4 constant_dynamic-update-slice_fusion.12
  1718.8 2.4 constant_dynamic-update-slice_fusion.13
  1721.1 9.6 store_rows.7.refs_1_
  1730.7 9.6 store_rows.8.refs_1_
  1740.2 4.6 all-gather.30.cloned.1.call-done.refs_0_
  1744.8 5.9 store_rows.9
  (104 shorter events, 17.7 us)
Async XLA Ops:
  7.2 5.9 copy-start.10
  7.2 408.6 %all-gather.38.cloned.1.call-start = ((), (), s32[]{:S(2)}) async-start(), calls=%async_computation.11 | async-start | bytes 6881280 | tf_op jit(solution)/shard_map/all_gather | solution.py:338
  7.2 8.4 copy-start.9
  13.1 4.6 copy-start.16
  47.7 1.8 copy-start.5
  58.7 376.9 %all-gather.42.cloned.1.call-start = ((), (), s32[]{:S(2)}) async-start(), calls=%async_computation.13 | async-start | bytes 13762560 | tf_op jit(solution)/shard_map/all_gather | solution.py:338
  59.1 1.3 copy-start.8
  115.5 359.2 %all-gather.40.cloned.1.call-start = ((), (), s32[]{:S(2)}) async-start(), calls=%async_computation.12 | async-start | bytes 6881280 | tf_op jit(solution)/shard_map/all_gather | solution.py:349
  121.6 133.6 %collective-permute-start = (bf16[896,1792]{1,0:T(8,128)(2,1)}, bf16[896,1792]{1,0:T(8,128)(2,1)}, u32[]{:S(2)}, u32[]{:S(2)}) collective-permute-start(bf16[896,1792]{1,0:T(8,128)(2,1)} %get-tuple-element.34), channel_id=1, source_target_pairs={{0,2},{1,3},{2,0},{3,1},{4,6},{5,7},{6,4},{7,5}} | collective-permute-start | bytes 9633800 | tf_op jit(solution)/shard_map/ppermute | solution.py:317
  125.5 196.2 %collective-permute-start.1 = (bf16[896,1792]{1,0:T(8,128)(2,1)}, bf16[896,1792]{1,0:T(8,128)(2,1)}, u32[]{:S(2)}, u32[]{:S(2)}) collective-permute-start(bf16[896,1792]{1,0:T(8,128)(2,1)} %get-tuple-element.33), channel_id=1, source_target_pairs={{0,3},{1,2},{2,1},{3,0},{4,7},{5,6},{6,5},{7,4}} | collective-permute-start | bytes 9633800 | tf_op jit(solution)/shard_map/ppermute | solution.py:317
  125.5 7.3 copy-start.6
  132.7 283.0 %collective-permute-start.2 = (bf16[1792,1792]{1,0:T(8,128)(2,1)}, bf16[1792,1792]{1,0:T(8,128)(2,1)}, u32[]{:S(2)}, u32[]{:S(2)}) collective-permute-start(bf16[1792,1792]{1,0:T(8,128)(2,1)} %constant_dynamic-slice_fusion), channel_id=1, source_target_pairs={{0,1},{1,0},{2,3},{3,2},{4,5},{5,4},{6,7},{7,6}} | collective-permute-start | bytes 19267592 | tf_op jit(solution)/shard_map/ppermute | solution.py:320
  255.2 160.5 %collective-permute-start.3 = (bf16[896,1792]{1,0:T(8,128)(2,1)}, bf16[896,1792]{1,0:T(8,128)(2,1)}, u32[]{:S(2)}, u32[]{:S(2)}) collective-permute-start(bf16[896,1792]{1,0:T(8,128)(2,1)} %collective-permute-done.rest_1_.rest_0_), channel_id=1, source_target_pairs={{0,4},{4,0},{1,5},{5,1},{2,6},{6,2},{3,7},{7,3}} | collective-permute-start | bytes 9633800 | tf_op jit(solution)/shard_map/ppermute | solution.py:318
  321.8 94.0 %collective-permute-start.4 = (bf16[896,1792]{1,0:T(8,128)(2,1)}, bf16[896,1792]{1,0:T(8,128)(2,1)}, u32[]{:S(2)}, u32[]{:S(2)}) collective-permute-start(bf16[896,1792]{1,0:T(8,128)(2,1)} %collective-permute-done.1.rest_1_.rest_2_), channel_id=1, source_target_pairs={{0,4},{4,0},{1,5},{5,1},{2,6},{6,2},{3,7},{7,3}} | collective-permute-start | bytes 9633800 | tf_op jit(solution)/shard_map/ppermute | solution.py:318
  323.4 1.8 copy-start.7
  379.8 1.8 copy-start
  435.0 156.7 %all-gather.46.cloned.1.call-start = ((), (), s32[]{:S(2)}) async-start(), calls=%async_computation.15 | async-start | bytes 13762560 | tf_op jit(solution)/shard_map/all_gather | solution.py:338
  435.6 204.4 %all-gather.44.cloned.1.call-start = ((), (), s32[]{:S(2)}) async-start(), calls=%async_computation.14 | async-start | bytes 13762560 | tf_op jit(solution)/shard_map/all_gather | solution.py:349
  468.0 0.7 copy-start.17
  468.0 6.7 copy-start.3
  468.1 376.0 %all-gather.50.cloned.1.call-start = ((), (), s32[]{:S(2)}) async-start(), calls=%async_computation.17 | async-start | bytes 13762560 | tf_op jit(solution)/shard_map/all_gather | solution.py:338
  586.5 251.8 %all-to-all-start = ((bf16[4,96,7168]{2,1,0:T(8,128)(2,1)}), bf16[4,96,7168]{2,1,0:T(8,128)(2,1)}, u32[]{:S(2)}, u32[]{:S(2)}) async-start(bf16[4,96,7168]{2,1,0:T(8,128)(2,1)} %bitcast.60), calls=%async_computation | async-start | bytes 11010048 | tf_op jit(solution)/shard_map/all_to_all | solution.py:366
  591.6 285.1 %all-gather.48.cloned.1.call-start = ((), (), s32[]{:S(2)}) async-start(), calls=%async_computation.16 | async-start | bytes 13762560 | tf_op jit(solution)/shard_map/all_gather | solution.py:349
  622.4 527.1 %all-gather.26.cloned.1.call-start = ((), (), s32[]{:S(2)}) async-start(), calls=%async_computation.5 | async-start | bytes 6881280 | tf_op jit(solution)/shard_map/all_gather | solution.py:354
  640.0 1.8 copy-start.2
  843.3 312.6 %all-gather.36.cloned.1.call-start = ((), (), s32[]{:S(2)}) async-start(), calls=%async_computation.10 | async-start | bytes 6881280 | tf_op jit(solution)/shard_map/all_gather | solution.py:338
  844.0 331.3 %all-gather.54.cloned.1.call-start = ((), (), s32[]{:S(2)}) async-start(), calls=%async_computation.19 | async-start | bytes 13762560 | tf_op jit(solution)/shard_map/all_gather | solution.py:349
  876.7 1.8 copy-start.1
  1007.9 127.3 %all-to-all-start.1 = ((bf16[4,192,7168]{2,1,0:T(8,128)(2,1)}), bf16[4,192,7168]{2,1,0:T(8,128)(2,1)}, u32[]{:S(2)}, u32[]{:S(2)}) async-start(bf16[4,192,7168]{2,1,0:T(8,128)(2,1)} %bitcast.57), calls=%async_computation.1 | async-start | bytes 22020096 | tf_op jit(solution)/shard_map/all_to_all | solution.py:366
  1013.9 371.9 %all-gather.28.cloned.1.call-start = ((), (), s32[]{:S(2)}) async-start(), calls=%async_computation.6 | async-start | bytes 13762560 | tf_op jit(solution)/shard_map/all_gather | solution.py:354
  1143.0 228.7 %all-to-all-start.2 = ((bf16[4,192,7168]{2,1,0:T(8,128)(2,1)}), bf16[4,192,7168]{2,1,0:T(8,128)(2,1)}, u32[]{:S(2)}, u32[]{:S(2)}) async-start(bf16[4,192,7168]{2,1,0:T(8,128)(2,1)} %bitcast.56), calls=%async_computation.2 | async-start | bytes 22020096 | tf_op jit(solution)/shard_map/all_to_all | solution.py:366
  1149.4 247.0 %all-gather.52.cloned.1.call-start = ((), (), s32[]{:S(2)}) async-start(), calls=%async_computation.18 | async-start | bytes 6881280 | tf_op jit(solution)/shard_map/all_gather | solution.py:349
  1175.2 545.9 %all-gather.34.cloned.1.call-start = ((), (), s32[]{:S(2)}) async-start(), calls=%async_computation.9 | async-start | bytes 13762560 | tf_op jit(solution)/shard_map/all_gather | solution.py:354
  1175.3 1.3 copy-start.4
  1379.5 186.4 %all-to-all-start.4 = ((bf16[4,192,7168]{2,1,0:T(8,128)(2,1)}), bf16[4,192,7168]{2,1,0:T(8,128)(2,1)}, u32[]{:S(2)}, u32[]{:S(2)}) async-start(bf16[4,192,7168]{2,1,0:T(8,128)(2,1)} %bitcast.58), calls=%async_computation.4 | async-start | bytes 22020096 | tf_op jit(solution)/shard_map/all_to_all | solution.py:366
  1385.7 345.0 %all-gather.32.cloned.1.call-start = ((), (), s32[]{:S(2)}) async-start(), calls=%async_computation.8 | async-start | bytes 13762560 | tf_op jit(solution)/shard_map/all_gather | solution.py:354
  1573.7 171.1 %all-gather.30.cloned.1.call-start = ((), (), s32[]{:S(2)}) async-start(), calls=%async_computation.7 | async-start | bytes 6881280 | tf_op jit(solution)/shard_map/all_gather | solution.py:354
  1700.6 6.8 copy-start.12
  1700.6 6.9 copy-start.14
  1700.6 6.9 copy-start.11
  1700.6 7.7 copy-start.13
  1705.7 5.9 copy-start.15
Sparse Core Ops, SparseCore 0:
  58.9 41.9 all-gather.37
  115.6 132.4 all-gather.41
  435.1 39.5 all-gather.39
  476.1 70.3 all-gather.45
  547.9 92.0 all-gather.43
  641.4 94.8 all-gather.49
  737.8 70.3 all-gather.47
  843.4 38.7 all-gather.25
  883.7 39.1 all-gather.35
  924.3 70.3 all-gather.53
  1143.1 128.7 all-gather.27
  1273.3 68.9 all-gather.51
  1379.6 130.0 all-gather.33
  1573.9 128.0 all-gather.31
  1705.8 38.9 all-gather.29

commit v3 on v2

--- a/solution.py
+++ b/solution.py
@@ -13,7 +13,7 @@
 CHUNKS = (1, 2, 2, 2, 1)
 F32 = jnp.float32
 BF16 = jnp.bfloat16
-ANY = pl.BlockSpec(memory_space=pl.ANY)
+ANY = pl.BlockSpec(memory_space=pltpu.MemorySpace.HBM)
 
 
 def rope_tables(seq_len, head_dim):
@@ -31,7 +31,8 @@
     return vecs * cos_tab + swapped * sin_tab
 
 
-def attention_kernel(first_seq, group_size, head_dim, lens_ref, q_ref, k_ref, v_ref, cos_ref, sin_ref, o_ref, k_out_ref, v_out_ref):
+def attention_kernel(first_seq, group_size, head_dim, lens_ref, q_ref, k_ref, v_ref, cos_ref, sin_ref, *rest):
+    o_ref, k_out_ref, v_out_ref = rest[-3:]
     seq_len = q_ref.shape[0]
     length = lens_ref[first_seq + pl.program_id(0)]
     cos_tab = cos_ref[...]
@@ -63,7 +64,7 @@
             o_ref[start:stop, head * head_dim:(head + 1) * head_dim] = mixed[head * step:(head + 1) * step]
 
 
-def attention(lens, qkv, cos_tab, sin_tab, first_seq, n_seq, seq_len, head_dim, kv_local):
+def attention(lens, qkv, cos_tab, sin_tab, first_seq, n_seq, seq_len, head_dim, kv_local, deps):
     rows = n_seq * seq_len
     heads = qkv.shape[1] // head_dim - 2 * kv_local
     group_size = heads // kv_local
@@ -76,7 +77,7 @@
         grid_spec=pltpu.PrefetchScalarGridSpec(
             num_scalar_prefetch=1,
             grid=(n_seq, kv_local),
-            in_specs=[grouped, per_head[0], per_head[1], table, table],
+            in_specs=[grouped, per_head[0], per_head[1], table, table] + [ANY] * len(deps),
             out_specs=[grouped, per_head[2], per_head[2]],
         ),
         out_shape=[
@@ -86,7 +87,7 @@
         ],
         cost_estimate=pl.CostEstimate(flops=16 * rows * heads * head_dim * seq_len, bytes_accessed=rows * heads * head_dim * 8, transcendentals=rows * seq_len * heads),
         name="attention",
-    )(lens, qkv, qkv, qkv, cos_tab, sin_tab)
+    )(lens, qkv, qkv, qkv, cos_tab, sin_tab, *deps)
 
 
 NORM_ROWS = 128
@@ -197,7 +198,9 @@
 
 
 def out_proj_kernel(n_far, place_ref, heads_ref, x_ref, own_ref, near_ref, *rest):
-    far_refs, h_ref = rest[:n_far], rest[-1]
+    far_refs = rest[:n_far]
+    h_ref, token_ref = rest[-2:]
+    token_ref[...] = jnp.zeros_like(token_ref)
     tp_index, dp_index = place_ref[0], place_ref[1]
     total = x_ref[...].astype(F32)
     half = far_refs[0].shape[0]
@@ -229,9 +232,9 @@
                 pl.BlockSpec((width, block), lambda n, place: (0, place[0] * steps + n)),
                 pl.BlockSpec((width, block), lambda n, place: (0, n)),
             ] + [pl.BlockSpec((half, block), lambda n, place: (0, n))] * len(far) + [ANY] * len(deps),
-            out_specs=pl.BlockSpec((rows, block), lambda n, place: (0, n)),
+            out_specs=[pl.BlockSpec((rows, block), lambda n, place: (0, n)), pl.BlockSpec((8, 128), lambda n, place: (0, 0))],
         ),
-        out_shape=jax.ShapeDtypeStruct((rows, cols), BF16),
+        out_shape=[jax.ShapeDtypeStruct((rows, cols), BF16), jax.ShapeDtypeStruct((8, 128), F32)],
         compiler_params=pltpu.CompilerParams(vmem_limit_bytes=56 * 2**20),
         cost_estimate=pl.CostEstimate(flops=2 * parts * rows * width * cols, bytes_accessed=parts * (rows + cols) * width * 2, transcendentals=0),
         name="out_proj",
@@ -330,11 +333,11 @@
         deps = []
         for c in range(chunks):
             rows = CHUNKS[c] * seq_len
-            if c >= 3:
-                deps = deps + [mine[c - 3]]
+            if c == 2:
+                deps = deps + [mine[0]]
             qkv = qkv_proj(x_rows, gain, w_query, w_kv, first[c] * seq_len, rows, deps)
-            out, keys, values = attention(seq_lens, qkv, cos_tab, sin_tab, first[c], CHUNKS[c], seq_len, head_dim, kv_local)
-            deps = [out]
+            out, keys, values = attention(seq_lens, qkv, cos_tab, sin_tab, first[c], CHUNKS[c], seq_len, head_dim, kv_local, mine[1:] if c == 2 else [])
+            deps = [keys]
             heads.append(lax.all_gather(out, "tp", axis=0))
             new_keys.append(keys)
             new_values.append(values)
@@ -345,9 +348,9 @@
         y = None
 
         def project(c, deps):
-            local = out_proj(place, heads[c], x_rows, w_out, near, [mine[0], other[0], mine[1], other[1]], first[c] * seq_len, deps)
+            local, token = out_proj(place, heads[c], x_rows, w_out, near, [mine[0], other[0], mine[1], other[1]], first[c] * seq_len, deps)
             hidden[c] = lax.all_gather(local, "tp", axis=0)
-            return [local]
+            return [token]
 
         def finish(c, deps):
             y_rows = sum_rows(place, received[c], hidden[c], deps)
@@ -367,18 +370,19 @@
             deps = [part]
             if c >= 1:
                 deps = finish(c - 1, deps)
-            if c >= 2:
-                y = store(c - 2, y, deps)
+            if c >= 3:
+                y = store(c - 3, y, deps)
                 deps = [y]
             if c + 2 < chunks:
                 deps = project(c + 2, deps)
+        y = store(chunks - 3, y, [])
         y = store(chunks - 2, y, [])
         finish(chunks - 1, [])
         y = store(chunks - 1, y, [])
 
         def cache(old, new):
             new = jnp.concatenate(new, axis=0).reshape(batch_size, seq_len, kv_local, head_dim)
-            return lax.dynamic_update_slice(old, new, (0, 0, 0, 0))
+            return jnp.concatenate([new, old[:, seq_len:]], axis=1)
 
         return y.reshape(x.shape), cache(k_cache, new_keys), cache(v_cache, new_values)
 

time: 1770 us -> 1740 us (0.983)
  waiting for transfers between devices: 280 us -> 247 us
    all_to_all x4, waiting for transfers between devices: 119 us -> 91.1 us  [layer_shard(): lax.all_to_all(part.reshape(tp_size, rows // tp_size, width), 'tp', 0, 0,...]
  transfers between devices with their start and end apart: 24 -> 24, of which waited for: 7 -> 6; matrix products, arithmetic and copies ran while one was open for 17% -> 18% of each run, Pallas kernels for 53% -> 54%
where the time goes in v3:
time: 1740 us; the launch traced here: 1730 us
  Pallas kernels  971 us (56%)
  matrix products  276 us (16%)
  waiting for transfers between devices  247 us (14%)
  blocking collectives  127 us (7%)
  local copies, waits for them, and re-layouts  49.6 us (3%)
  starting transfers between devices  32.4 us (2%)
    pallas_call x5, Pallas kernels, gated_proj(): pl.pallas_call(functools.partial(gated_kernel, steps), grid=(steps + cols...  533 us
    dot_general x5, matrix products, layer_shard(): part = jnp.dot(gated, w_down, preferred_element_type=F32).astype(BF16)  276 us
    pallas_call x5, Pallas kernels, qkv_proj(): pl.pallas_call(functools.partial(qkv_kernel, steps, q_tiles), grid=(steps...  165 us
    ppermute x2, waiting for transfers between devices, layer_shard(): mine.append(lax.ppermute(block, 'tp', swaps[hop]))  147 us
    pallas_call x5, Pallas kernels, out_proj(): pl.pallas_call(functools.partial(out_proj_kernel, len(far)), grid_spec=pl...  132 us
    all_to_all x1, blocking collectives, layer_shard(): lax.all_to_all(part.reshape(tp_size, rows // tp_size, width), 'tp', 0, 0,...  127 us
    all_to_all x4, waiting for transfers between devices, layer_shard(): lax.all_to_all(part.reshape(tp_size, rows // tp_size, width), 'tp', 0, 0,...  91.1 us
    pallas_call x5, Pallas kernels, attention(): pl.pallas_call(functools.partial(attention_kernel, first_seq, group_size,...  64.7 us
  transfers between devices with their start and end apart: 24, of which 6 were waited for; matrix products, arithmetic and copies ran while one was open for 18% of the time, Pallas kernels for 54%

profile of v3, /device:TPU:0, one launch (start us, length us, event | category | flops | bytes accessed | tf_op | source)
XLA Modules:
  0.0 1732.9 jit_solution(6351328723262699760)
XLA Ops:
  8.1 4.1 constant_dynamic-update-slice_fusion.1
  14.3 4.1 constant_dynamic-update-slice_fusion.wkv_ref
  18.4 23.7 %qkv_proj.5.q_ref.k_ref.v_ref = f32[384,2304]{1,0:T(8,128)S(1)} custom-call(bf16[3072,7168]{1,0:T(8,128)(2,1)} %bitcast.45, f32[1,7168]{1,0:T(1,128)S(1)} %bitcast.35, bf16[7168,1792]{1,0:T(8,128)(2,1)} %wq_ref.9, bf16[7168,512]{1,0:T(8,128)(2,1)} %constant_dynamic-update-slice_fusion.wkv_ref), custom_call_target="tpu_custom_call" | custom-call | flops 12683575296 | bytes 42074112 | tf_op jit(solution)/shard_map/qkv_proj/pallas_call | solution.py:144
  42.1 1.8 copy-done.2
  43.9 9.2 attention.5
  54.6 39.6 %qkv_proj.6.q_ref.k_ref.v_ref = f32[768,2304]{1,0:T(8,128)} custom-call(bf16[3072,7168]{1,0:T(8,128)(2,1)} %bitcast.46, f32[1,7168]{1,0:T(1,128)S(1)} %bitcast.36, bf16[7168,1792]{1,0:T(8,128)(2,1)} %wq_ref.9, bf16[7168,512]{1,0:T(8,128)(2,1)} %constant_dynamic-update-slice_fusion.wkv_ref, bf16[384,256]{1,0:T(8,128)(2,1)S(1)} %copy-done.9), custom_call_target="tpu_custom_call" | custom-call | flops 25367150592 | bytes 51118080 | tf_op jit(solution)/shard_map/qkv_proj/pallas_call | solution.py:144
  94.2 15.4 attention.6
  109.6 6.1 fusion.1
  115.7 3.6 collective-permute-start
  119.3 7.2 constant_dynamic-slice_fusion
  127.2 121.7 %collective-permute-done.rest_1_.rest_0_ = bf16[896,1792]{1,0:T(8,128)(2,1)S(1)} collective-permute-done((bf16[896,1792]{1,0:T(8,128)(2,1)}, bf16[896,1792]{1,0:T(8,128)(2,1)S(1)}, u32[]{:S(2)}, u32[]{:S(2)}) %collective-permute-start) | collective-permute-done | bytes 3211296 | tf_op jit(solution)/shard_map/ppermute | solution.py:320
  248.9 2.1 collective-permute-start.3
  251.0 39.3 %qkv_proj.7.q_ref.k_ref.v_ref = f32[768,2304]{1,0:T(8,128)} custom-call(bf16[3072,7168]{1,0:T(8,128)(2,1)} %bitcast.47, f32[1,7168]{1,0:T(1,128)S(1)} %bitcast.37, bf16[7168,1792]{1,0:T(8,128)(2,1)} %wq_ref.9, bf16[7168,512]{1,0:T(8,128)(2,1)} %constant_dynamic-update-slice_fusion.wkv_ref, bf16[768,256]{1,0:T(8,128)(2,1)S(1)} %copy-done.5, ...), custom_call_target="tpu_custom_call" | custom-call | flops 25367150592 | bytes 51118080 | tf_op jit(solution)/shard_map/qkv_proj/pallas_call | solution.py:144
  290.3 25.3 %collective-permute-done.1.rest_0_.rest_2_ = bf16[896,1792]{1,0:T(8,128)(2,1)} collective-permute-done((bf16[896,1792]{1,0:T(8,128)(2,1)}, bf16[896,1792]{1,0:T(8,128)(2,1)}, u32[]{:S(2)}, u32[]{:S(2)}) %collective-permute-start.1) | collective-permute-done | bytes 3211296 | tf_op jit(solution)/shard_map/ppermute | solution.py:320
  315.6 1.5 collective-permute-start.4
  317.2 15.4 attention.7
  333.5 39.1 %qkv_proj.8.q_ref.k_ref.v_ref = f32[768,2304]{1,0:T(8,128)} custom-call(bf16[3072,7168]{1,0:T(8,128)(2,1)} %bitcast.48, f32[1,7168]{1,0:T(1,128)S(1)} %bitcast.38, bf16[7168,1792]{1,0:T(8,128)(2,1)} %wq_ref.9, bf16[7168,512]{1,0:T(8,128)(2,1)} %constant_dynamic-update-slice_fusion.wkv_ref, bf16[768,256]{1,0:T(8,128)(2,1)S(1)} %copy-done.7), custom_call_target="tpu_custom_call" | custom-call | flops 25367150592 | bytes 51118080 | tf_op jit(solution)/shard_map/qkv_proj/pallas_call | solution.py:144
  372.6 15.6 attention.8
  388.2 1.0 copy-done.3
  389.2 23.7 %qkv_proj.9.q_ref.k_ref.v_ref = f32[384,2304]{1,0:T(8,128)S(1)} custom-call(bf16[3072,7168]{1,0:T(8,128)(2,1)} %bitcast.49, f32[1,7168]{1,0:T(1,128)S(1)} %bitcast.39, bf16[7168,1792]{1,0:T(8,128)(2,1)} %wq_ref.9, bf16[7168,512]{1,0:T(8,128)(2,1)} %constant_dynamic-update-slice_fusion.wkv_ref, bf16[768,256]{1,0:T(8,128)(2,1)S(1)} %copy-done.3), custom_call_target="tpu_custom_call" | custom-call | flops 12683575296 | bytes 42074112 | tf_op jit(solution)/shard_map/qkv_proj/pallas_call | solution.py:144
  412.9 1.8 copy-done.1
  414.7 9.2 attention.9
  424.0 19.2 %out_proj.5 = (bf16[384,1792]{1,0:T(8,128)(2,1)}, f32[8,128]{1,0:T(8,128)}) custom-call(s32[2]{0:T(128)} %pad_add_fusion.place_ref, bf16[4,384,1792]{2,1,0:T(8,128)(2,1)} %bitcast.74, bf16[3072,7168]{1,0:T(8,128)(2,1)} %bitcast.50, bf16[1792,7168]{1,0:T(8,128)(2,1)} %own_ref.9, bf16[1792,1792]{1,0:T(8,128)(2,1)} %collective-permute-done.2.near_ref, ...), custom_call_target="tpu_custom_call" | custom-call | flops 9865003008 | bytes 31195136 | tf_op jit(solution)/shard_map/out_proj/pallas_call | solution.py:224
  443.9 32.4 %out_proj.6 = (bf16[768,1792]{1,0:T(8,128)(2,1)}, f32[8,128]{1,0:T(8,128)}) custom-call(s32[2]{0:T(128)} %pad_add_fusion.place_ref, bf16[4,768,1792]{2,1,0:T(8,128)(2,1)} %bitcast.69, bf16[3072,7168]{1,0:T(8,128)(2,1)} %bitcast.51, bf16[1792,7168]{1,0:T(8,128)(2,1)} %own_ref.9, bf16[1792,1792]{1,0:T(8,128)(2,1)} %collective-permute-done.2.near_ref, ...), custom_call_target="tpu_custom_call" | custom-call | flops 19730006016 | bytes 36700160 | tf_op jit(solution)/shard_map/out_proj/pallas_call | solution.py:224
  477.0 6.0 all-gather.46.cloned.1.call-done
  483.0 72.0 %gated_proj.5 = bf16[384,5120]{1,0:T(8,128)(2,1)S(1)} custom-call(bf16[4,384,1792]{2,1,0:T(8,128)(2,1)} %bitcast.70, f32[1,7168]{1,0:T(1,128)S(1)} %bitcast.40, bf16[7168,5120]{1,0:T(8,128)(2,1)} %gate_ref.9, bf16[7168,5120]{1,0:T(8,128)(2,1)} %up_ref.9, f32[8,128]{1,0:T(8,128)S(1)} %copy-done.14), custom_call_target="tpu_custom_call" | custom-call | flops 56371445760 | bytes 156237824 | tf_op jit(solution)/shard_map/gated_proj/pallas_call | solution.py:182
  555.0 1.9 copy-done.15
  556.9 39.6 %convolution_convert_fusion.4.rest_4_ = bf16[384,7168]{1,0:T(8,128)(2,1)} fusion(bf16[384,5120]{1,0:T(8,128)(2,1)} %copy-done.15, bf16[5120,7168]{1,0:T(8,128)(2,1)} %param.21), kind=kOutput, calls=%fused_computation.4 | convolution fusion | flops 28188475392 | bytes 82837504 | tf_op jit(solution)/shard_map/dot_general | solution.py:368
  596.5 30.7 %out_proj.7 = (bf16[768,1792]{1,0:T(8,128)(2,1)}, f32[8,128]{1,0:T(8,128)}) custom-call(s32[2]{0:T(128)} %pad_add_fusion.place_ref, bf16[4,768,1792]{2,1,0:T(8,128)(2,1)} %bitcast.62, bf16[3072,7168]{1,0:T(8,128)(2,1)} %bitcast.52, bf16[1792,7168]{1,0:T(8,128)(2,1)} %own_ref.9, bf16[1792,1792]{1,0:T(8,128)(2,1)} %collective-permute-done.2.near_ref, ...), custom_call_target="tpu_custom_call" | custom-call | flops 19730006016 | bytes 36700160 | tf_op jit(solution)/shard_map/out_proj/pallas_call | solution.py:224
  628.0 5.1 all-to-all-start.1
  633.2 130.9 %gated_proj.6 = bf16[768,5120]{1,0:T(8,128)(2,1)} custom-call(bf16[4,768,1792]{2,1,0:T(8,128)(2,1)} %bitcast.67, f32[1,7168]{1,0:T(1,128)S(1)} %bitcast.41, bf16[7168,5120]{1,0:T(8,128)(2,1)} %gate_ref.9, bf16[7168,5120]{1,0:T(8,128)(2,1)} %up_ref.9, f32[8,128]{1,0:T(8,128)S(1)} %copy-done.12), custom_call_target="tpu_custom_call" | custom-call | flops 112742891520 | bytes 165675008 | tf_op jit(solution)/shard_map/gated_proj/pallas_call | solution.py:182
  764.2 67.7 %convolution_convert_fusion.2.rest_0_ = bf16[768,7168]{1,0:T(8,128)(2,1)} fusion(bf16[768,5120]{1,0:T(8,128)(2,1)} %gated_proj.6, bf16[5120,7168]{1,0:T(8,128)(2,1)} %param.21), kind=kOutput, calls=%fused_computation.2 | convolution fusion | flops 56376950784 | bytes 92274688 | tf_op jit(solution)/shard_map/dot_general | solution.py:368
  831.9 5.8 sum_rows.5.rest_4_
  837.7 30.7 %out_proj.8 = (bf16[768,1792]{1,0:T(8,128)(2,1)}, f32[8,128]{1,0:T(8,128)}) custom-call(s32[2]{0:T(128)} %pad_add_fusion.place_ref, bf16[4,768,1792]{2,1,0:T(8,128)(2,1)} %bitcast.61, bf16[3072,7168]{1,0:T(8,128)(2,1)} %bitcast.53, bf16[1792,7168]{1,0:T(8,128)(2,1)} %own_ref.9, bf16[1792,1792]{1,0:T(8,128)(2,1)} %collective-permute-done.2.near_ref, ...), custom_call_target="tpu_custom_call" | custom-call | flops 19730006016 | bytes 36700160 | tf_op jit(solution)/shard_map/out_proj/pallas_call | solution.py:224
  868.4 6.1 all-to-all-start
  875.2 130.9 %gated_proj.7 = bf16[768,5120]{1,0:T(8,128)(2,1)} custom-call(bf16[4,768,1792]{2,1,0:T(8,128)(2,1)} %bitcast.63, f32[1,7168]{1,0:T(1,128)S(1)} %bitcast.42, bf16[7168,5120]{1,0:T(8,128)(2,1)} %gate_ref.9, bf16[7168,5120]{1,0:T(8,128)(2,1)} %up_ref.9, f32[8,128]{1,0:T(8,128)S(1)} %copy-done.13), custom_call_target="tpu_custom_call" | custom-call | flops 112742891520 | bytes 165675008 | tf_op jit(solution)/shard_map/gated_proj/pallas_call | solution.py:182
  1006.1 66.8 %convolution_convert_fusion.1.rest_0_ = bf16[768,7168]{1,0:T(8,128)(2,1)} fusion(bf16[768,5120]{1,0:T(8,128)(2,1)} %gated_proj.7, bf16[5120,7168]{1,0:T(8,128)(2,1)} %param.21), kind=kOutput, calls=%fused_computation.1 | convolution fusion | flops 56376950784 | bytes 92274688 | tf_op jit(solution)/shard_map/dot_general | solution.py:368
  1072.9 11.3 all-to-all-done.received_ref
  1084.2 7.9 sum_rows.6.rest_4_
  1092.1 19.2 %out_proj.9 = (bf16[384,1792]{1,0:T(8,128)(2,1)}, f32[8,128]{1,0:T(8,128)}) custom-call(s32[2]{0:T(128)} %pad_add_fusion.place_ref, bf16[4,384,1792]{2,1,0:T(8,128)(2,1)} %bitcast.75, bf16[3072,7168]{1,0:T(8,128)(2,1)} %bitcast.54, bf16[1792,7168]{1,0:T(8,128)(2,1)} %own_ref.9, bf16[1792,1792]{1,0:T(8,128)(2,1)} %collective-permute-done.2.near_ref, ...), custom_call_target="tpu_custom_call" | custom-call | flops 9865003008 | bytes 31195136 | tf_op jit(solution)/shard_map/out_proj/pallas_call | solution.py:224
  1111.4 6.3 all-to-all-start.2
  1118.4 129.6 %gated_proj.8 = bf16[768,5120]{1,0:T(8,128)(2,1)} custom-call(bf16[4,768,1792]{2,1,0:T(8,128)(2,1)} %bitcast.65, f32[1,7168]{1,0:T(1,128)S(1)} %bitcast.43, bf16[7168,5120]{1,0:T(8,128)(2,1)} %gate_ref.9, bf16[7168,5120]{1,0:T(8,128)(2,1)} %up_ref.9, f32[8,128]{1,0:T(8,128)S(1)} %copy-done.11), custom_call_target="tpu_custom_call" | custom-call | flops 112742891520 | bytes 165675008 | tf_op jit(solution)/shard_map/gated_proj/pallas_call | solution.py:182
  1248.0 65.7 %convolution_convert_fusion.rest_0_ = bf16[768,7168]{1,0:T(8,128)(2,1)} fusion(bf16[768,5120]{1,0:T(8,128)(2,1)} %gated_proj.8, bf16[5120,7168]{1,0:T(8,128)(2,1)} %param.21), kind=kOutput, calls=%fused_computation | convolution fusion | flops 56376950784 | bytes 92274688 | tf_op jit(solution)/shard_map/dot_general | solution.py:368
  1313.7 12.5 all-to-all-done.2.received_ref
  1326.2 7.9 sum_rows.7.refs_1_
  1334.1 6.4 all-to-all-start.4
  1340.6 6.6 store_rows.5.rest_0_.refs_1_
  1347.2 69.8 %gated_proj.9 = bf16[384,5120]{1,0:T(8,128)(2,1)S(1)} custom-call(bf16[4,384,1792]{2,1,0:T(8,128)(2,1)} %bitcast.72, f32[1,7168]{1,0:T(1,128)S(1)} %bitcast.44, bf16[7168,5120]{1,0:T(8,128)(2,1)} %gate_ref.9, bf16[7168,5120]{1,0:T(8,128)(2,1)} %up_ref.9, bf16[3072,7168]{1,0:T(8,128)(2,1)} %store_rows.5.rest_0_.refs_1_), custom_call_target="tpu_custom_call" | custom-call | flops 56371445760 | bytes 156237824 | tf_op jit(solution)/shard_map/gated_proj/pallas_call | solution.py:182
  1417.1 36.5 %convolution_convert_fusion.3.rest_0_ = bf16[384,7168]{1,0:T(8,128)(2,1)} fusion(bf16[384,5120]{1,0:T(8,128)(2,1)S(1)} %gated_proj.9, bf16[5120,7168]{1,0:T(8,128)(2,1)} %param.21), kind=kOutput, calls=%fused_computation.3 | convolution fusion | flops 28188475392 | bytes 82837504 | tf_op jit(solution)/shard_map/dot_general | solution.py:368
  1453.6 67.2 %all-to-all-done.4.received_ref = bf16[4,192,7168]{2,1,0:T(8,128)(2,1)} async-done(((bf16[4,192,7168]{2,1,0:T(8,128)(2,1)}), bf16[4,192,7168]{2,1,0:T(8,128)(2,1)}, u32[]{:S(2)}, u32[]{:S(2)}) %all-to-all-start.4) | async-done | bytes 11010080 | tf_op jit(solution)/shard_map/all_to_all | solution.py:369
  1520.7 7.8 sum_rows.9.refs_2_
  1528.7 127.4 %all_to_all.25.received_ref = bf16[4,96,7168]{2,1,0:T(8,128)(2,1)} all-to-all(bf16[4,96,7168]{2,1,0:T(8,128)(2,1)} %bitcast.59), channel_id=1, replica_groups=mesh['dp'=2,'tp'=4] {'tp'}, dimensions={0} | all-to-all | bytes 11010048 | tf_op jit(solution)/shard_map/all_to_all | solution.py:369
  1656.1 4.9 sum_rows.8
  1663.5 1.2 constant_dynamic-update-slice_fusion.10
  1667.0 3.7 reshape.171
  1670.7 1.8 constant_dynamic-update-slice_fusion.9
  1672.5 1.9 constant_dynamic-update-slice_fusion.8
  1675.0 3.5 reshape.172
  1678.5 7.2 pad_maximum_fusion
  1685.8 5.7 pad_maximum_fusion.1
  1691.5 9.6 store_rows.6.refs_1_
  1701.1 9.5 store_rows.7.refs_1_
  1710.6 9.5 store_rows.8.refs_1_
  1720.2 5.9 store_rows.9
  (116 shorter events, 15.2 us)
Async XLA Ops:
  7.2 5.0 copy-start.21
  7.2 416.8 %all-gather.40.cloned.1.call-start = ((), (), s32[]{:S(2)}) async-start(), calls=%async_computation.12 | async-start | bytes 6881280 | tf_op jit(solution)/shard_map/all_gather | solution.py:341
  42.1 1.8 copy-start.2
  53.1 390.8 %all-gather.38.cloned.1.call-start = ((), (), s32[]{:S(2)}) async-start(), calls=%async_computation.11 | async-start | bytes 13762560 | tf_op jit(solution)/shard_map/all_gather | solution.py:341
  53.7 0.9 copy-start.9
  109.5 373.5 %all-gather.46.cloned.1.call-start = ((), (), s32[]{:S(2)}) async-start(), calls=%async_computation.15 | async-start | bytes 6881280 | tf_op jit(solution)/shard_map/all_gather | solution.py:352
  115.7 133.2 %collective-permute-start = (bf16[896,1792]{1,0:T(8,128)(2,1)}, bf16[896,1792]{1,0:T(8,128)(2,1)S(1)}, u32[]{:S(2)}, u32[]{:S(2)}) collective-permute-start(bf16[896,1792]{1,0:T(8,128)(2,1)} %get-tuple-element.54), channel_id=1, source_target_pairs={{0,2},{1,3},{2,0},{3,1},{4,6},{5,7},{6,4},{7,5}} | collective-permute-start | bytes 9633800 | tf_op jit(solution)/shard_map/ppermute | solution.py:320
  119.3 196.3 %collective-permute-start.1 = (bf16[896,1792]{1,0:T(8,128)(2,1)}, bf16[896,1792]{1,0:T(8,128)(2,1)}, u32[]{:S(2)}, u32[]{:S(2)}) collective-permute-start(bf16[896,1792]{1,0:T(8,128)(2,1)} %get-tuple-element.53), channel_id=1, source_target_pairs={{0,3},{1,2},{2,1},{3,0},{4,7},{5,6},{6,5},{7,4}} | collective-permute-start | bytes 9633800 | tf_op jit(solution)/shard_map/ppermute | solution.py:320
  119.3 131.7 %copy-start.5 = (bf16[768,256]{1,0:T(8,128)(2,1)S(1)}, bf16[768,256]{1,0:T(8,128)(2,1)}, u32[]{:S(2)}) copy-start(bf16[768,256]{1,0:T(8,128)(2,1)} %get-tuple-element.29.rest_0_) | copy-start | bytes 1179652
  126.5 297.4 %collective-permute-start.2 = (bf16[1792,1792]{1,0:T(8,128)(2,1)}, bf16[1792,1792]{1,0:T(8,128)(2,1)}, u32[]{:S(2)}, u32[]{:S(2)}) collective-permute-start(bf16[1792,1792]{1,0:T(8,128)(2,1)} %constant_dynamic-slice_fusion), channel_id=1, source_target_pairs={{0,1},{1,0},{2,3},{3,2},{4,5},{5,4},{6,7},{7,6}} | collective-permute-start | bytes 19267592 | tf_op jit(solution)/shard_map/ppermute | solution.py:323
  248.9 41.4 %copy-start = (bf16[896,1792]{1,0:T(8,128)(2,1)}, bf16[896,1792]{1,0:T(8,128)(2,1)S(1)}, u32[]{:S(2)}) copy-start(bf16[896,1792]{1,0:T(8,128)(2,1)S(1)} %collective-permute-done.rest_1_.rest_0_) | copy-start | bytes 9633796
  248.9 175.1 %collective-permute-start.3 = (bf16[896,1792]{1,0:T(8,128)(2,1)S(1)}, bf16[896,1792]{1,0:T(8,128)(2,1)}, u32[]{:S(2)}, u32[]{:S(2)}) collective-permute-start(bf16[896,1792]{1,0:T(8,128)(2,1)S(1)} %collective-permute-done.rest_1_.rest_0_), channel_id=1, source_target_pairs={{0,4},{4,0},{1,5},{5,1},{2,6},{6,2},{3,7},{7,3}} | collective-permute-start | bytes 9633800 | tf_op jit(solution)/shard_map/ppermute | solution.py:321
  315.6 108.3 %collective-permute-start.4 = (bf16[896,1792]{1,0:T(8,128)(2,1)}, bf16[896,1792]{1,0:T(8,128)(2,1)}, u32[]{:S(2)}, u32[]{:S(2)}) collective-permute-start(bf16[896,1792]{1,0:T(8,128)(2,1)} %collective-permute-done.1.rest_0_.rest_2_), channel_id=1, source_target_pairs={{0,4},{4,0},{1,5},{5,1},{2,6},{6,2},{3,7},{7,3}} | collective-permute-start | bytes 9633800 | tf_op jit(solution)/shard_map/ppermute | solution.py:321
  332.5 1.0 copy-start.7
  388.2 1.0 copy-start.3
  412.9 1.8 copy-start.1
  443.3 153.3 %all-gather.44.cloned.1.call-start = ((), (), s32[]{:S(2)}) async-start(), calls=%async_computation.14 | async-start | bytes 13762560 | tf_op jit(solution)/shard_map/all_gather | solution.py:341
  443.8 189.4 %all-gather.42.cloned.1.call-start = ((), (), s32[]{:S(2)}) async-start(), calls=%async_computation.13 | async-start | bytes 13762560 | tf_op jit(solution)/shard_map/all_gather | solution.py:352
  476.3 0.7 copy-start.22
  476.3 6.7 copy-start.14
  476.3 361.4 %all-gather.50.cloned.1.call-start = ((), (), s32[]{:S(2)}) async-start(), calls=%async_computation.17 | async-start | bytes 13762560 | tf_op jit(solution)/shard_map/all_gather | solution.py:341
  476.9 398.3 %all-gather.48.cloned.1.call-start = ((), (), s32[]{:S(2)}) async-start(), calls=%async_computation.16 | async-start | bytes 13762560 | tf_op jit(solution)/shard_map/all_gather | solution.py:352
  555.0 1.9 copy-start.15
  627.2 464.9 %all-gather.36.cloned.1.call-start = ((), (), s32[]{:S(2)}) async-start(), calls=%async_computation.10 | async-start | bytes 6881280 | tf_op jit(solution)/shard_map/all_gather | solution.py:341
  628.0 5.2 copy-start.12
  628.0 203.9 %all-to-all-start.1 = ((bf16[4,96,7168]{2,1,0:T(8,128)(2,1)}), bf16[4,96,7168]{2,1,0:T(8,128)(2,1)}, u32[]{:S(2)}, u32[]{:S(2)}) async-start(bf16[4,96,7168]{2,1,0:T(8,128)(2,1)} %bitcast.60), calls=%async_computation.1 | async-start | bytes 11010048 | tf_op jit(solution)/shard_map/all_to_all | solution.py:369
  633.1 485.2 %all-gather.54.cloned.1.call-start = ((), (), s32[]{:S(2)}) async-start(), calls=%async_computation.19 | async-start | bytes 13762560 | tf_op jit(solution)/shard_map/all_gather | solution.py:352
  868.4 6.8 copy-start.13
  868.4 215.8 %all-to-all-start = ((bf16[4,192,7168]{2,1,0:T(8,128)(2,1)}), bf16[4,192,7168]{2,1,0:T(8,128)(2,1)}, u32[]{:S(2)}, u32[]{:S(2)}) async-start(bf16[4,192,7168]{2,1,0:T(8,128)(2,1)} %bitcast.57), calls=%async_computation | async-start | bytes 22020096 | tf_op jit(solution)/shard_map/all_to_all | solution.py:369
  874.5 466.1 %all-gather.26.cloned.1.call-start = ((), (), s32[]{:S(2)}) async-start(), calls=%async_computation.5 | async-start | bytes 6881280 | tf_op jit(solution)/shard_map/all_gather | solution.py:357
  875.1 472.1 %all-gather.52.cloned.1.call-start = ((), (), s32[]{:S(2)}) async-start(), calls=%async_computation.18 | async-start | bytes 6881280 | tf_op jit(solution)/shard_map/all_gather | solution.py:352
  1111.4 7.0 copy-start.11
  1111.4 214.8 %all-to-all-start.2 = ((bf16[4,192,7168]{2,1,0:T(8,128)(2,1)}), bf16[4,192,7168]{2,1,0:T(8,128)(2,1)}, u32[]{:S(2)}, u32[]{:S(2)}) async-start(bf16[4,192,7168]{2,1,0:T(8,128)(2,1)} %bitcast.56), calls=%async_computation.2 | async-start | bytes 22020096 | tf_op jit(solution)/shard_map/all_to_all | solution.py:369
  1117.7 573.8 %all-gather.34.cloned.1.call-start = ((), (), s32[]{:S(2)}) async-start(), calls=%async_computation.9 | async-start | bytes 13762560 | tf_op jit(solution)/shard_map/all_gather | solution.py:357
  1118.3 582.8 %all-gather.32.cloned.1.call-start = ((), (), s32[]{:S(2)}) async-start(), calls=%async_computation.8 | async-start | bytes 13762560 | tf_op jit(solution)/shard_map/all_gather | solution.py:357
  1334.1 186.6 %all-to-all-start.4 = ((bf16[4,192,7168]{2,1,0:T(8,128)(2,1)}), bf16[4,192,7168]{2,1,0:T(8,128)(2,1)}, u32[]{:S(2)}, u32[]{:S(2)}) async-start(bf16[4,192,7168]{2,1,0:T(8,128)(2,1)} %bitcast.58), calls=%async_computation.4 | async-start | bytes 22020096 | tf_op jit(solution)/shard_map/all_to_all | solution.py:369
  1340.5 370.1 %all-gather.30.cloned.1.call-start = ((), (), s32[]{:S(2)}) async-start(), calls=%async_computation.7 | async-start | bytes 13762560 | tf_op jit(solution)/shard_map/all_gather | solution.py:357
  1528.6 191.6 %all-gather.28.cloned.1.call-start = ((), (), s32[]{:S(2)}) async-start(), calls=%async_computation.6 | async-start | bytes 6881280 | tf_op jit(solution)/shard_map/all_gather | solution.py:357
  1661.0 0.9 copy-start.10
  1661.0 1.0 copy-start.20
  1661.0 1.7 copy-start.6
  1661.0 3.7 copy-start.8
  1661.0 4.5 copy-start.4
  1661.0 5.3 copy-start.18
  1661.1 13.3 copy-start.19
  1663.5 15.0 slice-start.1
  1664.7 1.6 copy-start.17
  1672.5 13.3 slice-start
  1678.5 7.2 copy-start.16
Sparse Core Ops, SparseCore 0:
  53.3 41.9 all-gather.39
  109.7 132.3 all-gather.37
  443.4 39.6 all-gather.45
  485.0 70.3 all-gather.43
  557.3 70.3 all-gather.41
  629.1 127.0 all-gather.49
  758.3 70.4 all-gather.47
  830.3 39.1 all-gather.35
  871.6 129.4 all-gather.53
  1002.4 68.7 all-gather.25
  1111.5 67.7 all-gather.51
  1180.7 129.6 all-gather.33
  1334.3 129.4 all-gather.31
  1528.7 129.0 all-gather.29
  1661.2 39.0 all-gather.27

commit v4 on v3

--- a/solution.py
+++ b/solution.py
@@ -365,6 +365,8 @@
         for c in range(chunks):
             rows = CHUNKS[c] * seq_len
             gated = gated_proj(hidden[c], mlp_gain32, w_gate, w_up, deps)
+            if c == 1:
+                project(2, [gated])
             part = jnp.dot(gated, w_down, preferred_element_type=F32).astype(BF16)
             received[c] = lax.all_to_all(part.reshape(tp_size, rows // tp_size, width), "tp", 0, 0, tiled=True)
             deps = [part]
@@ -373,18 +375,20 @@
             if c >= 3:
                 y = store(c - 3, y, deps)
                 deps = [y]
-            if c + 2 < chunks:
+            if c >= 1 and c + 2 < chunks:
                 deps = project(c + 2, deps)
-        y = store(chunks - 3, y, [])
-        y = store(chunks - 2, y, [])
-        finish(chunks - 1, [])
-        y = store(chunks - 1, y, [])
 
         def cache(old, new):
             new = jnp.concatenate(new, axis=0).reshape(batch_size, seq_len, kv_local, head_dim)
             return jnp.concatenate([new, old[:, seq_len:]], axis=1)
 
-        return y.reshape(x.shape), cache(k_cache, new_keys), cache(v_cache, new_values)
+        caches = [cache(k_cache, new_keys), cache(v_cache, new_values)]
+        y = store(chunks - 3, y, [])
+        finish(chunks - 1, [y] + caches)
+        y = store(chunks - 2, y, [])
+        y = store(chunks - 1, y, [])
+
+        return y.reshape(x.shape), caches[0], caches[1]
 
     cache_spec = P("dp", None, "tp", None)
     return jax.shard_map(layer_shard, mesh=mesh, in_specs=(P("dp", None, None), P("dp"), P(None, "tp"), P(None, "tp"), P(None, "tp"), P("tp", None), P(None, "tp"), P(None, "tp"), P("tp", None), P(), P(), cache_spec, cache_spec), out_specs=(P("dp", None, None), cache_spec, cache_spec), check_vma=False)

time: 1740 us -> 1770 us (1.017)
  waiting for transfers between devices: 247 us -> 399 us
  blocking collectives: 127 us -> 0 us
    all_to_all x1 -> x0, blocking collectives: 127 us -> none  [layer_shard(): lax.all_to_all(part.reshape(tp_size, rows // tp_size, width), 'tp', 0, 0,...]
    all_to_all x4 -> x5, waiting for transfers between devices: 91.1 us -> 213 us  [layer_shard(): lax.all_to_all(part.reshape(tp_size, rows // tp_size, width), 'tp', 0, 0,...]
    all_gather x5, waiting for transfers between devices: 0.02 us -> 28.6 us  [finish(): gathered[c] = lax.all_gather(y_rows, 'tp', axis=0, tiled=True)]
  transfers between devices with their start and end apart: 24 -> 25, of which waited for: 6 -> 9; matrix products, arithmetic and copies ran while one was open for 18% -> 18% of each run, Pallas kernels for 54% -> 53%
where the time goes in v4:
time: 1770 us; the launch traced here: 1760 us
  Pallas kernels  970 us (55%)
  waiting for transfers between devices  399 us (23%)
  matrix products  277 us (16%)
  local copies, waits for them, and re-layouts  51.3 us (3%)
  starting transfers between devices  37.9 us (2%)
    pallas_call x5, Pallas kernels, gated_proj(): pl.pallas_call(functools.partial(gated_kernel, steps), grid=(steps + cols...  531 us
    dot_general x5, matrix products, layer_shard(): part = jnp.dot(gated, w_down, preferred_element_type=F32).astype(BF16)  277 us
    all_to_all x5, waiting for transfers between devices, layer_shard(): lax.all_to_all(part.reshape(tp_size, rows // tp_size, width), 'tp', 0, 0,...  213 us
    pallas_call x5, Pallas kernels, qkv_proj(): pl.pallas_call(functools.partial(qkv_kernel, steps, q_tiles), grid=(steps...  165 us
    ppermute x2, waiting for transfers between devices, layer_shard(): mine.append(lax.ppermute(block, 'tp', swaps[hop]))  147 us
    pallas_call x5, Pallas kernels, out_proj(): pl.pallas_call(functools.partial(out_proj_kernel, len(far)), grid_spec=pl...  133 us
    pallas_call x5, Pallas kernels, attention(): pl.pallas_call(functools.partial(attention_kernel, first_seq, group_size,...  64.8 us
    pallas_call x5, Pallas kernels, store_rows(): pl.pallas_call(store_kernel, grid=(rows // block,), in_specs=[pl.BlockSpe...  41.6 us
  transfers between devices with their start and end apart: 25, of which 9 were waited for; matrix products, arithmetic and copies ran while one was open for 18% of the time, Pallas kernels for 53%

profile of v4, /device:TPU:0, one launch (start us, length us, event | category | flops | bytes accessed | tf_op | source)
XLA Modules:
  0.0 1763.6 jit_solution(10784610662494723106)
XLA Ops:
  8.1 4.1 constant_dynamic-update-slice_fusion.1
  14.3 4.1 constant_dynamic-update-slice_fusion.wkv_ref
  18.5 23.7 %qkv_proj.5.q_ref.k_ref.v_ref = f32[384,2304]{1,0:T(8,128)S(1)} custom-call(bf16[3072,7168]{1,0:T(8,128)(2,1)} %bitcast.45, f32[1,7168]{1,0:T(1,128)S(1)} %bitcast.35, bf16[7168,1792]{1,0:T(8,128)(2,1)} %wq_ref.9, bf16[7168,512]{1,0:T(8,128)(2,1)} %constant_dynamic-update-slice_fusion.wkv_ref), custom_call_target="tpu_custom_call" | custom-call | flops 12683575296 | bytes 42074112 | tf_op jit(solution)/shard_map/qkv_proj/pallas_call | solution.py:144
  42.1 1.8 copy-done.2
  43.9 9.2 attention.5
  54.7 39.7 %qkv_proj.6.q_ref.k_ref.v_ref = f32[768,2304]{1,0:T(8,128)} custom-call(bf16[3072,7168]{1,0:T(8,128)(2,1)} %bitcast.46, f32[1,7168]{1,0:T(1,128)S(1)} %bitcast.36, bf16[7168,1792]{1,0:T(8,128)(2,1)} %wq_ref.9, bf16[7168,512]{1,0:T(8,128)(2,1)} %constant_dynamic-update-slice_fusion.wkv_ref, bf16[384,256]{1,0:T(8,128)(2,1)S(1)} %copy-done.9), custom_call_target="tpu_custom_call" | custom-call | flops 25367150592 | bytes 51118080 | tf_op jit(solution)/shard_map/qkv_proj/pallas_call | solution.py:144
  94.4 15.4 attention.6
  109.8 6.0 fusion.1
  115.8 3.7 collective-permute-start
  119.5 7.1 constant_dynamic-slice_fusion
  127.2 121.8 %collective-permute-done.rest_1_.rest_0_ = bf16[896,1792]{1,0:T(8,128)(2,1)S(1)} collective-permute-done((bf16[896,1792]{1,0:T(8,128)(2,1)}, bf16[896,1792]{1,0:T(8,128)(2,1)S(1)}, u32[]{:S(2)}, u32[]{:S(2)}) %collective-permute-start) | collective-permute-done | bytes 3211296 | tf_op jit(solution)/shard_map/ppermute | solution.py:320
  249.1 2.1 collective-permute-start.3
  251.2 39.3 %qkv_proj.7.q_ref.k_ref.v_ref = f32[768,2304]{1,0:T(8,128)} custom-call(bf16[3072,7168]{1,0:T(8,128)(2,1)} %bitcast.47, f32[1,7168]{1,0:T(1,128)S(1)} %bitcast.37, bf16[7168,1792]{1,0:T(8,128)(2,1)} %wq_ref.9, bf16[7168,512]{1,0:T(8,128)(2,1)} %constant_dynamic-update-slice_fusion.wkv_ref, bf16[768,256]{1,0:T(8,128)(2,1)S(1)} %copy-done.5, ...), custom_call_target="tpu_custom_call" | custom-call | flops 25367150592 | bytes 51118080 | tf_op jit(solution)/shard_map/qkv_proj/pallas_call | solution.py:144
  290.5 25.3 %collective-permute-done.1.rest_0_.rest_2_ = bf16[896,1792]{1,0:T(8,128)(2,1)} collective-permute-done((bf16[896,1792]{1,0:T(8,128)(2,1)}, bf16[896,1792]{1,0:T(8,128)(2,1)}, u32[]{:S(2)}, u32[]{:S(2)}) %collective-permute-start.1) | collective-permute-done | bytes 3211296 | tf_op jit(solution)/shard_map/ppermute | solution.py:320
  317.3 15.4 attention.7
  333.7 39.1 %qkv_proj.8.q_ref.k_ref.v_ref = f32[768,2304]{1,0:T(8,128)} custom-call(bf16[3072,7168]{1,0:T(8,128)(2,1)} %bitcast.48, f32[1,7168]{1,0:T(1,128)S(1)} %bitcast.38, bf16[7168,1792]{1,0:T(8,128)(2,1)} %wq_ref.9, bf16[7168,512]{1,0:T(8,128)(2,1)} %constant_dynamic-update-slice_fusion.wkv_ref, bf16[768,256]{1,0:T(8,128)(2,1)S(1)} %copy-done.7), custom_call_target="tpu_custom_call" | custom-call | flops 25367150592 | bytes 51118080 | tf_op jit(solution)/shard_map/qkv_proj/pallas_call | solution.py:144
  372.8 15.6 attention.8
  389.4 23.7 %qkv_proj.9.q_ref.k_ref.v_ref = f32[384,2304]{1,0:T(8,128)S(1)} custom-call(bf16[3072,7168]{1,0:T(8,128)(2,1)} %bitcast.49, f32[1,7168]{1,0:T(1,128)S(1)} %bitcast.39, bf16[7168,1792]{1,0:T(8,128)(2,1)} %wq_ref.9, bf16[7168,512]{1,0:T(8,128)(2,1)} %constant_dynamic-update-slice_fusion.wkv_ref, bf16[768,256]{1,0:T(8,128)(2,1)S(1)} %copy-done.3), custom_call_target="tpu_custom_call" | custom-call | flops 12683575296 | bytes 42074112 | tf_op jit(solution)/shard_map/qkv_proj/pallas_call | solution.py:144
  413.1 1.8 copy-done.1
  414.9 9.2 attention.9
  424.2 19.2 %out_proj.5 = (bf16[384,1792]{1,0:T(8,128)(2,1)}, f32[8,128]{1,0:T(8,128)}) custom-call(s32[2]{0:T(128)} %pad_add_fusion.place_ref, bf16[4,384,1792]{2,1,0:T(8,128)(2,1)} %bitcast.74, bf16[3072,7168]{1,0:T(8,128)(2,1)} %bitcast.50, bf16[1792,7168]{1,0:T(8,128)(2,1)} %own_ref.9, bf16[1792,1792]{1,0:T(8,128)(2,1)} %collective-permute-done.2.near_ref, ...), custom_call_target="tpu_custom_call" | custom-call | flops 9865003008 | bytes 31195136 | tf_op jit(solution)/shard_map/out_proj/pallas_call | solution.py:224
  443.5 31.8 %out_proj.6 = (bf16[768,1792]{1,0:T(8,128)(2,1)}, f32[8,128]{1,0:T(8,128)}) custom-call(s32[2]{0:T(128)} %pad_add_fusion.place_ref, bf16[4,768,1792]{2,1,0:T(8,128)(2,1)} %bitcast.68, bf16[3072,7168]{1,0:T(8,128)(2,1)} %bitcast.51, bf16[1792,7168]{1,0:T(8,128)(2,1)} %own_ref.9, bf16[1792,1792]{1,0:T(8,128)(2,1)} %collective-permute-done.2.near_ref, ...), custom_call_target="tpu_custom_call" | custom-call | flops 19730006016 | bytes 36700160 | tf_op jit(solution)/shard_map/out_proj/pallas_call | solution.py:224
  476.5 6.7 all-gather.44.cloned.1.call-done
  483.2 72.0 %gated_proj.5 = bf16[384,5120]{1,0:T(8,128)(2,1)S(1)} custom-call(bf16[4,384,1792]{2,1,0:T(8,128)(2,1)} %bitcast.69, f32[1,7168]{1,0:T(1,128)S(1)} %bitcast.40, bf16[7168,5120]{1,0:T(8,128)(2,1)} %gate_ref.9, bf16[7168,5120]{1,0:T(8,128)(2,1)} %up_ref.9, f32[8,128]{1,0:T(8,128)S(1)} %copy-done.11), custom_call_target="tpu_custom_call" | custom-call | flops 56371445760 | bytes 156237824 | tf_op jit(solution)/shard_map/gated_proj/pallas_call | solution.py:182
  555.2 1.9 copy-done.15
  557.1 39.5 %convolution_convert_fusion.4.rest_0_ = bf16[384,7168]{1,0:T(8,128)(2,1)} fusion(bf16[384,5120]{1,0:T(8,128)(2,1)} %copy-done.15, bf16[5120,7168]{1,0:T(8,128)(2,1)} %param.21), kind=kOutput, calls=%fused_computation.4 | convolution fusion | flops 28188475392 | bytes 82837504 | tf_op jit(solution)/shard_map/dot_general | solution.py:370
  596.6 129.4 %gated_proj.6.rest_4_ = bf16[768,5120]{1,0:T(8,128)(2,1)} custom-call(bf16[4,768,1792]{2,1,0:T(8,128)(2,1)} %bitcast.62, f32[1,7168]{1,0:T(1,128)S(1)} %bitcast.41, bf16[7168,5120]{1,0:T(8,128)(2,1)} %gate_ref.9, bf16[7168,5120]{1,0:T(8,128)(2,1)} %up_ref.9, bf16[384,7168]{1,0:T(8,128)(2,1)} %convolution_convert_fusion.4.rest_0_), custom_call_target="tpu_custom_call" | custom-call | flops 112742891520 | bytes 165675008 | tf_op jit(solution)/shard_map/gated_proj/pallas_call | solution.py:182
  726.1 30.5 %out_proj.7 = (bf16[768,1792]{1,0:T(8,128)(2,1)}, f32[8,128]{1,0:T(8,128)}) custom-call(s32[2]{0:T(128)} %pad_add_fusion.place_ref, bf16[4,768,1792]{2,1,0:T(8,128)(2,1)} %bitcast.61, bf16[3072,7168]{1,0:T(8,128)(2,1)} %bitcast.52, bf16[1792,7168]{1,0:T(8,128)(2,1)} %own_ref.9, bf16[1792,1792]{1,0:T(8,128)(2,1)} %collective-permute-done.2.near_ref, ...), custom_call_target="tpu_custom_call" | custom-call | flops 19730006016 | bytes 36700160 | tf_op jit(solution)/shard_map/out_proj/pallas_call | solution.py:224
  757.3 5.3 all-to-all-start.1
  762.7 67.8 %convolution_convert_fusion.2.rest_0_ = bf16[768,7168]{1,0:T(8,128)(2,1)} fusion(bf16[768,5120]{1,0:T(8,128)(2,1)} %gated_proj.6.rest_4_, bf16[5120,7168]{1,0:T(8,128)(2,1)} %param.21), kind=kOutput, calls=%fused_computation.2 | convolution fusion | flops 56376950784 | bytes 92274688 | tf_op jit(solution)/shard_map/dot_general | solution.py:370
  830.5 53.3 %all-to-all-done.1.received_ref = bf16[4,96,7168]{2,1,0:T(8,128)(2,1)} async-done(((bf16[4,96,7168]{2,1,0:T(8,128)(2,1)}), bf16[4,96,7168]{2,1,0:T(8,128)(2,1)}, u32[]{:S(2)}, u32[]{:S(2)}) %all-to-all-start.1) | async-done | bytes 5505056 | tf_op jit(solution)/shard_map/all_to_all | solution.py:371
  883.9 5.0 sum_rows.5.rest_4_
  888.8 32.3 %out_proj.8 = (bf16[768,1792]{1,0:T(8,128)(2,1)}, f32[8,128]{1,0:T(8,128)}) custom-call(s32[2]{0:T(128)} %pad_add_fusion.place_ref, bf16[4,768,1792]{2,1,0:T(8,128)(2,1)} %bitcast.60, bf16[3072,7168]{1,0:T(8,128)(2,1)} %bitcast.53, bf16[1792,7168]{1,0:T(8,128)(2,1)} %own_ref.9, bf16[1792,1792]{1,0:T(8,128)(2,1)} %collective-permute-done.2.near_ref, ...), custom_call_target="tpu_custom_call" | custom-call | flops 19730006016 | bytes 36700160 | tf_op jit(solution)/shard_map/out_proj/pallas_call | solution.py:224
  921.1 6.1 all-to-all-start
  927.9 130.7 %gated_proj.7 = bf16[768,5120]{1,0:T(8,128)(2,1)} custom-call(bf16[4,768,1792]{2,1,0:T(8,128)(2,1)} %bitcast.64, f32[1,7168]{1,0:T(1,128)S(1)} %bitcast.42, bf16[7168,5120]{1,0:T(8,128)(2,1)} %gate_ref.9, bf16[7168,5120]{1,0:T(8,128)(2,1)} %up_ref.9, f32[8,128]{1,0:T(8,128)S(1)} %copy-done.13), custom_call_target="tpu_custom_call" | custom-call | flops 112742891520 | bytes 165675008 | tf_op jit(solution)/shard_map/gated_proj/pallas_call | solution.py:182
  1058.6 66.3 %convolution_convert_fusion.1.rest_0_ = bf16[768,7168]{1,0:T(8,128)(2,1)} fusion(bf16[768,5120]{1,0:T(8,128)(2,1)} %gated_proj.7, bf16[5120,7168]{1,0:T(8,128)(2,1)} %param.21), kind=kOutput, calls=%fused_computation.1 | convolution fusion | flops 56376950784 | bytes 92274688 | tf_op jit(solution)/shard_map/dot_general | solution.py:370
  1124.9 12.1 all-to-all-done.received_ref
  1137.0 7.8 sum_rows.6.rest_4_
  1144.8 19.2 %out_proj.9 = (bf16[384,1792]{1,0:T(8,128)(2,1)}, f32[8,128]{1,0:T(8,128)}) custom-call(s32[2]{0:T(128)} %pad_add_fusion.place_ref, bf16[4,384,1792]{2,1,0:T(8,128)(2,1)} %bitcast.75, bf16[3072,7168]{1,0:T(8,128)(2,1)} %bitcast.54, bf16[1792,7168]{1,0:T(8,128)(2,1)} %own_ref.9, bf16[1792,1792]{1,0:T(8,128)(2,1)} %collective-permute-done.2.near_ref, ...), custom_call_target="tpu_custom_call" | custom-call | flops 9865003008 | bytes 31195136 | tf_op jit(solution)/shard_map/out_proj/pallas_call | solution.py:224
  1164.0 6.3 all-to-all-start.2
  1171.0 129.5 %gated_proj.8 = bf16[768,5120]{1,0:T(8,128)(2,1)} custom-call(bf16[4,768,1792]{2,1,0:T(8,128)(2,1)} %bitcast.66, f32[1,7168]{1,0:T(1,128)S(1)} %bitcast.43, bf16[7168,5120]{1,0:T(8,128)(2,1)} %gate_ref.9, bf16[7168,5120]{1,0:T(8,128)(2,1)} %up_ref.9, f32[8,128]{1,0:T(8,128)S(1)} %copy-done.12), custom_call_target="tpu_custom_call" | custom-call | flops 112742891520 | bytes 165675008 | tf_op jit(solution)/shard_map/gated_proj/pallas_call | solution.py:182
  1300.4 65.7 %convolution_convert_fusion.rest_0_ = bf16[768,7168]{1,0:T(8,128)(2,1)} fusion(bf16[768,5120]{1,0:T(8,128)(2,1)} %gated_proj.8, bf16[5120,7168]{1,0:T(8,128)(2,1)} %param.21), kind=kOutput, calls=%fused_computation | convolution fusion | flops 56376950784 | bytes 92274688 | tf_op jit(solution)/shard_map/dot_general | solution.py:370
  1366.1 12.7 all-to-all-done.2.received_ref
  1378.8 7.8 sum_rows.7.refs_1_
  1386.7 6.4 all-to-all-start.4
  1393.1 6.7 store_rows.5.rest_0_.refs_1_
  1399.8 69.8 %gated_proj.9 = bf16[384,5120]{1,0:T(8,128)(2,1)S(1)} custom-call(bf16[4,384,1792]{2,1,0:T(8,128)(2,1)} %bitcast.72, f32[1,7168]{1,0:T(1,128)S(1)} %bitcast.44, bf16[7168,5120]{1,0:T(8,128)(2,1)} %gate_ref.9, bf16[7168,5120]{1,0:T(8,128)(2,1)} %up_ref.9, bf16[3072,7168]{1,0:T(8,128)(2,1)} %store_rows.5.rest_0_.refs_1_), custom_call_target="tpu_custom_call" | custom-call | flops 56371445760 | bytes 156237824 | tf_op jit(solution)/shard_map/gated_proj/pallas_call | solution.py:182
  1469.6 2.0 copy-done.14
  1471.6 37.5 %convolution_convert_fusion.3.rest_0_ = bf16[384,7168]{1,0:T(8,128)(2,1)} fusion(bf16[384,5120]{1,0:T(8,128)(2,1)} %copy-done.14, bf16[5120,7168]{1,0:T(8,128)(2,1)} %param.21), kind=kOutput, calls=%fused_computation.3 | convolution fusion | flops 28188475392 | bytes 82837504 | tf_op jit(solution)/shard_map/dot_general | solution.py:370
  1509.1 64.1 %all-to-all-done.4.received_ref = bf16[4,192,7168]{2,1,0:T(8,128)(2,1)} async-done(((bf16[4,192,7168]{2,1,0:T(8,128)(2,1)}), bf16[4,192,7168]{2,1,0:T(8,128)(2,1)}, u32[]{:S(2)}, u32[]{:S(2)}) %all-to-all-start.4) | async-done | bytes 11010080 | tf_op jit(solution)/shard_map/all_to_all | solution.py:371
  1573.3 7.8 sum_rows.8.refs_2_
  1581.1 5.3 all-to-all-start.3
  1591.3 3.8 reshape.170
  1596.9 1.9 constant_dynamic-update-slice_fusion.8
  1600.4 3.5 reshape.171
  1603.9 7.2 pad_maximum_fusion.rest_1_
  1611.2 5.7 pad_maximum_fusion.1.rest_2_
  1616.9 9.6 store_rows.6.refs_1_
  1626.5 9.5 store_rows.7.rest_0_.refs_1_
  1636.0 71.2 %all-to-all-done.3.received_ref = bf16[4,96,7168]{2,1,0:T(8,128)(2,1)} async-done(((bf16[4,96,7168]{2,1,0:T(8,128)(2,1)}), bf16[4,96,7168]{2,1,0:T(8,128)(2,1)}, u32[]{:S(2)}, u32[]{:S(2)}) %all-to-all-start.3) | async-done | bytes 5505056 | tf_op jit(solution)/shard_map/all_to_all | solution.py:371
  1707.2 5.0 sum_rows.9
  1712.3 9.9 store_rows.8.refs_1_
  1722.1 28.6 %all-gather.32.cloned.1.call-done.refs_0_ = bf16[384,7168]{1,0:T(8,128)(2,1)} async-done(((bf16[96,7168]{1,0:T(8,128)(2,1)}), bf16[384,7168]{1,0:T(8,128)(2,1)}) %all-gather.32.cloned.1.call-update) | async-done | bytes 5505040 | tf_op jit(solution)/shard_map/all_gather | solution.py:357
  1750.7 5.9 store_rows.9
  (117 shorter events, 20.5 us)
Async XLA Ops:
  7.2 5.0 copy-start.21
  7.2 417.0 %all-gather.40.cloned.1.call-start = ((), (), s32[]{:S(2)}) async-start(), calls=%async_computation.12 | async-start | bytes 6881280 | tf_op jit(solution)/shard_map/all_gather | solution.py:341
  42.1 1.8 copy-start.2
  53.2 390.3 %all-gather.38.cloned.1.call-start = ((), (), s32[]{:S(2)}) async-start(), calls=%async_computation.11 | async-start | bytes 13762560 | tf_op jit(solution)/shard_map/all_gather | solution.py:341
  53.7 0.9 copy-start.9
  109.7 373.4 %all-gather.44.cloned.1.call-start = ((), (), s32[]{:S(2)}) async-start(), calls=%async_computation.14 | async-start | bytes 6881280 | tf_op jit(solution)/shard_map/all_gather | solution.py:352
  115.8 133.3 %collective-permute-start = (bf16[896,1792]{1,0:T(8,128)(2,1)}, bf16[896,1792]{1,0:T(8,128)(2,1)S(1)}, u32[]{:S(2)}, u32[]{:S(2)}) collective-permute-start(bf16[896,1792]{1,0:T(8,128)(2,1)} %get-tuple-element.52), channel_id=1, source_target_pairs={{0,2},{1,3},{2,0},{3,1},{4,6},{5,7},{6,4},{7,5}} | collective-permute-start | bytes 9633800 | tf_op jit(solution)/shard_map/ppermute | solution.py:320
  119.5 196.2 %collective-permute-start.1 = (bf16[896,1792]{1,0:T(8,128)(2,1)}, bf16[896,1792]{1,0:T(8,128)(2,1)}, u32[]{:S(2)}, u32[]{:S(2)}) collective-permute-start(bf16[896,1792]{1,0:T(8,128)(2,1)} %get-tuple-element.51), channel_id=1, source_target_pairs={{0,3},{1,2},{2,1},{3,0},{4,7},{5,6},{6,5},{7,4}} | collective-permute-start | bytes 9633800 | tf_op jit(solution)/shard_map/ppermute | solution.py:320
  119.5 131.7 %copy-start.5 = (bf16[768,256]{1,0:T(8,128)(2,1)S(1)}, bf16[768,256]{1,0:T(8,128)(2,1)}, u32[]{:S(2)}) copy-start(bf16[768,256]{1,0:T(8,128)(2,1)} %get-tuple-element.28.rest_0_) | copy-start | bytes 1179652
  126.6 297.5 %collective-permute-start.2 = (bf16[1792,1792]{1,0:T(8,128)(2,1)}, bf16[1792,1792]{1,0:T(8,128)(2,1)}, u32[]{:S(2)}, u32[]{:S(2)}) collective-permute-start(bf16[1792,1792]{1,0:T(8,128)(2,1)} %constant_dynamic-slice_fusion), channel_id=1, source_target_pairs={{0,1},{1,0},{2,3},{3,2},{4,5},{5,4},{6,7},{7,6}} | collective-permute-start | bytes 19267592 | tf_op jit(solution)/shard_map/ppermute | solution.py:323
  249.1 41.4 %copy-start = (bf16[896,1792]{1,0:T(8,128)(2,1)}, bf16[896,1792]{1,0:T(8,128)(2,1)S(1)}, u32[]{:S(2)}) copy-start(bf16[896,1792]{1,0:T(8,128)(2,1)S(1)} %collective-permute-done.rest_1_.rest_0_) | copy-start | bytes 9633796
  249.1 175.0 %collective-permute-start.3 = (bf16[896,1792]{1,0:T(8,128)(2,1)S(1)}, bf16[896,1792]{1,0:T(8,128)(2,1)}, u32[]{:S(2)}, u32[]{:S(2)}) collective-permute-start(bf16[896,1792]{1,0:T(8,128)(2,1)S(1)} %collective-permute-done.rest_1_.rest_0_), channel_id=1, source_target_pairs={{0,4},{4,0},{1,5},{5,1},{2,6},{6,2},{3,7},{7,3}} | collective-permute-start | bytes 9633800 | tf_op jit(solution)/shard_map/ppermute | solution.py:321
  315.8 108.4 %collective-permute-start.4 = (bf16[896,1792]{1,0:T(8,128)(2,1)}, bf16[896,1792]{1,0:T(8,128)(2,1)}, u32[]{:S(2)}, u32[]{:S(2)}) collective-permute-start(bf16[896,1792]{1,0:T(8,128)(2,1)} %collective-permute-done.1.rest_0_.rest_2_), channel_id=1, source_target_pairs={{0,4},{4,0},{1,5},{5,1},{2,6},{6,2},{3,7},{7,3}} | collective-permute-start | bytes 9633800 | tf_op jit(solution)/shard_map/ppermute | solution.py:321
  332.7 1.0 copy-start.7
  388.4 1.0 copy-start.3
  413.1 1.8 copy-start.1
  443.4 153.2 %all-gather.42.cloned.1.call-start = ((), (), s32[]{:S(2)}) async-start(), calls=%async_computation.13 | async-start | bytes 13762560 | tf_op jit(solution)/shard_map/all_gather | solution.py:352
  475.3 0.7 copy-start.22
  475.3 7.9 copy-start.11
  475.3 250.8 %all-gather.46.cloned.1.call-start = ((), (), s32[]{:S(2)}) async-start(), calls=%async_computation.15 | async-start | bytes 13762560 | tf_op jit(solution)/shard_map/all_gather | solution.py:341
  475.9 412.9 %all-gather.50.cloned.1.call-start = ((), (), s32[]{:S(2)}) async-start(), calls=%async_computation.17 | async-start | bytes 13762560 | tf_op jit(solution)/shard_map/all_gather | solution.py:341
  476.5 451.5 %all-gather.48.cloned.1.call-start = ((), (), s32[]{:S(2)}) async-start(), calls=%async_computation.16 | async-start | bytes 13762560 | tf_op jit(solution)/shard_map/all_gather | solution.py:352
  555.2 1.9 copy-start.15
  756.6 388.2 %all-gather.36.cloned.1.call-start = ((), (), s32[]{:S(2)}) async-start(), calls=%async_computation.10 | async-start | bytes 6881280 | tf_op jit(solution)/shard_map/all_gather | solution.py:341
  757.3 126.5 %all-to-all-start.1 = ((bf16[4,96,7168]{2,1,0:T(8,128)(2,1)}), bf16[4,96,7168]{2,1,0:T(8,128)(2,1)}, u32[]{:S(2)}, u32[]{:S(2)}) async-start(bf16[4,96,7168]{2,1,0:T(8,128)(2,1)} %bitcast.71), calls=%async_computation.1 | async-start | bytes 11010048 | tf_op jit(solution)/shard_map/all_to_all | solution.py:371
  762.7 408.3 %all-gather.54.cloned.1.call-start = ((), (), s32[]{:S(2)}) async-start(), calls=%async_computation.19 | async-start | bytes 13762560 | tf_op jit(solution)/shard_map/all_gather | solution.py:352
  921.1 6.8 copy-start.13
  921.1 215.8 %all-to-all-start = ((bf16[4,192,7168]{2,1,0:T(8,128)(2,1)}), bf16[4,192,7168]{2,1,0:T(8,128)(2,1)}, u32[]{:S(2)}, u32[]{:S(2)}) async-start(bf16[4,192,7168]{2,1,0:T(8,128)(2,1)} %bitcast.57), calls=%async_computation | async-start | bytes 22020096 | tf_op jit(solution)/shard_map/all_to_all | solution.py:371
  927.3 465.9 %all-gather.26.cloned.1.call-start = ((), (), s32[]{:S(2)}) async-start(), calls=%async_computation.5 | async-start | bytes 6881280 | tf_op jit(solution)/shard_map/all_gather | solution.py:357
  927.8 471.9 %all-gather.52.cloned.1.call-start = ((), (), s32[]{:S(2)}) async-start(), calls=%async_computation.18 | async-start | bytes 6881280 | tf_op jit(solution)/shard_map/all_gather | solution.py:352
  1164.0 7.0 copy-start.12
  1164.0 214.8 %all-to-all-start.2 = ((bf16[4,192,7168]{2,1,0:T(8,128)(2,1)}), bf16[4,192,7168]{2,1,0:T(8,128)(2,1)}, u32[]{:S(2)}, u32[]{:S(2)}) async-start(bf16[4,192,7168]{2,1,0:T(8,128)(2,1)} %bitcast.56), calls=%async_computation.2 | async-start | bytes 22020096 | tf_op jit(solution)/shard_map/all_to_all | solution.py:371
  1170.3 446.6 %all-gather.30.cloned.1.call-start = ((), (), s32[]{:S(2)}) async-start(), calls=%async_computation.7 | async-start | bytes 13762560 | tf_op jit(solution)/shard_map/all_gather | solution.py:357
  1170.9 455.6 %all-gather.28.cloned.1.call-start = ((), (), s32[]{:S(2)}) async-start(), calls=%async_computation.6 | async-start | bytes 13762560 | tf_op jit(solution)/shard_map/all_gather | solution.py:357
  1386.7 186.6 %all-to-all-start.4 = ((bf16[4,192,7168]{2,1,0:T(8,128)(2,1)}), bf16[4,192,7168]{2,1,0:T(8,128)(2,1)}, u32[]{:S(2)}, u32[]{:S(2)}) async-start(bf16[4,192,7168]{2,1,0:T(8,128)(2,1)} %bitcast.58), calls=%async_computation.4 | async-start | bytes 22020096 | tf_op jit(solution)/shard_map/all_to_all | solution.py:371
  1393.0 319.2 %all-gather.34.cloned.1.call-start = ((), (), s32[]{:S(2)}) async-start(), calls=%async_computation.9 | async-start | bytes 13762560 | tf_op jit(solution)/shard_map/all_gather | solution.py:357
  1469.6 2.0 copy-start.14
  1581.1 126.1 %all-to-all-start.3 = ((bf16[4,96,7168]{2,1,0:T(8,128)(2,1)}), bf16[4,96,7168]{2,1,0:T(8,128)(2,1)}, u32[]{:S(2)}, u32[]{:S(2)}) async-start(bf16[4,96,7168]{2,1,0:T(8,128)(2,1)} %bitcast.59), calls=%async_computation.3 | async-start | bytes 11010048 | tf_op jit(solution)/shard_map/all_to_all | solution.py:371
  1586.4 1.0 copy-start.10
  1586.4 1.1 copy-start.20
  1586.4 1.8 copy-start.6
  1586.4 2.6 copy-start.19
  1586.5 2.6 copy-start.8
  1586.5 3.4 copy-start.4
  1586.5 4.2 copy-start.18
  1586.5 164.2 %all-gather.32.cloned.1.call-start = ((), (), s32[]{:S(2)}) async-start(), calls=%async_computation.8 | async-start | bytes 6881280 | tf_op jit(solution)/shard_map/all_gather | solution.py:357
  1589.0 14.9 slice-start.1
  1589.1 1.6 copy-start.17
  1596.9 14.2 slice-start
  1603.9 7.2 copy-start.16
Sparse Core Ops, SparseCore 0:
  53.3 41.9 all-gather.39
  109.9 132.3 all-gather.37
  443.5 39.6 all-gather.43
  485.1 70.3 all-gather.41
  557.5 70.3 all-gather.45
  629.3 70.3 all-gather.49
  756.7 128.9 all-gather.47
  887.2 39.2 all-gather.35
  928.6 129.4 all-gather.53
  1059.5 68.6 all-gather.25
  1164.1 67.6 all-gather.51
  1233.2 129.7 all-gather.29
  1386.8 129.4 all-gather.27
  1581.2 128.1 all-gather.33
  1712.4 38.3 all-gather.31

commit v5 on v4

--- a/solution.py
+++ b/solution.py
@@ -197,22 +197,39 @@
     )(hidden, gain, w_gate, w_up, *deps)
 
 
-def out_proj_kernel(n_far, place_ref, heads_ref, x_ref, own_ref, near_ref, *rest):
+def out_proj_kernel(n_far, place_ref, all_heads_ref, x_ref, own_ref, near_ref, *rest):
     far_refs = rest[:n_far]
-    h_ref, token_ref = rest[-2:]
+    h_ref, token_ref, heads_ref, sems = rest[-4:]
+    tp_index, dp_index = place_ref[0], place_ref[1]
+    half = far_refs[0].shape[0]
+    parts = heads_ref.shape[0]
     token_ref[...] = jnp.zeros_like(token_ref)
-    tp_index, dp_index = place_ref[0], place_ref[1]
-    total = x_ref[...].astype(F32)
-    half = far_refs[0].shape[0]
-    for hop, block in enumerate((own_ref, near_ref)):
-        total = total + jnp.dot(heads_ref[tp_index ^ hop], block[...], preferred_element_type=F32).astype(BF16).astype(F32)
-    for hop in range(2, 2 + len(far_refs) // 2):
-        part = 0.0
-        for side in range(2):
-            start = pl.multiple_of((dp_index ^ side) * half, half)
-            part = part + jnp.dot(heads_ref[tp_index ^ hop, :, pl.ds(start, half)], far_refs[2 * (hop - 2) + side][...], preferred_element_type=F32)
-        total = total + part.astype(BF16).astype(F32)
-    h_ref[...] = total.astype(BF16)
+    copies = [pltpu.make_async_copy(all_heads_ref.at[tp_index ^ hop], heads_ref.at[hop], sems.at[hop]) for hop in range(parts)]
+
+    def body(arriving):
+        total = x_ref[...].astype(F32)
+        for hop in range(parts):
+            if arriving:
+                copies[hop].wait()
+            if hop < 2:
+                part = jnp.dot(heads_ref[hop], (own_ref, near_ref)[hop][...], preferred_element_type=F32)
+            else:
+                part = 0.0
+                for side in range(2):
+                    start = pl.multiple_of((dp_index ^ side) * half, half)
+                    part = part + jnp.dot(heads_ref[hop, :, pl.ds(start, half)], far_refs[2 * (hop - 2) + side][...], preferred_element_type=F32)
+            total = total + part.astype(BF16).astype(F32)
+        h_ref[...] = total.astype(BF16)
+
+    @pl.when(pl.program_id(0) == 0)
+    def _():
+        for copy in copies:
+            copy.start()
+        body(True)
+
+    @pl.when(pl.program_id(0) > 0)
+    def _():
+        body(False)
 
 
 def out_proj(place, heads, x_rows, w_out, near, far, first_row, deps):
@@ -227,12 +244,13 @@
             num_scalar_prefetch=1,
             grid=(steps,),
             in_specs=[
-                pl.BlockSpec((parts, rows, width), lambda n, place: (0, 0, 0)),
+                ANY,
                 pl.BlockSpec((rows, block), lambda n, place: (first_row // rows, place[0] * steps + n)) if first_row % rows == 0 else pl.BlockSpec((pl.Element(rows), pl.Element(block)), lambda n, place: (first_row, (place[0] * steps + n) * block)),
                 pl.BlockSpec((width, block), lambda n, place: (0, place[0] * steps + n)),
                 pl.BlockSpec((width, block), lambda n, place: (0, n)),
             ] + [pl.BlockSpec((half, block), lambda n, place: (0, n))] * len(far) + [ANY] * len(deps),
             out_specs=[pl.BlockSpec((rows, block), lambda n, place: (0, n)), pl.BlockSpec((8, 128), lambda n, place: (0, 0))],
+            scratch_shapes=[pltpu.VMEM((parts, rows, width), BF16), pltpu.SemaphoreType.DMA((parts,))],
         ),
         out_shape=[jax.ShapeDtypeStruct((rows, cols), BF16), jax.ShapeDtypeStruct((8, 128), F32)],
         compiler_params=pltpu.CompilerParams(vmem_limit_bytes=56 * 2**20),

time: 1770 us -> 1780 us (level)
  no operation moved by 1% of the time
where the time goes in v5:
time: 1780 us; the launch traced here: 1770 us
  Pallas kernels  978 us (55%)
  waiting for transfers between devices  396 us (22%)
  matrix products  278 us (16%)
  local copies, waits for them, and re-layouts  51.2 us (3%)
  starting transfers between devices  37.5 us (2%)
    pallas_call x5, Pallas kernels, gated_proj(): pl.pallas_call(functools.partial(gated_kernel, steps), grid=(steps + cols...  531 us
    dot_general x5, matrix products, layer_shard(): part = jnp.dot(gated, w_down, preferred_element_type=F32).astype(BF16)  278 us
    all_to_all x5, waiting for transfers between devices, layer_shard(): lax.all_to_all(part.reshape(tp_size, rows // tp_size, width), 'tp', 0, 0,...  212 us
    pallas_call x5, Pallas kernels, qkv_proj(): pl.pallas_call(functools.partial(qkv_kernel, steps, q_tiles), grid=(steps...  165 us
    ppermute x2, waiting for transfers between devices, layer_shard(): mine.append(lax.ppermute(block, 'tp', swaps[hop]))  148 us
    pallas_call x5, Pallas kernels, out_proj(): pl.pallas_call(functools.partial(out_proj_kernel, len(far)), grid_spec=pl...  141 us
    pallas_call x5, Pallas kernels, attention(): pl.pallas_call(functools.partial(attention_kernel, first_seq, group_size,...  65 us
    pallas_call x5, Pallas kernels, store_rows(): pl.pallas_call(store_kernel, grid=(rows // block,), in_specs=[pl.BlockSpe...  41.7 us
  transfers between devices with their start and end apart: 25, of which 9 were waited for; matrix products, arithmetic and copies ran while one was open for 18% of the time, Pallas kernels for 53%

profile of v5, /device:TPU:0, one launch (start us, length us, event | category | flops | bytes accessed | tf_op | source)
XLA Modules:
  0.0 1769.7 jit_solution(3666485813400076591)
XLA Ops:
  8.1 4.1 constant_dynamic-update-slice_fusion.1
  14.3 4.1 constant_dynamic-update-slice_fusion.wkv_ref
  18.5 23.7 %qkv_proj.5.q_ref.k_ref.v_ref = f32[384,2304]{1,0:T(8,128)S(1)} custom-call(bf16[3072,7168]{1,0:T(8,128)(2,1)} %bitcast.45, f32[1,7168]{1,0:T(1,128)S(1)} %bitcast.35, bf16[7168,1792]{1,0:T(8,128)(2,1)} %wq_ref.9, bf16[7168,512]{1,0:T(8,128)(2,1)} %constant_dynamic-update-slice_fusion.wkv_ref), custom_call_target="tpu_custom_call" | custom-call | flops 12683575296 | bytes 42074112 | tf_op jit(solution)/shard_map/qkv_proj/pallas_call | solution.py:144
  42.1 1.8 copy-done.2
  43.9 9.2 attention.5
  54.4 39.6 %qkv_proj.6.q_ref.k_ref.v_ref = f32[768,2304]{1,0:T(8,128)} custom-call(bf16[3072,7168]{1,0:T(8,128)(2,1)} %bitcast.46, f32[1,7168]{1,0:T(1,128)S(1)} %bitcast.36, bf16[7168,1792]{1,0:T(8,128)(2,1)} %wq_ref.9, bf16[7168,512]{1,0:T(8,128)(2,1)} %constant_dynamic-update-slice_fusion.wkv_ref, bf16[384,256]{1,0:T(8,128)(2,1)S(1)} %copy-done.9), custom_call_target="tpu_custom_call" | custom-call | flops 25367150592 | bytes 51118080 | tf_op jit(solution)/shard_map/qkv_proj/pallas_call | solution.py:144
  94.0 15.4 attention.6
  109.4 6.0 fusion.1
  115.5 3.5 collective-permute-start
  118.9 7.1 constant_dynamic-slice_fusion
  126.7 121.8 %collective-permute-done.rest_1_.rest_0_ = bf16[896,1792]{1,0:T(8,128)(2,1)S(1)} collective-permute-done((bf16[896,1792]{1,0:T(8,128)(2,1)}, bf16[896,1792]{1,0:T(8,128)(2,1)S(1)}, u32[]{:S(2)}, u32[]{:S(2)}) %collective-permute-start) | collective-permute-done | bytes 3211296 | tf_op jit(solution)/shard_map/ppermute | solution.py:338
  248.5 2.1 collective-permute-start.3
  250.6 39.3 %qkv_proj.7.q_ref.k_ref.v_ref = f32[768,2304]{1,0:T(8,128)} custom-call(bf16[3072,7168]{1,0:T(8,128)(2,1)} %bitcast.47, f32[1,7168]{1,0:T(1,128)S(1)} %bitcast.37, bf16[7168,1792]{1,0:T(8,128)(2,1)} %wq_ref.9, bf16[7168,512]{1,0:T(8,128)(2,1)} %constant_dynamic-update-slice_fusion.wkv_ref, bf16[768,256]{1,0:T(8,128)(2,1)S(1)} %copy-done.5, ...), custom_call_target="tpu_custom_call" | custom-call | flops 25367150592 | bytes 51118080 | tf_op jit(solution)/shard_map/qkv_proj/pallas_call | solution.py:144
  289.9 25.8 %collective-permute-done.1.rest_0_.rest_2_ = bf16[896,1792]{1,0:T(8,128)(2,1)} collective-permute-done((bf16[896,1792]{1,0:T(8,128)(2,1)}, bf16[896,1792]{1,0:T(8,128)(2,1)}, u32[]{:S(2)}, u32[]{:S(2)}) %collective-permute-start.1) | collective-permute-done | bytes 3211296 | tf_op jit(solution)/shard_map/ppermute | solution.py:338
  317.2 15.4 attention.7
  333.5 39.1 %qkv_proj.8.q_ref.k_ref.v_ref = f32[768,2304]{1,0:T(8,128)} custom-call(bf16[3072,7168]{1,0:T(8,128)(2,1)} %bitcast.48, f32[1,7168]{1,0:T(1,128)S(1)} %bitcast.38, bf16[7168,1792]{1,0:T(8,128)(2,1)} %wq_ref.9, bf16[7168,512]{1,0:T(8,128)(2,1)} %constant_dynamic-update-slice_fusion.wkv_ref, bf16[768,256]{1,0:T(8,128)(2,1)S(1)} %copy-done.7), custom_call_target="tpu_custom_call" | custom-call | flops 25367150592 | bytes 51118080 | tf_op jit(solution)/shard_map/qkv_proj/pallas_call | solution.py:144
  372.6 15.9 attention.8
  389.5 23.7 %qkv_proj.9.q_ref.k_ref.v_ref = f32[384,2304]{1,0:T(8,128)S(1)} custom-call(bf16[3072,7168]{1,0:T(8,128)(2,1)} %bitcast.49, f32[1,7168]{1,0:T(1,128)S(1)} %bitcast.39, bf16[7168,1792]{1,0:T(8,128)(2,1)} %wq_ref.9, bf16[7168,512]{1,0:T(8,128)(2,1)} %constant_dynamic-update-slice_fusion.wkv_ref, bf16[768,256]{1,0:T(8,128)(2,1)S(1)} %copy-done.3), custom_call_target="tpu_custom_call" | custom-call | flops 12683575296 | bytes 42074112 | tf_op jit(solution)/shard_map/qkv_proj/pallas_call | solution.py:144
  413.2 1.8 copy-done.1
  415.0 9.2 attention.9
  424.3 20.7 %out_proj.5 = (bf16[384,1792]{1,0:T(8,128)(2,1)}, f32[8,128]{1,0:T(8,128)}) custom-call(s32[2]{0:T(128)} %pad_add_fusion.place_ref, bf16[4,384,1792]{2,1,0:T(8,128)(2,1)} %bitcast.74, bf16[3072,7168]{1,0:T(8,128)(2,1)} %bitcast.50, bf16[1792,7168]{1,0:T(8,128)(2,1)} %own_ref.9, bf16[1792,1792]{1,0:T(8,128)(2,1)} %collective-permute-done.2.near_ref, ...), custom_call_target="tpu_custom_call" | custom-call | flops 9865003008 | bytes 31195136 | tf_op jit(solution)/shard_map/out_proj/pallas_call | solution.py:241
  445.1 33.2 %out_proj.6 = (bf16[768,1792]{1,0:T(8,128)(2,1)}, f32[8,128]{1,0:T(8,128)}) custom-call(s32[2]{0:T(128)} %pad_add_fusion.place_ref, bf16[4,768,1792]{2,1,0:T(8,128)(2,1)} %bitcast.68, bf16[3072,7168]{1,0:T(8,128)(2,1)} %bitcast.51, bf16[1792,7168]{1,0:T(8,128)(2,1)} %own_ref.9, bf16[1792,1792]{1,0:T(8,128)(2,1)} %collective-permute-done.2.near_ref, ...), custom_call_target="tpu_custom_call" | custom-call | flops 19730006016 | bytes 36700160 | tf_op jit(solution)/shard_map/out_proj/pallas_call | solution.py:241
  479.6 5.2 all-gather.44.cloned.1.call-done
  484.8 71.7 %gated_proj.5 = bf16[384,5120]{1,0:T(8,128)(2,1)S(1)} custom-call(bf16[4,384,1792]{2,1,0:T(8,128)(2,1)} %bitcast.69, f32[1,7168]{1,0:T(1,128)S(1)} %bitcast.40, bf16[7168,5120]{1,0:T(8,128)(2,1)} %gate_ref.9, bf16[7168,5120]{1,0:T(8,128)(2,1)} %up_ref.9, f32[8,128]{1,0:T(8,128)S(1)} %copy-done.11), custom_call_target="tpu_custom_call" | custom-call | flops 56371445760 | bytes 156237824 | tf_op jit(solution)/shard_map/gated_proj/pallas_call | solution.py:182
  556.6 1.9 copy-done.15
  558.5 39.5 %convolution_convert_fusion.4.rest_0_ = bf16[384,7168]{1,0:T(8,128)(2,1)} fusion(bf16[384,5120]{1,0:T(8,128)(2,1)} %copy-done.15, bf16[5120,7168]{1,0:T(8,128)(2,1)} %param.21), kind=kOutput, calls=%fused_computation.4 | convolution fusion | flops 28188475392 | bytes 82837504 | tf_op jit(solution)/shard_map/dot_general | solution.py:388
  597.9 129.5 %gated_proj.6.rest_4_ = bf16[768,5120]{1,0:T(8,128)(2,1)} custom-call(bf16[4,768,1792]{2,1,0:T(8,128)(2,1)} %bitcast.62, f32[1,7168]{1,0:T(1,128)S(1)} %bitcast.41, bf16[7168,5120]{1,0:T(8,128)(2,1)} %gate_ref.9, bf16[7168,5120]{1,0:T(8,128)(2,1)} %up_ref.9, bf16[384,7168]{1,0:T(8,128)(2,1)} %convolution_convert_fusion.4.rest_0_), custom_call_target="tpu_custom_call" | custom-call | flops 112742891520 | bytes 165675008 | tf_op jit(solution)/shard_map/gated_proj/pallas_call | solution.py:182
  727.5 32.5 %out_proj.7 = (bf16[768,1792]{1,0:T(8,128)(2,1)}, f32[8,128]{1,0:T(8,128)}) custom-call(s32[2]{0:T(128)} %pad_add_fusion.place_ref, bf16[4,768,1792]{2,1,0:T(8,128)(2,1)} %bitcast.61, bf16[3072,7168]{1,0:T(8,128)(2,1)} %bitcast.52, bf16[1792,7168]{1,0:T(8,128)(2,1)} %own_ref.9, bf16[1792,1792]{1,0:T(8,128)(2,1)} %collective-permute-done.2.near_ref, ...), custom_call_target="tpu_custom_call" | custom-call | flops 19730006016 | bytes 36700160 | tf_op jit(solution)/shard_map/out_proj/pallas_call | solution.py:241
  760.8 5.3 all-to-all-start.1
  766.2 67.9 %convolution_convert_fusion.2.rest_0_ = bf16[768,7168]{1,0:T(8,128)(2,1)} fusion(bf16[768,5120]{1,0:T(8,128)(2,1)} %gated_proj.6.rest_4_, bf16[5120,7168]{1,0:T(8,128)(2,1)} %param.21), kind=kOutput, calls=%fused_computation.2 | convolution fusion | flops 56376950784 | bytes 92274688 | tf_op jit(solution)/shard_map/dot_general | solution.py:388
  834.1 53.2 %all-to-all-done.1.received_ref = bf16[4,96,7168]{2,1,0:T(8,128)(2,1)} async-done(((bf16[4,96,7168]{2,1,0:T(8,128)(2,1)}), bf16[4,96,7168]{2,1,0:T(8,128)(2,1)}, u32[]{:S(2)}, u32[]{:S(2)}) %all-to-all-start.1) | async-done | bytes 5505056 | tf_op jit(solution)/shard_map/all_to_all | solution.py:389
  887.3 5.0 sum_rows.5.rest_4_
  892.3 34.0 %out_proj.8 = (bf16[768,1792]{1,0:T(8,128)(2,1)}, f32[8,128]{1,0:T(8,128)}) custom-call(s32[2]{0:T(128)} %pad_add_fusion.place_ref, bf16[4,768,1792]{2,1,0:T(8,128)(2,1)} %bitcast.60, bf16[3072,7168]{1,0:T(8,128)(2,1)} %bitcast.53, bf16[1792,7168]{1,0:T(8,128)(2,1)} %own_ref.9, bf16[1792,1792]{1,0:T(8,128)(2,1)} %collective-permute-done.2.near_ref, ...), custom_call_target="tpu_custom_call" | custom-call | flops 19730006016 | bytes 36700160 | tf_op jit(solution)/shard_map/out_proj/pallas_call | solution.py:241
  926.3 6.2 all-to-all-start
  933.2 130.8 %gated_proj.7 = bf16[768,5120]{1,0:T(8,128)(2,1)} custom-call(bf16[4,768,1792]{2,1,0:T(8,128)(2,1)} %bitcast.64, f32[1,7168]{1,0:T(1,128)S(1)} %bitcast.42, bf16[7168,5120]{1,0:T(8,128)(2,1)} %gate_ref.9, bf16[7168,5120]{1,0:T(8,128)(2,1)} %up_ref.9, f32[8,128]{1,0:T(8,128)S(1)} %copy-done.13), custom_call_target="tpu_custom_call" | custom-call | flops 112742891520 | bytes 165675008 | tf_op jit(solution)/shard_map/gated_proj/pallas_call | solution.py:182
  1063.9 67.2 %convolution_convert_fusion.1.rest_0_ = bf16[768,7168]{1,0:T(8,128)(2,1)} fusion(bf16[768,5120]{1,0:T(8,128)(2,1)} %gated_proj.7, bf16[5120,7168]{1,0:T(8,128)(2,1)} %param.21), kind=kOutput, calls=%fused_computation.1 | convolution fusion | flops 56376950784 | bytes 92274688 | tf_op jit(solution)/shard_map/dot_general | solution.py:388
  1131.1 11.1 all-to-all-done.received_ref
  1142.2 7.8 sum_rows.6.rest_4_
  1150.0 20.7 %out_proj.9 = (bf16[384,1792]{1,0:T(8,128)(2,1)}, f32[8,128]{1,0:T(8,128)}) custom-call(s32[2]{0:T(128)} %pad_add_fusion.place_ref, bf16[4,384,1792]{2,1,0:T(8,128)(2,1)} %bitcast.75, bf16[3072,7168]{1,0:T(8,128)(2,1)} %bitcast.54, bf16[1792,7168]{1,0:T(8,128)(2,1)} %own_ref.9, bf16[1792,1792]{1,0:T(8,128)(2,1)} %collective-permute-done.2.near_ref, ...), custom_call_target="tpu_custom_call" | custom-call | flops 9865003008 | bytes 31195136 | tf_op jit(solution)/shard_map/out_proj/pallas_call | solution.py:241
  1170.8 6.4 all-to-all-start.2
  1177.9 129.3 %gated_proj.8 = bf16[768,5120]{1,0:T(8,128)(2,1)} custom-call(bf16[4,768,1792]{2,1,0:T(8,128)(2,1)} %bitcast.66, f32[1,7168]{1,0:T(1,128)S(1)} %bitcast.43, bf16[7168,5120]{1,0:T(8,128)(2,1)} %gate_ref.9, bf16[7168,5120]{1,0:T(8,128)(2,1)} %up_ref.9, f32[8,128]{1,0:T(8,128)S(1)} %copy-done.12), custom_call_target="tpu_custom_call" | custom-call | flops 112742891520 | bytes 165675008 | tf_op jit(solution)/shard_map/gated_proj/pallas_call | solution.py:182
  1307.2 65.7 %convolution_convert_fusion.rest_0_ = bf16[768,7168]{1,0:T(8,128)(2,1)} fusion(bf16[768,5120]{1,0:T(8,128)(2,1)} %gated_proj.8, bf16[5120,7168]{1,0:T(8,128)(2,1)} %param.21), kind=kOutput, calls=%fused_computation | convolution fusion | flops 56376950784 | bytes 92274688 | tf_op jit(solution)/shard_map/dot_general | solution.py:388
  1372.9 12.3 all-to-all-done.2.received_ref
  1385.2 7.8 sum_rows.7.refs_1_
  1393.0 6.4 all-to-all-start.4
  1399.5 6.8 store_rows.5.rest_0_.refs_1_
  1406.3 69.8 %gated_proj.9 = bf16[384,5120]{1,0:T(8,128)(2,1)S(1)} custom-call(bf16[4,384,1792]{2,1,0:T(8,128)(2,1)} %bitcast.72, f32[1,7168]{1,0:T(1,128)S(1)} %bitcast.44, bf16[7168,5120]{1,0:T(8,128)(2,1)} %gate_ref.9, bf16[7168,5120]{1,0:T(8,128)(2,1)} %up_ref.9, bf16[3072,7168]{1,0:T(8,128)(2,1)} %store_rows.5.rest_0_.refs_1_), custom_call_target="tpu_custom_call" | custom-call | flops 56371445760 | bytes 156237824 | tf_op jit(solution)/shard_map/gated_proj/pallas_call | solution.py:182
  1476.1 2.0 copy-done.14
  1478.1 37.5 %convolution_convert_fusion.3.rest_0_ = bf16[384,7168]{1,0:T(8,128)(2,1)} fusion(bf16[384,5120]{1,0:T(8,128)(2,1)} %copy-done.14, bf16[5120,7168]{1,0:T(8,128)(2,1)} %param.21), kind=kOutput, calls=%fused_computation.3 | convolution fusion | flops 28188475392 | bytes 82837504 | tf_op jit(solution)/shard_map/dot_general | solution.py:388
  1515.7 64.0 %all-to-all-done.4.received_ref = bf16[4,192,7168]{2,1,0:T(8,128)(2,1)} async-done(((bf16[4,192,7168]{2,1,0:T(8,128)(2,1)}), bf16[4,192,7168]{2,1,0:T(8,128)(2,1)}, u32[]{:S(2)}, u32[]{:S(2)}) %all-to-all-start.4) | async-done | bytes 11010080 | tf_op jit(solution)/shard_map/all_to_all | solution.py:389
  1579.6 7.8 sum_rows.8.refs_2_
  1587.5 5.3 all-to-all-start.3
  1597.7 3.8 reshape.170
  1603.2 1.9 constant_dynamic-update-slice_fusion.8
  1606.7 3.5 reshape.171
  1610.2 7.2 pad_maximum_fusion.rest_1_
  1617.5 5.7 pad_maximum_fusion.1.rest_2_
  1623.2 9.6 store_rows.6.refs_1_
  1632.7 9.5 store_rows.7.rest_0_.refs_1_
  1642.3 71.3 %all-to-all-done.3.received_ref = bf16[4,96,7168]{2,1,0:T(8,128)(2,1)} async-done(((bf16[4,96,7168]{2,1,0:T(8,128)(2,1)}), bf16[4,96,7168]{2,1,0:T(8,128)(2,1)}, u32[]{:S(2)}, u32[]{:S(2)}) %all-to-all-start.3) | async-done | bytes 5505056 | tf_op jit(solution)/shard_map/all_to_all | solution.py:389
  1713.5 5.0 sum_rows.9
  1718.6 9.9 store_rows.8.refs_1_
  1728.5 28.6 %all-gather.32.cloned.1.call-done.refs_0_ = bf16[384,7168]{1,0:T(8,128)(2,1)} async-done(((bf16[96,7168]{1,0:T(8,128)(2,1)}), bf16[384,7168]{1,0:T(8,128)(2,1)}) %all-gather.32.cloned.1.call-update) | async-done | bytes 5505040 | tf_op jit(solution)/shard_map/all_gather | solution.py:375
  1757.1 5.9 store_rows.9
  (117 shorter events, 20.1 us)
Async XLA Ops:
  7.2 5.0 copy-start.21
  7.2 417.1 %all-gather.40.cloned.1.call-start = ((), (), s32[]{:S(2)}) async-start(), calls=%async_computation.12 | async-start | bytes 6881280 | tf_op jit(solution)/shard_map/all_gather | solution.py:359
  42.1 1.8 copy-start.2
  53.2 391.9 %all-gather.38.cloned.1.call-start = ((), (), s32[]{:S(2)}) async-start(), calls=%async_computation.11 | async-start | bytes 13762560 | tf_op jit(solution)/shard_map/all_gather | solution.py:359
  53.4 0.9 copy-start.9
  109.4 375.5 %all-gather.44.cloned.1.call-start = ((), (), s32[]{:S(2)}) async-start(), calls=%async_computation.14 | async-start | bytes 6881280 | tf_op jit(solution)/shard_map/all_gather | solution.py:370
  115.5 133.0 %collective-permute-start = (bf16[896,1792]{1,0:T(8,128)(2,1)}, bf16[896,1792]{1,0:T(8,128)(2,1)S(1)}, u32[]{:S(2)}, u32[]{:S(2)}) collective-permute-start(bf16[896,1792]{1,0:T(8,128)(2,1)} %get-tuple-element.52), channel_id=1, source_target_pairs={{0,2},{1,3},{2,0},{3,1},{4,6},{5,7},{6,4},{7,5}} | collective-permute-start | bytes 9633800 | tf_op jit(solution)/shard_map/ppermute | solution.py:338
  118.9 196.7 %collective-permute-start.1 = (bf16[896,1792]{1,0:T(8,128)(2,1)}, bf16[896,1792]{1,0:T(8,128)(2,1)}, u32[]{:S(2)}, u32[]{:S(2)}) collective-permute-start(bf16[896,1792]{1,0:T(8,128)(2,1)} %get-tuple-element.51), channel_id=1, source_target_pairs={{0,3},{1,2},{2,1},{3,0},{4,7},{5,6},{6,5},{7,4}} | collective-permute-start | bytes 9633800 | tf_op jit(solution)/shard_map/ppermute | solution.py:338
  118.9 131.6 %copy-start.5 = (bf16[768,256]{1,0:T(8,128)(2,1)S(1)}, bf16[768,256]{1,0:T(8,128)(2,1)}, u32[]{:S(2)}) copy-start(bf16[768,256]{1,0:T(8,128)(2,1)} %get-tuple-element.28.rest_0_) | copy-start | bytes 1179652
  126.0 298.2 %collective-permute-start.2 = (bf16[1792,1792]{1,0:T(8,128)(2,1)}, bf16[1792,1792]{1,0:T(8,128)(2,1)}, u32[]{:S(2)}, u32[]{:S(2)}) collective-permute-start(bf16[1792,1792]{1,0:T(8,128)(2,1)} %constant_dynamic-slice_fusion), channel_id=1, source_target_pairs={{0,1},{1,0},{2,3},{3,2},{4,5},{5,4},{6,7},{7,6}} | collective-permute-start | bytes 19267592 | tf_op jit(solution)/shard_map/ppermute | solution.py:341
  248.5 41.4 %copy-start = (bf16[896,1792]{1,0:T(8,128)(2,1)}, bf16[896,1792]{1,0:T(8,128)(2,1)S(1)}, u32[]{:S(2)}) copy-start(bf16[896,1792]{1,0:T(8,128)(2,1)S(1)} %collective-permute-done.rest_1_.rest_0_) | copy-start | bytes 9633796
  248.5 175.7 %collective-permute-start.3 = (bf16[896,1792]{1,0:T(8,128)(2,1)S(1)}, bf16[896,1792]{1,0:T(8,128)(2,1)}, u32[]{:S(2)}, u32[]{:S(2)}) collective-permute-start(bf16[896,1792]{1,0:T(8,128)(2,1)S(1)} %collective-permute-done.rest_1_.rest_0_), channel_id=1, source_target_pairs={{0,4},{4,0},{1,5},{5,1},{2,6},{6,2},{3,7},{7,3}} | collective-permute-start | bytes 9633800 | tf_op jit(solution)/shard_map/ppermute | solution.py:339
  315.7 108.6 %collective-permute-start.4 = (bf16[896,1792]{1,0:T(8,128)(2,1)}, bf16[896,1792]{1,0:T(8,128)(2,1)}, u32[]{:S(2)}, u32[]{:S(2)}) collective-permute-start(bf16[896,1792]{1,0:T(8,128)(2,1)} %collective-permute-done.1.rest_0_.rest_2_), channel_id=1, source_target_pairs={{0,4},{4,0},{1,5},{5,1},{2,6},{6,2},{3,7},{7,3}} | collective-permute-start | bytes 9633800 | tf_op jit(solution)/shard_map/ppermute | solution.py:339
  332.5 1.0 copy-start.7
  388.5 1.0 copy-start.3
  413.2 1.8 copy-start.1
  445.1 152.9 %all-gather.42.cloned.1.call-start = ((), (), s32[]{:S(2)}) async-start(), calls=%async_computation.13 | async-start | bytes 13762560 | tf_op jit(solution)/shard_map/all_gather | solution.py:370
  478.4 0.7 copy-start.22
  478.4 6.4 copy-start.11
  478.4 249.0 %all-gather.46.cloned.1.call-start = ((), (), s32[]{:S(2)}) async-start(), calls=%async_computation.15 | async-start | bytes 13762560 | tf_op jit(solution)/shard_map/all_gather | solution.py:359
  479.0 413.2 %all-gather.50.cloned.1.call-start = ((), (), s32[]{:S(2)}) async-start(), calls=%async_computation.17 | async-start | bytes 13762560 | tf_op jit(solution)/shard_map/all_gather | solution.py:359
  479.6 453.6 %all-gather.48.cloned.1.call-start = ((), (), s32[]{:S(2)}) async-start(), calls=%async_computation.16 | async-start | bytes 13762560 | tf_op jit(solution)/shard_map/all_gather | solution.py:370
  556.5 1.9 copy-start.15
  760.0 390.0 %all-gather.36.cloned.1.call-start = ((), (), s32[]{:S(2)}) async-start(), calls=%async_computation.10 | async-start | bytes 6881280 | tf_op jit(solution)/shard_map/all_gather | solution.py:359
  760.8 126.5 %all-to-all-start.1 = ((bf16[4,96,7168]{2,1,0:T(8,128)(2,1)}), bf16[4,96,7168]{2,1,0:T(8,128)(2,1)}, u32[]{:S(2)}, u32[]{:S(2)}) async-start(bf16[4,96,7168]{2,1,0:T(8,128)(2,1)} %bitcast.71), calls=%async_computation.1 | async-start | bytes 11010048 | tf_op jit(solution)/shard_map/all_to_all | solution.py:389
  766.1 411.7 %all-gather.54.cloned.1.call-start = ((), (), s32[]{:S(2)}) async-start(), calls=%async_computation.19 | async-start | bytes 13762560 | tf_op jit(solution)/shard_map/all_gather | solution.py:370
  926.3 6.8 copy-start.13
  926.3 215.9 %all-to-all-start = ((bf16[4,192,7168]{2,1,0:T(8,128)(2,1)}), bf16[4,192,7168]{2,1,0:T(8,128)(2,1)}, u32[]{:S(2)}, u32[]{:S(2)}) async-start(bf16[4,192,7168]{2,1,0:T(8,128)(2,1)} %bitcast.57), calls=%async_computation | async-start | bytes 22020096 | tf_op jit(solution)/shard_map/all_to_all | solution.py:389
  932.5 467.0 %all-gather.26.cloned.1.call-start = ((), (), s32[]{:S(2)}) async-start(), calls=%async_computation.5 | async-start | bytes 6881280 | tf_op jit(solution)/shard_map/all_gather | solution.py:375
  933.1 473.2 %all-gather.52.cloned.1.call-start = ((), (), s32[]{:S(2)}) async-start(), calls=%async_computation.18 | async-start | bytes 6881280 | tf_op jit(solution)/shard_map/all_gather | solution.py:370
  1170.8 7.1 copy-start.12
  1170.8 214.4 %all-to-all-start.2 = ((bf16[4,192,7168]{2,1,0:T(8,128)(2,1)}), bf16[4,192,7168]{2,1,0:T(8,128)(2,1)}, u32[]{:S(2)}, u32[]{:S(2)}) async-start(bf16[4,192,7168]{2,1,0:T(8,128)(2,1)} %bitcast.56), calls=%async_computation.2 | async-start | bytes 22020096 | tf_op jit(solution)/shard_map/all_to_all | solution.py:389
  1177.2 446.0 %all-gather.30.cloned.1.call-start = ((), (), s32[]{:S(2)}) async-start(), calls=%async_computation.7 | async-start | bytes 13762560 | tf_op jit(solution)/shard_map/all_gather | solution.py:375
  1177.8 454.9 %all-gather.28.cloned.1.call-start = ((), (), s32[]{:S(2)}) async-start(), calls=%async_computation.6 | async-start | bytes 13762560 | tf_op jit(solution)/shard_map/all_gather | solution.py:375
  1393.0 186.6 %all-to-all-start.4 = ((bf16[4,192,7168]{2,1,0:T(8,128)(2,1)}), bf16[4,192,7168]{2,1,0:T(8,128)(2,1)}, u32[]{:S(2)}, u32[]{:S(2)}) async-start(bf16[4,192,7168]{2,1,0:T(8,128)(2,1)} %bitcast.58), calls=%async_computation.4 | async-start | bytes 22020096 | tf_op jit(solution)/shard_map/all_to_all | solution.py:389
  1399.4 319.2 %all-gather.34.cloned.1.call-start = ((), (), s32[]{:S(2)}) async-start(), calls=%async_computation.9 | async-start | bytes 13762560 | tf_op jit(solution)/shard_map/all_gather | solution.py:375
  1476.1 2.0 copy-start.14
  1587.5 126.1 %all-to-all-start.3 = ((bf16[4,96,7168]{2,1,0:T(8,128)(2,1)}), bf16[4,96,7168]{2,1,0:T(8,128)(2,1)}, u32[]{:S(2)}, u32[]{:S(2)}) async-start(bf16[4,96,7168]{2,1,0:T(8,128)(2,1)} %bitcast.59), calls=%async_computation.3 | async-start | bytes 11010048 | tf_op jit(solution)/shard_map/all_to_all | solution.py:389
  1592.8 1.0 copy-start.10
  1592.8 1.1 copy-start.20
  1592.8 1.8 copy-start.6
  1592.8 2.6 copy-start.19
  1592.8 2.6 copy-start.8
  1592.8 3.4 copy-start.4
  1592.8 4.2 copy-start.18
  1592.8 164.2 %all-gather.32.cloned.1.call-start = ((), (), s32[]{:S(2)}) async-start(), calls=%async_computation.8 | async-start | bytes 6881280 | tf_op jit(solution)/shard_map/all_gather | solution.py:375
  1595.4 14.8 slice-start.1
  1595.4 1.6 copy-start.17
  1603.2 14.2 slice-start
  1610.2 7.2 copy-start.16
Sparse Core Ops, SparseCore 0:
  53.3 41.9 all-gather.39
  109.5 132.0 all-gather.37
  445.2 39.6 all-gather.43
  486.8 70.3 all-gather.41
  559.1 70.3 all-gather.45
  630.9 70.3 all-gather.49
  760.2 128.9 all-gather.47
  890.7 39.1 all-gather.35
  932.0 129.4 all-gather.53
  1062.8 68.6 all-gather.25
  1170.9 66.6 all-gather.51
  1239.0 130.3 all-gather.29
  1393.1 129.4 all-gather.27
  1587.6 128.1 all-gather.33
  1718.7 38.2 all-gather.31
